TPU v7x, 1024 devices: a whole 4x8x16 slice. The times are simulated.
1024 devices in a mesh: node: 32 (over z, core), local: 32 (over y, x).
Axes of the slice: x: 4, y: 8, z: 16, core: 2. Of those that a mesh axis runs over, the one named last changes fastest.
Arguments:
- tokens: bfloat16 [32, 32, 7168], P('local', 'node'), may hold values from -6 to 6
- node_ids: int32 [32, 32, 4], P('local', 'node'), may hold values from 0 to 15, all different within a row; in each aligned block of 32 rows (0 to 31, 32 to 63, ..., all dimensions but the last counted through in order) at most 9 rows name the same one
- gates: bfloat16 [32, 32, 8], P('local', 'node'), may hold values from 0.19921875 to 2
- w_in: bfloat16 [1024, 3584, 256], P(('node', 'local')), may hold values from -0.0625 to 0.0625
- w_out: bfloat16 [32, 2048, 7168], P('node', 'local'), may hold values from -0.125 to 0.125
Outputs:
- mixed: bfloat16 [32, 32, 7168], P('local', 'node')
- balance: float32 [32], P('node')
Inputs may be any that keep to these rules, and one draw needn't show every extreme that they name: `node_ids`: each token names 4 different nodes. Among the 32 tokens of one index along the first dimension, no node is named by more than 9 tokens, and in every draw, for some index, some node is named by exactly 9 of them.
All inputs are finite; a program needn't handle non-finite values.
Results may differ from a plain program's by a relative error of at most 0.017.
Values may be sent and summed in bfloat16 or wider, within the bound.
No kernel may reach another device: no remote copies, remote signals or barrier semaphores. Data moves between devices by JAX's collectives and lax.ppermute only.
A program may use at most 64 MiB of HBM per device.

v0:
```python
import math

import jax
import jax.numpy as jnp
from jax import lax
from jax.sharding import PartitionSpec as P

NODE_TOP = 4


def swapped(value, axis, apart):
    mask = 2**apart
    pairs = [(source, source ^ mask) for source in range(lax.axis_size(axis))]
    return lax.ppermute(value, axis, pairs)


def in_one_piece(arrays, axis, split_dim, concat_dim, along):
    widths = [math.prod(a.shape[along:]) for a in arrays]
    both = jnp.concatenate(
        [a.reshape(*a.shape[:along], w) for a, w in zip(arrays, widths)], axis=along
    )
    out = lax.all_to_all(both, axis, split_axis=split_dim, concat_axis=concat_dim, tiled=True)
    parts = jnp.split(out, [sum(widths[:k]) for k in range(1, len(widths))], axis=along)
    return tuple((b.reshape(*out.shape[:along], *a.shape[along:]) for a, b in zip(arrays, parts)))


def in_order(parts, dim):
    shape = list(parts.shape[1:])
    shape[dim] *= parts.shape[0]
    return jnp.moveaxis(parts, 0, dim).reshape(shape)


def copy_for_each(x, axis):
    copies = jnp.broadcast_to(x, (lax.axis_size(axis), *x.shape))
    return lax.all_to_all(copies, axis, split_axis=0, concat_axis=0, tiled=True)


def gather_directly(x, axis, dim):
    return in_order(copy_for_each(x, axis), dim)


def packing(flat_gate, capacity):
    live = flat_gate > 0
    order = jnp.cumsum(live.astype(jnp.int32)) - 1
    wanted = jnp.arange(capacity, dtype=jnp.int32)[:, None]
    return (live[None, :] & (order[None, :] == wanted)).astype(jnp.bfloat16)


def shards(tokens, node_ids, gates, w_in, w_out):
    nodes = lax.axis_size("node")
    local_count = lax.axis_size("local")
    parity = lax.axis_index("local") % 2
    own = tokens[0]
    routes = node_ids[0]
    tok_count = own.shape[0]
    model = own.shape[1]
    half = model // 2
    groups = nodes // 2
    capacity = tok_count * min(nodes, 2 * NODE_TOP + 1)
    slots = nodes * tok_count
    pair_gates = gates[0].astype(jnp.float32).reshape(tok_count, NODE_TOP, 2)
    member = routes[:, :, None] == jnp.arange(groups, dtype=jnp.int32)
    group_visits = jnp.any(member, axis=1)
    row_visits = jnp.repeat(group_visits, 2, axis=1)
    expert_gate = jnp.sum(
        jnp.where(member[:, :, :, None], pair_gates[:, :, None, :], jnp.float32(0.0)), axis=1
    ).reshape(tok_count, nodes)
    gate_out = expert_gate.T.astype(jnp.bfloat16)
    sides = jnp.tile(own.reshape(tok_count, 2, half).transpose(1, 0, 2), (groups, 1, 1))
    outbound = jnp.where(row_visits.T[:, :, None], sides, jnp.zeros((), own.dtype))
    arrived, arrived_gate = (
        lax.all_to_all(outbound, "node", split_axis=0, concat_axis=0, tiled=True),
        lax.all_to_all(gate_out, "node", split_axis=0, concat_axis=0, tiled=True),
    )
    flat_gate = arrived_gate.reshape(slots)
    select = packing(flat_gate, capacity)
    held = jnp.dot(select, arrived.reshape(slots, half), preferred_element_type=jnp.float32).astype(
        jnp.bfloat16
    )
    partner = swapped(held, "node", 0)
    leading = lax.axis_index("node") % 2 == 0
    first = jnp.where(leading, held, partner)
    second = jnp.where(leading, partner, held)
    packed = jnp.concatenate([first, second], axis=1)
    packed_gate = jnp.dot(select, flat_gate[:, None], preferred_element_type=jnp.float32)[
        :, 0
    ].astype(jnp.bfloat16)
    outgoing = jnp.tile(
        packed.reshape(capacity, 2, half).transpose(1, 0, 2), (local_count // 2, 1, 1)
    )
    gate_copies = jnp.broadcast_to(packed_gate[None, :], (local_count, capacity))
    parts, gate_parts = in_one_piece((outgoing, gate_copies), "local", 0, 0, 2)
    my_rows = parts.reshape(local_count * capacity, half)
    row_gate = gate_parts.reshape(local_count * capacity)
    partial_value = jnp.dot(my_rows, w_in[0], preferred_element_type=jnp.float32)
    summed_pre = partial_value + swapped(partial_value, "local", 0)
    ff_dev = w_in.shape[2] // 2
    hidden = (
        row_gate.astype(jnp.float32)[:, None]
        * jax.nn.silu(summed_pre[:, :ff_dev])
        * summed_pre[:, ff_dev:]
    ).astype(jnp.bfloat16)
    block = w_out.shape[1]
    mine = lax.dynamic_slice_in_dim(hidden, parity * block, block, 1)
    columns = lax.all_to_all(w_out[0], "local", split_axis=1, concat_axis=0, tiled=True)
    column_width = columns.shape[1]
    every_hidden = gather_directly(mine, "local", 1)
    row_total = every_hidden.shape[0]
    stacked = every_hidden.reshape(row_total, local_count, block)
    weights = columns.reshape(local_count, block, column_width)
    terms = jnp.einsum("sbk,bkc->sbc", stacked, weights, preferred_element_type=jnp.float32).astype(
        jnp.bfloat16
    )
    terms = lax.optimization_barrier(terms)
    column_out = jnp.sum(terms.astype(jnp.float32), axis=1).astype(jnp.bfloat16)
    node_out = lax.all_to_all(column_out, "local", split_axis=0, concat_axis=1, tiled=True)
    unpacked = jnp.dot(select.T, node_out, preferred_element_type=jnp.float32).astype(jnp.bfloat16)
    returned = lax.all_to_all(
        unpacked.reshape(nodes, tok_count, model), "node", split_axis=0, concat_axis=0, tiled=True
    )
    mixed = jnp.sum(returned.astype(jnp.float32), axis=0).astype(jnp.bfloat16)[None]
    tokens_all = tok_count * nodes * local_count
    scale = jnp.float32(nodes / (2 * NODE_TOP * tokens_all))
    counted = jnp.sum((row_gate > 0).astype(jnp.float32)).reshape(1)
    gate_total = jnp.sum(row_gate.astype(jnp.float32)).reshape(1)
    balance = counted * scale * (gate_total * scale)
    return (mixed, balance)


def solution(mesh):
    placed = (
        P("local", "node", None),
        P("local", "node", None),
        P("local", "node", None),
        P(("node", "local"), None, None),
        P("node", "local", None),
    )
    return jax.shard_map(
        shards,
        mesh=mesh,
        in_specs=placed,
        out_specs=(P("local", "node", None), P("node")),
        check_vma=False,
    )
```

profile of v0, /device:TPU:1, one launch (start us, length us, event | category | flops | bytes accessed | tf_op | source)
XLA Modules:
  0.0 308.9 jit_solution(17835626352909410853)
XLA Ops:
  0.6 0.9 iota_compare_fusion.2
  1.5 0.7 convert_reduce_fusion.3
  2.2 0.1 reshape.258
  2.3 0.1 copy.31
  2.4 0.1 select_reduce_fusion
  2.5 0.1 copy.32
  2.6 0.7 convert_element_type.104
  3.2 20.4 %all-to-all-start = ((bf16[32,1,1]{2,1,0:T(2,128)(2,1)}), bf16[32,1,1]{2,1,0:T(2,128)(2,1)S(1)}, u32[]{:S(2)}, u32[]{:S(2)}) async-start(bf16[32,1,1]{2,1,0:T(2,128)(2,1)} %convert_element_type.104), calls=%async_computation | async-start | bytes 32768 | tf_op jit(solution)/shard_map/all_to_all | solution.py:73
  23.7 0.7 fusion.21
  24.4 0.1 broadcast_in_dim.56
  24.5 0.1 broadcast_in_dim.57
  24.6 0.8 reduce.10
  25.4 0.1 tile.20
  25.6 0.1 tile.21
  25.7 0.1 broadcast_select_fusion
  25.7 0.5 broadcast.133
  26.3 0.7 reduce.18
  27.0 0.7 reshape.276
  27.7 7.7 %all-to-all-done = bf16[32,1,1]{2,1,0:T(2,128)(2,1)S(1)} async-done(((bf16[32,1,1]{2,1,0:T(2,128)(2,1)}), bf16[32,1,1]{2,1,0:T(2,128)(2,1)S(1)}, u32[]{:S(2)}, u32[]{:S(2)}) %all-to-all-start) | async-done | bytes 96 | tf_op jit(solution)/shard_map/all_to_all | solution.py:73
  35.4 4.5 %all-to-all-start.1 = ((bf16[32,2,1792]{2,1,0:T(2,128)(2,1)}), bf16[32,2,1792]{2,1,0:T(2,128)(2,1)S(1)}, u32[]{:S(2)}, u32[]{:S(2)}) async-start(bf16[32,2,1792]{2,1,0:T(2,128)(2,1)} %reshape.276), calls=%async_computation.1 | async-start | bytes 458752 | tf_op jit(solution)/shard_map/all_to_all | solution.py:72
  40.0 0.3 reduce.8
  40.3 0.1 add_reduce_fusion
  40.5 19.7 %all-to-all-done.1 = bf16[32,2,1792]{2,1,0:T(2,128)(2,1)S(1)} async-done(((bf16[32,2,1792]{2,1,0:T(2,128)(2,1)}), bf16[32,2,1792]{2,1,0:T(2,128)(2,1)S(1)}, u32[]{:S(2)}, u32[]{:S(2)}) %all-to-all-start.1) | async-done | bytes 229408 | tf_op jit(solution)/shard_map/all_to_all | solution.py:72
  60.2 0.2 reshape.277
  60.4 0.2 convolution_convert_fusion.1
  60.5 3.3 %collective-permute-start = (bf16[9,3584]{1,0:T(8,128)(2,1)S(1)}, bf16[9,3584]{1,0:T(8,128)(2,1)S(1)}, u32[]{:S(2)}, u32[]{:S(2)}) collective-permute-start(bf16[9,3584]{1,0:T(8,128)(2,1)S(1)} %convolution_convert_fusion.1), channel_id=1, source_target_pairs={{0,32},{32,0},{64,96},{96,64},{128,160},{160,128},{192,224},{224,1... | collective-permute-start | bytes 193544 | tf_op jit(solution)/shard_map/ppermute | solution.py:14
  63.8 0.1 fusion.4
  63.9 0.8 collective-permute-done
  64.8 0.1 reshape.254
  64.9 0.1 reshape.255
  65.0 0.4 tile.22
  65.4 2.2 pad_maximum_fusion
  67.7 9.8 %all-to-all-start.2 = ((bf16[32,9,3585]{2,1,0:T(8,128)(2,1)}), bf16[32,9,3585]{2,1,0:T(8,128)(2,1)}, u32[]{:S(2)}, u32[]{:S(2)}) async-start(bf16[32,9,3585]{2,1,0:T(8,128)(2,1)} %pad_maximum_fusion), calls=%async_computation.2 | async-start | bytes 7602176 | tf_op jit(solution)/shard_map/all_to_all | solution.py:22
  77.5 2.7 all_to_all.46
  80.1 1.5 copy.38
  81.7 80.9 %all-to-all-done.2 = bf16[32,9,3585]{2,1,0:T(8,128)(2,1)} async-done(((bf16[32,9,3585]{2,1,0:T(8,128)(2,1)}), bf16[32,9,3585]{2,1,0:T(8,128)(2,1)}, u32[]{:S(2)}, u32[]{:S(2)}) %all-to-all-start.2) | async-done | bytes 2064992 | tf_op jit(solution)/shard_map/all_to_all | solution.py:22
  162.6 7.6 %all-to-all-start.4 = ((bf16[64,32,224]{2,0,1:T(8,128)(2,1)}), bf16[64,32,224]{2,0,1:T(8,128)(2,1)S(1)}, u32[]{:S(2)}, u32[]{:S(2)}) async-start(bf16[64,32,224]{2,0,1:T(8,128)(2,1)} %copy.38), calls=%async_computation.4 | async-start | bytes 2097152 | tf_op jit(solution)/shard_map/all_to_all | solution.py:105
  170.2 4.1 %split.9 = bf16[32,9,3584]{2,1,0:T(8,128)(2,1)} slice(bf16[32,9,3585]{2,1,0:T(8,128)(2,1)} %all-to-all-done.2), slice={[0:32], [0:9], [0:3584]} | slice | bytes 4128768 | tf_op jit(solution)/shard_map/split | solution.py:23
  174.3 4.5 %reshape.256 = bf16[288,3584]{1,0:T(8,128)(2,1)} reshape(bf16[32,9,3584]{2,1,0:T(8,128)(2,1)} %split.9) | data formatting | bytes 4128768 | tf_op jit(solution)/shard_map/reshape | solution.py:93
  178.8 2.3 fusion.1
  181.1 3.1 %collective-permute-start.1 = (f32[288,256]{1,0:T(8,128)S(1)}, f32[288,256]{1,0:T(8,128)S(1)}, u32[]{:S(2)}, u32[]{:S(2)}) collective-permute-start(f32[288,256]{1,0:T(8,128)S(1)} %fusion.1), channel_id=1, source_target_pairs={{0,1},{1,0},{2,3},{3,2},{4,5},{5,4},{6,7},{7,6},{8,9},{9,8},{10,11... | collective-permute-start | bytes 884744 | tf_op jit(solution)/shard_map/ppermute | solution.py:14
  184.3 1.7 convert_reduce_fusion
  185.9 0.1 reshape.260
  186.0 8.7 %collective-permute-done.1 = f32[288,256]{1,0:T(8,128)S(1)} collective-permute-done((f32[288,256]{1,0:T(8,128)S(1)}, f32[288,256]{1,0:T(8,128)S(1)}, u32[]{:S(2)}, u32[]{:S(2)}) %collective-permute-start.1) | collective-permute-done | bytes 294944 | tf_op jit(solution)/shard_map/ppermute | solution.py:14
  194.8 0.2 fusion.8
  195.1 0.1 copy.37
  195.2 1.3 all-to-all-done.4
  196.4 0.2 broadcast_in_dim.60
  196.7 46.9 %all_to_all.61 = bf16[32,288,64]{1,2,0:T(8,128)(2,1)S(1)} all-to-all(bf16[32,288,64]{1,2,0:T(8,128)(2,1)S(1)} %broadcast_in_dim.60), channel_id=1, replica_groups=mesh['node'=32,'local'=32] {'local'}, dimensions={0} | all-to-all | bytes 2359296 | tf_op jit(solution)/shard_map/all_to_all | solution.py:35
  243.6 3.6 %convert_bitcast_fusion = bf16[288,32,224]{2,0,1:T(8,128)(2,1)} fusion(bf16[32,288,64]{1,2,0:T(8,128)(2,1)S(1)} %all_to_all.61, bf16[64,32,224]{2,0,1:T(8,128)(2,1)S(1)} %all-to-all-done.4), kind=kOutput, calls=%fused_computation.2 | convolution fusion | flops 266305536 | bytes 6225920 | tf_op jit(solution)/shard_map/sbk,bkc->sbc/dot_general | solution.py:111
  247.2 3.1 %reduce_sum.52 = bf16[288,224]{1,0:T(8,128)(2,1)S(1)} reduce(bf16[288,32,224]{2,0,1:T(8,128)(2,1)} %convert_bitcast_fusion, bf16[]{:T(256)} %constant.40.clone.1), dimensions={1}, to_apply=%region_3.4 | reduce | flops 1999872 | bytes 4257794 | tf_op jit(solution)/shard_map/reduce_sum | solution.py:115
  250.3 0.1 all_to_all.49
  250.4 0.4 reshape.278
  250.8 14.5 %all_to_all.62 = bf16[32,2,1008]{2,1,0:T(2,128)(2,1)S(1)} all-to-all(bf16[32,2,1008]{2,1,0:T(2,128)(2,1)S(1)} %reshape.278), channel_id=1, replica_groups=mesh['node'=32,'local'=32] {'local'}, dimensions={0} | all-to-all | bytes 258048 | tf_op jit(solution)/shard_map/all_to_all | solution.py:116
  265.3 0.5 reshape.279
  265.8 0.3 all_to_all.52
  266.1 0.3 fusion
  266.4 0.9 reduce.19
  267.4 1.1 reshape.280
  268.5 6.7 %all-to-all-start.6 = ((bf16[32,2,3584]{2,1,0:T(2,128)(2,1)}), bf16[32,2,3584]{2,1,0:T(2,128)(2,1)S(1)}, u32[]{:S(2)}, u32[]{:S(2)}) async-start(bf16[32,2,3584]{2,1,0:T(2,128)(2,1)} %reshape.280), calls=%async_computation.6 | async-start | bytes 917504 | tf_op jit(solution)/shard_map/all_to_all | solution.py:118
  276.4 29.6 %all-to-all-done.6 = bf16[32,2,3584]{2,1,0:T(2,128)(2,1)S(1)} async-done(((bf16[32,2,3584]{2,1,0:T(2,128)(2,1)}), bf16[32,2,3584]{2,1,0:T(2,128)(2,1)S(1)}, u32[]{:S(2)}, u32[]{:S(2)}) %all-to-all-start.6) | async-done | bytes 458784 | tf_op jit(solution)/shard_map/all_to_all | solution.py:118
  305.9 0.4 reshape.281
  306.3 0.8 reduce_sum.53
  307.1 0.6 broadcast_in_dim.61
  (12 shorter events, 0.3 us)
Async XLA Ops:
  0.6 178.2 %copy-start = (bf16[1,3584,256]{2,1,0:T(8,128)(2,1)S(1)}, bf16[1,3584,256]{2,1,0:T(8,128)(2,1)}, u32[]{:S(2)}) copy-start(bf16[1,3584,256]{2,1,0:T(8,128)(2,1)} %param.8) | copy-start | bytes 5505028
  3.2 32.2 %all-to-all-start = ((bf16[32,1,1]{2,1,0:T(2,128)(2,1)}), bf16[32,1,1]{2,1,0:T(2,128)(2,1)S(1)}, u32[]{:S(2)}, u32[]{:S(2)}) async-start(bf16[32,1,1]{2,1,0:T(2,128)(2,1)} %convert_element_type.104), calls=%async_computation | async-start | bytes 32768 | tf_op jit(solution)/shard_map/all_to_all | solution.py:73
  35.4 24.8 %all-to-all-start.1 = ((bf16[32,2,1792]{2,1,0:T(2,128)(2,1)}), bf16[32,2,1792]{2,1,0:T(2,128)(2,1)S(1)}, u32[]{:S(2)}, u32[]{:S(2)}) async-start(bf16[32,2,1792]{2,1,0:T(2,128)(2,1)} %reshape.276), calls=%async_computation.1 | async-start | bytes 458752 | tf_op jit(solution)/shard_map/all_to_all | solution.py:72
  60.5 4.2 %collective-permute-start = (bf16[9,3584]{1,0:T(8,128)(2,1)S(1)}, bf16[9,3584]{1,0:T(8,128)(2,1)S(1)}, u32[]{:S(2)}, u32[]{:S(2)}) collective-permute-start(bf16[9,3584]{1,0:T(8,128)(2,1)S(1)} %convolution_convert_fusion.1), channel_id=1, source_target_pairs={{0,32},{32,0},{64,96},{96,64},{128,160},{160,128},{192,224},{224,1... | collective-permute-start | bytes 193544 | tf_op jit(solution)/shard_map/ppermute | solution.py:14
  67.7 94.9 %all-to-all-start.2 = ((bf16[32,9,3585]{2,1,0:T(8,128)(2,1)}), bf16[32,9,3585]{2,1,0:T(8,128)(2,1)}, u32[]{:S(2)}, u32[]{:S(2)}) async-start(bf16[32,9,3585]{2,1,0:T(8,128)(2,1)} %pad_maximum_fusion), calls=%async_computation.2 | async-start | bytes 7602176 | tf_op jit(solution)/shard_map/all_to_all | solution.py:22
  162.6 33.8 %all-to-all-start.4 = ((bf16[64,32,224]{2,0,1:T(8,128)(2,1)}), bf16[64,32,224]{2,0,1:T(8,128)(2,1)S(1)}, u32[]{:S(2)}, u32[]{:S(2)}) async-start(bf16[64,32,224]{2,0,1:T(8,128)(2,1)} %copy.38), calls=%async_computation.4 | async-start | bytes 2097152 | tf_op jit(solution)/shard_map/all_to_all | solution.py:105
  181.1 13.7 %collective-permute-start.1 = (f32[288,256]{1,0:T(8,128)S(1)}, f32[288,256]{1,0:T(8,128)S(1)}, u32[]{:S(2)}, u32[]{:S(2)}) collective-permute-start(f32[288,256]{1,0:T(8,128)S(1)} %fusion.1), channel_id=1, source_target_pairs={{0,1},{1,0},{2,3},{3,2},{4,5},{5,4},{6,7},{7,6},{8,9},{9,8},{10,11... | collective-permute-start | bytes 884744 | tf_op jit(solution)/shard_map/ppermute | solution.py:14
  268.5 37.5 %all-to-all-start.6 = ((bf16[32,2,3584]{2,1,0:T(2,128)(2,1)}), bf16[32,2,3584]{2,1,0:T(2,128)(2,1)S(1)}, u32[]{:S(2)}, u32[]{:S(2)}) async-start(bf16[32,2,3584]{2,1,0:T(2,128)(2,1)} %reshape.280), calls=%async_computation.6 | async-start | bytes 917504 | tf_op jit(solution)/shard_map/all_to_all | solution.py:118
where the time goes:
time: 310 us; the launch traced here: 309 us
  waiting for transfers between devices  149 us (48%)
  blocking collectives  61.4 us (20%)
  starting transfers between devices  55.5 us (18%)
  local copies, waits for them, and re-layouts  20 us (6%)
  other arithmetic  13.6 us (4%)
  matrix products  6.43 us (2%)
  between operations  3.25 us (1%)
    all_to_all x1, waiting for transfers between devices, in_one_piece(): lax.all_to_all(both, axis, split_axis=split_dim, concat_axis=concat_dim,...  80.9 us
    all_to_all x1, blocking collectives, copy_for_each(): return lax.all_to_all(copies, axis, split_axis=0, concat_axis=0, tiled=True)  46.9 us
    all_to_all x1, waiting for transfers between devices, shards(): lax.all_to_all(unpacked.reshape(nodes, tok_count, model), 'node', split_a...  29.6 us
    all_to_all x1, starting transfers between devices, shards(): lax.all_to_all(gate_out, 'node', split_axis=0, concat_axis=0, tiled=True)  20.4 us
    all_to_all x1, waiting for transfers between devices, shards(): lax.all_to_all(outbound, 'node', split_axis=0, concat_axis=0, tiled=True)  19.7 us
    all_to_all x1, blocking collectives, shards(): lax.all_to_all(column_out, 'local', split_axis=0, concat_axis=1, tiled=True)  14.5 us
    all_to_all x1, starting transfers between devices, in_one_piece(): lax.all_to_all(both, axis, split_axis=split_dim, concat_axis=concat_dim,...  9.78 us
    ppermute x2, waiting for transfers between devices, swapped(): return lax.ppermute(value, axis, pairs)  9.55 us
  transfers between devices with their start and end apart: 7, of which 7 were waited for; matrix products, arithmetic and copies ran while one was open for 6% of the time, Pallas kernels for 0%

commit v1 on v0

v1 whole, which is shorter than its diff:
```python
import functools

import jax
import jax.numpy as jnp
import numpy as np
from jax import lax
from jax.experimental import pallas as pl
from jax.experimental.pallas import tpu as pltpu
from jax.sharding import Mesh
from jax.sharding import PartitionSpec as P

F32 = jnp.float32
BF16 = jnp.bfloat16

NZ, NC, NY, NXH, NXL = 16, 2, 8, 2, 2
NX = NXH * NXL
AXES = ("z", "c", "y", "xh", "xl")
COLUMN = ("z", "c")
PLANE = ("y", "xh", "xl")
ROW = ("c", "xh", "xl")

LANES = 128
SLOTS = 9
EIGHTH = 7
HALF = NX * EIGHTH
TOK = 32
IN_ROWS = SLOTS * (EIGHTH + 1)
OUT_ROWS = 64
ROWS = NY * NX * SLOTS
PAIR = ROWS // 4
BLOCK = 64
WIDTH = EIGHTH * LANES


def swap_halves(v):
    return pltpu.roll(v, LANES // 2, 1)


def left_half(shape):
    return lax.broadcasted_iota(jnp.int32, shape, 1) < LANES // 2


def one_hot(row_key, col_key):
    return (row_key == col_key).astype(F32).astype(BF16)


def dot(a, b):
    return jnp.dot(a, b, preferred_element_type=F32)


def dot_t(a, b):
    return lax.dot_general(a, b, (((1,), (1,)), ((), ())), preferred_element_type=F32)


def call(body, outs, ins, scratch=(), smem=(), flops=10**8, limit=24 * 2**20):
    return pl.pallas_call(
        body,
        out_shape=outs,
        in_specs=[
            pl.BlockSpec(memory_space=pltpu.SMEM if i in smem else pltpu.VMEM)
            for i in range(len(ins))
        ],
        out_specs=jax.tree.map(lambda _: pl.BlockSpec(memory_space=pltpu.VMEM), outs),
        scratch_shapes=list(scratch),
        compiler_params=pltpu.CompilerParams(vmem_limit_bytes=limit),
        cost_estimate=pl.CostEstimate(flops=flops, bytes_accessed=10**6, transcendentals=0),
    )(*ins)


def spread_body(ids, gates, token, pick, out):
    base = dot(pick[...], token[...])
    row = lax.broadcasted_iota(jnp.int32, base.shape, 0)
    gate_row = lax.rem(row, TOK) == HALF
    left = left_half(base.shape)
    for z in range(NZ):
        live = jnp.float32(0.0)
        first = jnp.float32(0.0)
        second = jnp.float32(0.0)
        for m in range(4):
            hit = ids[m] == z
            live = jnp.where(hit, jnp.float32(1.0), live)
            first = jnp.where(hit, gates[2 * m], first)
            second = jnp.where(hit, gates[2 * m + 1], second)
        rows = jnp.where(live > 0, base, 0.0)
        rows = jnp.where(gate_row, jnp.where(left, first, second), rows)
        out[2 * TOK * z : 2 * TOK * (z + 1), :] = rows.astype(BF16)


def slot_of(gate_rows):
    live = (gate_rows > 0).astype(F32)
    a = lax.broadcasted_iota(jnp.int32, (TOK, TOK), 0)
    b = lax.broadcasted_iota(jnp.int32, (TOK, TOK), 1)
    order = dot((b <= a).astype(F32).astype(BF16), live.astype(BF16)) - 1.0
    return jnp.where(live > 0, order, 15.0)


def pack_body(arrived, row_key, out, gate_out):
    a = lax.broadcasted_iota(jnp.int32, (TOK, TOK * TOK), 0)
    b = lax.broadcasted_iota(jnp.int32, (TOK, TOK * TOK), 1)
    gate_rows = dot(one_hot(a * TOK + HALF, b), arrived[...])
    gate_out[...] = gate_rows
    slot = slot_of(gate_rows)
    lane = lax.broadcasted_iota(jnp.int32, (8, LANES), 1)
    by_token = dot_t(one_hot(lane, 0), slot.astype(BF16))
    token_of = lax.shift_right_logical(b, 5)
    spread = dot(by_token.astype(BF16), one_hot(a, token_of))
    chunk = lax.bitwise_and(b[0:1], TOK - 1).astype(F32)
    col_key = chunk * 16.0 + spread[0:1]
    packed = dot(one_hot(row_key[...], col_key), arrived[...]).astype(BF16)
    for y in range(NY):
        out[y * NX * IN_ROWS : (y + 1) * NX * IN_ROWS, :] = packed


def up_body(core, rows, place, w, out, gate_out, balance_out, x):
    n = 2 * NX * IN_ROWS
    a = lax.broadcasted_iota(jnp.int32, (n, n), 0)
    p = one_hot(a, place[...])
    for g in range(4):
        moved = dot(p, rows[n * g : n * (g + 1), :])
        for k in range(EIGHTH + 1):
            x[k, PAIR * g : PAIR * (g + 1), :] = moved[PAIR * k : PAIR * (k + 1), :]
    gate = x[EIGHTH]
    gate = jnp.where(core[0] == 0, gate, swap_halves(gate))
    gate_out[...] = gate
    count = jnp.sum((gate > 0).astype(F32), axis=0, keepdims=True)
    total = jnp.sum(gate, axis=0, keepdims=True)
    scale = jnp.float32(1.0 / 256.0)
    balance_out[...] = jnp.broadcast_to((count * scale) * (total * scale), (8, LANES))
    features = jnp.concatenate([x[k].astype(BF16) for k in range(EIGHTH)], axis=1)
    left = left_half((ROWS, LANES))
    for j in range(4):
        both = dot(features, w[WIDTH * j : WIDTH * (j + 1), :])
        g, u = both[:, :LANES], both[:, LANES:]
        out[ROWS * 2 * j : ROWS * (2 * j + 1), :] = jnp.where(left, g, swap_halves(u)).astype(BF16)
        out[ROWS * (2 * j + 1) : ROWS * (2 * j + 2), :] = jnp.where(left, swap_halves(g), u).astype(BF16)


def hidden_body(parts, gate, out):
    total = parts[0:ROWS, :].astype(F32)
    for j in range(1, 8):
        total = total + parts[ROWS * j : ROWS * (j + 1), :].astype(F32)
    up = swap_halves(total)
    h = gate[...] * (total / (1.0 + jnp.exp(-total))) * up
    half = ROWS // 2
    h = jnp.where(left_half((half, LANES)), h[:half], swap_halves(h[half:])).astype(BF16)
    for j in range(8):
        out[half * j : half * (j + 1), :] = h


def down_body(hidden, w, place, out, acc):
    half = ROWS // 2
    left = left_half((half, LANES))
    top, bottom = [], []
    for j in range(0, 8, 2):
        a = hidden[half * j : half * (j + 1), :].astype(F32)
        b = hidden[half * (j + 1) : half * (j + 2), :].astype(F32)
        top.append(jnp.where(left, a, swap_halves(b)).astype(BF16))
        bottom.append(jnp.where(left, swap_halves(a), b).astype(BF16))
    acc[0:half, :] = dot(jnp.concatenate(top, axis=1), w[...])
    acc[half:ROWS, :] = dot(jnp.concatenate(bottom, axis=1), w[...])
    n = 2 * NX * OUT_ROWS
    a = lax.broadcasted_iota(jnp.int32, (n, EIGHTH * PAIR), 0)
    q = one_hot(a, place[...])
    for g in range(4):
        stacked = jnp.concatenate(
            [acc[PAIR * g : PAIR * (g + 1), LANES * k : LANES * (k + 1)] for k in range(EIGHTH)],
            axis=0,
        ).astype(BF16)
        out[n * g : n * (g + 1), :] = dot(q, stacked).astype(BF16)


def unpack_body(parts, gate_rows, col_key, out):
    n = NX * OUT_ROWS
    total = parts[0:n, :].astype(F32)
    for y in range(1, NY):
        total = total + parts[n * y : n * (y + 1), :].astype(F32)
    slot = slot_of(gate_rows[...])
    a = lax.broadcasted_iota(jnp.int32, (TOK * TOK, TOK), 0)
    b = lax.broadcasted_iota(jnp.int32, (TOK * TOK, TOK), 1)
    spread = dot(one_hot(lax.shift_right_logical(a, 5), b), slot.astype(BF16))
    chunk = lax.bitwise_and(lax.broadcasted_iota(jnp.int32, (TOK * TOK, LANES), 0), TOK - 1)
    key = (chunk.astype(F32) * 16.0 + spread)[:, 0:1]
    out[...] = dot(one_hot(key, col_key[...]), total.astype(BF16)).astype(BF16)


def finish_body(parts, pick, out):
    n = 2 * TOK
    total = parts[0:n, :].astype(F32)
    for z in range(1, NZ):
        total = total + parts[n * z : n * (z + 1), :].astype(F32)
    out[...] = dot(pick[...], total.astype(BF16)).astype(BF16)


@functools.cache
def tables():
    spread_pick = np.zeros((2 * TOK, 2 * HALF), np.float32)
    for c in range(NC):
        for xh in range(NXH):
            for xl in range(NXL):
                for k in range(EIGHTH):
                    j = (xh * NXL + xl) * EIGHTH + k
                    spread_pick[c * TOK + j, xl * HALF + (c * NXH + xh) * EIGHTH + k] = 1
    pack_key = np.zeros((NX * IN_ROWS, 1), np.float32)
    for x in range(NX):
        for k in range(EIGHTH + 1):
            for r in range(SLOTS):
                chunk = x * EIGHTH + k if k < EIGHTH else HALF
                pack_key[x * IN_ROWS + k * SLOTS + r, 0] = chunk * 16 + r
    cols = 2 * NX
    up_place = np.zeros((1, cols * IN_ROWS), np.int32)
    down_place = np.zeros((1, EIGHTH * PAIR), np.int32)
    for col in range(cols):
        for k in range(EIGHTH + 1):
            for r in range(SLOTS):
                up_place[0, col * IN_ROWS + k * SLOTS + r] = k * PAIR + col * SLOTS + r
                if k < EIGHTH:
                    down_place[0, k * PAIR + col * SLOTS + r] = col * OUT_ROWS + k * SLOTS + r
    unpack_key = np.full((1, NX * OUT_ROWS), -1, np.float32)
    for x in range(NX):
        for k in range(EIGHTH):
            for r in range(SLOTS):
                unpack_key[0, x * OUT_ROWS + k * SLOTS + r] = (x * EIGHTH + k) * 16 + r
    finish_pick = np.zeros((2 * HALF, 2 * TOK), np.float32)
    for c in range(NC):
        for j in range(HALF):
            finish_pick[c * HALF + j, c * TOK + j] = 1
    return spread_pick, pack_key, up_place, down_place, unpack_key, finish_pick


def exchange(x, axes, members):
    rows = x.shape[0] // members
    y = lax.all_to_all(
        x.reshape(members, rows, x.shape[1]), axes, split_axis=0, concat_axis=0, tiled=True
    )
    return y.reshape(x.shape)


def shards(tokens, node_ids, gates, w_in, w_out):
    spread_pick, pack_key, up_place, down_place, unpack_key, finish_pick = tables()
    shape = jax.ShapeDtypeStruct
    core = lax.axis_index("c").astype(jnp.int32).reshape(1)

    sent = call(
        spread_body,
        shape((TOK * TOK, LANES), BF16),
        (
            node_ids.reshape(4),
            gates.reshape(8).astype(F32),
            tokens.reshape(2 * HALF, LANES),
            jnp.asarray(spread_pick, BF16),
        ),
        smem=(0, 1),
    )
    arrived = exchange(sent, COLUMN, NZ * NC)
    w_up = exchange(w_in.reshape(4 * WIDTH, 2 * LANES), ("c", "xh"), NC * NXH)
    w_down = w_out.reshape(BLOCK, 8, WIDTH).transpose(1, 0, 2).reshape(8 * BLOCK, WIDTH)
    w_down = exchange(w_down, ROW, 8)

    packed, gate_rows = call(
        pack_body,
        (shape((NY * NX * IN_ROWS, LANES), BF16), shape((TOK, LANES), F32)),
        (arrived, jnp.asarray(pack_key)),
    )
    rows = exchange(packed, PLANE, NY * NX)

    partial_sums, gate, balance = call(
        up_body,
        (shape((8 * ROWS, LANES), BF16), shape((ROWS, LANES), F32), shape((8, LANES), F32)),
        (core, rows, jnp.asarray(up_place), w_up),
        scratch=(pltpu.VMEM((EIGHTH + 1, ROWS, LANES), F32),),
        smem=(0,),
        flops=10**9,
    )
    summands = exchange(partial_sums, ROW, 8)

    hidden = call(hidden_body, shape((4 * ROWS, LANES), BF16), (summands, gate))
    every_hidden = exchange(hidden, ROW, 8)

    down = call(
        down_body,
        shape((NY * NX * OUT_ROWS, LANES), BF16),
        (every_hidden, w_down, jnp.asarray(down_place)),
        scratch=(pltpu.VMEM((ROWS, WIDTH), F32),),
        flops=10**9,
    )
    returned = exchange(down, PLANE, NY * NX)

    unpacked = call(
        unpack_body,
        shape((TOK * TOK, LANES), BF16),
        (returned, gate_rows, jnp.asarray(unpack_key)),
    )
    back = exchange(unpacked, COLUMN, NZ * NC)

    mixed = call(
        finish_body,
        shape((2 * HALF, LANES), BF16),
        (back, jnp.asarray(finish_pick, BF16)),
    )
    return mixed.reshape(1, 1, 2 * HALF * LANES), balance[0, 0:1]


def solution(mesh):
    fine = Mesh(mesh.devices.reshape(NZ, NC, NY, NXH, NXL), AXES)
    token_spec = P(PLANE, COLUMN, None)
    return jax.shard_map(
        shards,
        mesh=fine,
        in_specs=(
            token_spec,
            token_spec,
            token_spec,
            P(AXES, None, None),
            P(COLUMN, PLANE, None),
        ),
        out_specs=(token_spec, P(COLUMN)),
        check_vma=False,
    )
```

time: 310 us -> 198 us (0.64)
  waiting for transfers between devices: 149 us -> 82.3 us
  starting transfers between devices: 55.5 us -> 28.5 us
  local copies, waits for them, and re-layouts: 20 us -> 3.73 us
  other arithmetic: 13.6 us -> 1.49 us
  blocking collectives: 61.4 us -> 73 us
  Pallas kernels: 0 us -> 7.58 us
  matrix products: 6.43 us -> 0 us
    all_to_all x5, waiting for transfers between devices: 139 us -> 82.3 us  [exchange(): lax.all_to_all(x.reshape(members, rows, x.shape[1]), axes, split_axis=0,...]
    all_to_all x5, starting transfers between devices: 49.1 us -> 28.5 us  [exchange(): lax.all_to_all(x.reshape(members, rows, x.shape[1]), axes, split_axis=0,...]
    all_to_all x2 -> x3, blocking collectives: 61.4 us -> 73 us  [exchange(): lax.all_to_all(x.reshape(members, rows, x.shape[1]), axes, split_axis=0,...]
    ppermute x2 -> x0, waiting for transfers between devices: 9.55 us -> none  [swapped(): return lax.ppermute(value, axis, pairs)]
    pallas_call x0 -> x7, Pallas kernels: none -> 7.58 us  [call(): pl.pallas_call(body, out_shape=outs, in_specs=[pl.BlockSpec(memory_space=...]
    dot_general x5 -> x0, matrix products: 6.43 us -> none  [the longest x1 3.56 us: shards(): jnp.einsum('sbk,bkc->sbc', stacked, weights, preferred_element_type=jnp.f...]
    ppermute x2 -> x0, starting transfers between devices: 6.41 us -> none  [swapped(): return lax.ppermute(value, axis, pairs)]
    reduce_sum x4 -> x0, other arithmetic: 5.71 us -> none  [the longest x1 3.13 us: shards(): column_out = jnp.sum(terms.astype(jnp.float32), axis=1).astype(jnp.bfloat16)]
  transfers between devices with their start and end apart: 7 -> 5, of which waited for: 7 -> 5; matrix products, arithmetic and copies ran while one was open for 6% -> 1% of each run, Pallas kernels for 0% -> 1%
where the time goes in v1:
time: 198 us; the launch traced here: 197 us
  waiting for transfers between devices  82.3 us (42%)
  blocking collectives  73 us (37%)
  starting transfers between devices  28.5 us (14%)
  Pallas kernels  7.58 us (4%)
  local copies, waits for them, and re-layouts  3.73 us (2%)
    all_to_all x5, waiting for transfers between devices, exchange(): lax.all_to_all(x.reshape(members, rows, x.shape[1]), axes, split_axis=0,...  82.3 us
    all_to_all x3, blocking collectives, exchange(): lax.all_to_all(x.reshape(members, rows, x.shape[1]), axes, split_axis=0,...  73 us
    all_to_all x5, starting transfers between devices, exchange(): lax.all_to_all(x.reshape(members, rows, x.shape[1]), axes, split_axis=0,...  28.5 us
    pallas_call x7, Pallas kernels, call(): pl.pallas_call(body, out_shape=outs, in_specs=[pl.BlockSpec(memory_space=...  7.58 us
  transfers between devices with their start and end apart: 5, of which 5 were waited for; matrix products, arithmetic and copies ran while one was open for 1% of the time, Pallas kernels for 1%

profile of v1, /device:TPU:1, one launch (start us, length us, event | category | flops | bytes accessed | tf_op | source)
XLA Modules:
  0.0 197.4 jit_solution(15300620967062917925)
XLA Ops:
  0.6 0.7 bitcast_convert_fusion.gates
  1.3 0.8 reduce
  2.1 0.0 copy-start.2
  2.1 0.6 copy-done.2
  2.8 0.0 copy-start.3
  2.8 0.7 copy-done.3
  3.5 0.7 shard_map.122
  4.2 42.5 %all_to_all.40 = bf16[32,32,128]{2,1,0:T(8,128)(2,1)S(1)} all-to-all(bf16[32,32,128]{2,1,0:T(8,128)(2,1)S(1)} %bitcast.38), channel_id=1, replica_groups=mesh['z'=16,'c'=2,'y'=8,'xh'=2,'xl'=2] {'z','c'}, dimensions={0} | all-to-all | bytes 524288 | tf_op jit(solution)/shard_map/all_to_all | solution.py:232
  46.7 0.0 copy-start
  46.7 0.0 copy-start.5
  46.7 5.1 %all-to-all-start.2 = ((bf16[4,896,256]{2,1,0:T(8,128)(2,1)}), bf16[4,896,256]{2,1,0:T(8,128)(2,1)S(1)}, u32[]{:S(2)}, u32[]{:S(2)}) async-start(bf16[4,896,256]{2,1,0:T(8,128)(2,1)} %bitcast.42), calls=%async_computation.2 | async-start | bytes 3670016 | tf_op jit(solution)/shard_map/all_to_all | solution.py:232
  51.8 0.0 copy-done
  51.8 1.6 shard_map.123
  53.4 21.7 %all-to-all-done.2 = bf16[4,896,256]{2,1,0:T(8,128)(2,1)S(1)} async-done(((bf16[4,896,256]{2,1,0:T(8,128)(2,1)}), bf16[4,896,256]{2,1,0:T(8,128)(2,1)S(1)}, u32[]{:S(2)}, u32[]{:S(2)}) %all-to-all-start.2) | async-done | bytes 1835040 | tf_op jit(solution)/shard_map/all_to_all | solution.py:232
  75.2 7.4 %all-to-all-start.1 = ((bf16[32,72,128]{2,1,0:T(8,128)(2,1)}), bf16[32,72,128]{2,1,0:T(8,128)(2,1)S(1)}, u32[]{:S(2)}, u32[]{:S(2)}) async-start(bf16[32,72,128]{2,1,0:T(8,128)(2,1)} %bitcast.5), calls=%async_computation.1 | async-start | bytes 1179648 | tf_op jit(solution)/shard_map/all_to_all | solution.py:232
  82.6 17.2 %all-to-all-done.1 = bf16[32,72,128]{2,1,0:T(8,128)(2,1)S(1)} async-done(((bf16[32,72,128]{2,1,0:T(8,128)(2,1)}), bf16[32,72,128]{2,1,0:T(8,128)(2,1)S(1)}, u32[]{:S(2)}, u32[]{:S(2)}) %all-to-all-start.1) | async-done | bytes 589856 | tf_op jit(solution)/shard_map/all_to_all | solution.py:232
  99.9 0.0 copy-done.5
  99.9 0.0 copy-start.7
  99.9 2.5 %shard_map.124 = (bf16[2304,128]{1,0:T(8,128)(2,1)}, f32[288,128]{1,0:T(8,128)S(1)}, f32[8,128]{1,0:T(8,128)S(1)}) custom-call(s32[1]{0:T(128)} %bitcast.core, bf16[2304,128]{1,0:T(8,128)(2,1)S(1)} %bitcast.34, s32[1,576]{1,0:T(1,128)S(1)} %copy-done.5, bf16[3584,256]{1,0:T(8,128)(2,1)S(1)} %bitcast.30), custom_call_target="tpu_custom_call" | custom-call | flops 1000000000 | bytes 1000000 | tf_op jit(solution)/shard_map/pallas_call | solution.py:56
  102.4 6.5 %all-to-all-start.3 = ((bf16[8,288,128]{2,1,0:T(8,128)(2,1)}), bf16[8,288,128]{2,1,0:T(8,128)(2,1)S(1)}, u32[]{:S(2)}, u32[]{:S(2)}) async-start(bf16[8,288,128]{2,1,0:T(8,128)(2,1)} %bitcast.9), calls=%async_computation.3 | async-start | bytes 1179648 | tf_op jit(solution)/shard_map/all_to_all | solution.py:232
  108.9 0.0 copy-done.7
  108.9 0.1 copy.14
  109.0 1.1 copy.16
  110.1 0.0 copy-start.6
  110.1 8.8 %all-to-all-done.3 = bf16[8,288,128]{2,1,0:T(8,128)(2,1)S(1)} async-done(((bf16[8,288,128]{2,1,0:T(8,128)(2,1)}), bf16[8,288,128]{2,1,0:T(8,128)(2,1)S(1)}, u32[]{:S(2)}, u32[]{:S(2)}) %all-to-all-start.3) | async-done | bytes 589856 | tf_op jit(solution)/shard_map/all_to_all | solution.py:232
  118.9 3.8 %all-to-all-start.5 = ((bf16[8,64,896]{2,1,0:T(8,128)(2,1)}), bf16[8,64,896]{2,1,0:T(8,128)(2,1)S(1)}, u32[]{:S(2)}, u32[]{:S(2)}) async-start(bf16[8,64,896]{2,1,0:T(8,128)(2,1)} %bitcast.27), calls=%async_computation.5 | async-start | bytes 1835008 | tf_op jit(solution)/shard_map/all_to_all | solution.py:232
  122.7 0.2 shard_map.125
  122.9 13.4 %all-to-all-done.5 = bf16[8,64,896]{2,1,0:T(8,128)(2,1)S(1)} async-done(((bf16[8,64,896]{2,1,0:T(8,128)(2,1)}), bf16[8,64,896]{2,1,0:T(8,128)(2,1)S(1)}, u32[]{:S(2)}, u32[]{:S(2)}) %all-to-all-start.5) | async-done | bytes 917536 | tf_op jit(solution)/shard_map/all_to_all | solution.py:232
  136.2 10.5 %all_to_all.41 = bf16[8,144,128]{2,1,0:T(8,128)(2,1)S(1)} all-to-all(bf16[8,144,128]{2,1,0:T(8,128)(2,1)S(1)} %bitcast.31), channel_id=1, replica_groups=mesh['z'=16,'c'=2,'y'=8,'xh'=2,'xl'=2] {'c','xh','xl'}, dimensions={0} | all-to-all | bytes 589824 | tf_op jit(solution)/shard_map/all_to_all | solution.py:232
  146.8 0.0 copy-done.6
  146.8 0.0 copy-start.1
  146.8 1.1 shard_map.126
  147.8 0.0 copy-start.4
  147.9 20.0 %all_to_all.42 = bf16[32,64,128]{2,1,0:T(8,128)(2,1)S(1)} all-to-all(bf16[32,64,128]{2,1,0:T(8,128)(2,1)S(1)} %bitcast.35), channel_id=1, replica_groups=mesh['z'=16,'c'=2,'y'=8,'xh'=2,'xl'=2] {'y','xh','xl'}, dimensions={0} | all-to-all | bytes 1048576 | tf_op jit(solution)/shard_map/all_to_all | solution.py:232
  167.9 0.0 copy-done.1
  167.9 1.3 shard_map.127
  169.2 5.7 %all-to-all-start.7 = ((bf16[32,32,128]{2,1,0:T(8,128)(2,1)}), bf16[32,32,128]{2,1,0:T(8,128)(2,1)S(1)}, u32[]{:S(2)}, u32[]{:S(2)}) async-start(bf16[32,32,128]{2,1,0:T(8,128)(2,1)} %bitcast.17), calls=%async_computation.7 | async-start | bytes 524288 | tf_op jit(solution)/shard_map/all_to_all | solution.py:232
  175.0 0.5 slice.3
  175.5 21.1 %all-to-all-done.7 = bf16[32,32,128]{2,1,0:T(8,128)(2,1)S(1)} async-done(((bf16[32,32,128]{2,1,0:T(8,128)(2,1)}), bf16[32,32,128]{2,1,0:T(8,128)(2,1)S(1)}, u32[]{:S(2)}, u32[]{:S(2)}) %all-to-all-start.7) | async-done | bytes 262176 | tf_op jit(solution)/shard_map/all_to_all | solution.py:232
  196.6 0.0 copy-done.4
  196.6 0.2 shard_map.128
  196.8 0.6 reshape.82
Async XLA Ops:
  2.1 0.7 copy-start.2
  2.8 0.7 copy-start.3
  46.7 5.1 %copy-start = (f32[288,1]{1,0:T(8,128)S(1)}, f32[288,1]{1,0:T(8,128)}, u32[]{:S(2)}) copy-start(f32[288,1]{1,0:T(8,128)} %constant.19.clone.row_key) | copy-start | bytes 3460
  46.7 53.2 %copy-start.5 = (s32[1,576]{1,0:T(1,128)S(1)}, s32[1,576]{1,0:T(1,128)}, u32[]{:S(2)}) copy-start(s32[1,576]{1,0:T(1,128)} %constant.20.clone.place) | copy-start | bytes 6916
  46.7 28.5 %all-to-all-start.2 = ((bf16[4,896,256]{2,1,0:T(8,128)(2,1)}), bf16[4,896,256]{2,1,0:T(8,128)(2,1)S(1)}, u32[]{:S(2)}, u32[]{:S(2)}) async-start(bf16[4,896,256]{2,1,0:T(8,128)(2,1)} %bitcast.42), calls=%async_computation.2 | async-start | bytes 3670016 | tf_op jit(solution)/shard_map/all_to_all | solution.py:232
  75.2 24.7 %all-to-all-start.1 = ((bf16[32,72,128]{2,1,0:T(8,128)(2,1)}), bf16[32,72,128]{2,1,0:T(8,128)(2,1)S(1)}, u32[]{:S(2)}, u32[]{:S(2)}) async-start(bf16[32,72,128]{2,1,0:T(8,128)(2,1)} %bitcast.5), calls=%async_computation.1 | async-start | bytes 1179648 | tf_op jit(solution)/shard_map/all_to_all | solution.py:232
  99.9 9.0 %copy-start.7 = (bf16[1,64,7168]{2,1,0:T(8,128)(2,1)S(1)}, bf16[1,64,7168]{2,1,0:T(8,128)(2,1)}, u32[]{:S(2)}) copy-start(bf16[1,64,7168]{2,1,0:T(8,128)(2,1)} %param.15) | copy-start | bytes 2752516
  102.4 16.5 %all-to-all-start.3 = ((bf16[8,288,128]{2,1,0:T(8,128)(2,1)}), bf16[8,288,128]{2,1,0:T(8,128)(2,1)S(1)}, u32[]{:S(2)}, u32[]{:S(2)}) async-start(bf16[8,288,128]{2,1,0:T(8,128)(2,1)} %bitcast.9), calls=%async_computation.3 | async-start | bytes 1179648 | tf_op jit(solution)/shard_map/all_to_all | solution.py:232
  110.1 36.7 %copy-start.6 = (s32[1,504]{1,0:T(1,128)S(1)}, s32[1,504]{1,0:T(1,128)}, u32[]{:S(2)}) copy-start(s32[1,504]{1,0:T(1,128)} %constant.21.clone.place) | copy-start | bytes 6052
  118.9 17.3 %all-to-all-start.5 = ((bf16[8,64,896]{2,1,0:T(8,128)(2,1)}), bf16[8,64,896]{2,1,0:T(8,128)(2,1)S(1)}, u32[]{:S(2)}, u32[]{:S(2)}) async-start(bf16[8,64,896]{2,1,0:T(8,128)(2,1)} %bitcast.27), calls=%async_computation.5 | async-start | bytes 1835008 | tf_op jit(solution)/shard_map/all_to_all | solution.py:232
  146.8 21.1 %copy-start.1 = (f32[1,256]{1,0:T(1,128)S(1)}, f32[1,256]{1,0:T(1,128)}, u32[]{:S(2)}) copy-start(f32[1,256]{1,0:T(1,128)} %constant.22.clone.col_key) | copy-start | bytes 3076
  147.8 48.8 %copy-start.4 = (bf16[56,64]{1,0:T(8,128)(2,1)S(1)}, bf16[56,64]{1,0:T(8,128)(2,1)}, u32[]{:S(2)}) copy-start(bf16[56,64]{1,0:T(8,128)(2,1)} %constant.23.clone.pick) | copy-start | bytes 21508
  169.2 27.4 %all-to-all-start.7 = ((bf16[32,32,128]{2,1,0:T(8,128)(2,1)}), bf16[32,32,128]{2,1,0:T(8,128)(2,1)S(1)}, u32[]{:S(2)}, u32[]{:S(2)}) async-start(bf16[32,32,128]{2,1,0:T(8,128)(2,1)} %bitcast.17), calls=%async_computation.7 | async-start | bytes 524288 | tf_op jit(solution)/shard_map/all_to_all | solution.py:232

commit v2 on v1

--- a/solution.py
+++ b/solution.py
@@ -8,6 +8,7 @@
 from jax.experimental.pallas import tpu as pltpu
 from jax.sharding import Mesh
 from jax.sharding import PartitionSpec as P
+
 
 F32 = jnp.float32
 BF16 = jnp.bfloat16
@@ -111,7 +112,8 @@
         out[y * NX * IN_ROWS : (y + 1) * NX * IN_ROWS, :] = packed
 
 
-def up_body(core, rows, place, w, out, gate_out, balance_out, x):
+def up_body(place_ids, rows, place, w_here, w_there, out, gate_out, balance_out, x):
+    core, xh = place_ids[0], place_ids[1]
     n = 2 * NX * IN_ROWS
     a = lax.broadcasted_iota(jnp.int32, (n, n), 0)
     p = one_hot(a, place[...])
@@ -120,7 +122,7 @@
         for k in range(EIGHTH + 1):
             x[k, PAIR * g : PAIR * (g + 1), :] = moved[PAIR * k : PAIR * (k + 1), :]
     gate = x[EIGHTH]
-    gate = jnp.where(core[0] == 0, gate, swap_halves(gate))
+    gate = jnp.where(core == 0, gate, swap_halves(gate))
     gate_out[...] = gate
     count = jnp.sum((gate > 0).astype(F32), axis=0, keepdims=True)
     total = jnp.sum(gate, axis=0, keepdims=True)
@@ -129,10 +131,15 @@
     features = jnp.concatenate([x[k].astype(BF16) for k in range(EIGHTH)], axis=1)
     left = left_half((ROWS, LANES))
     for j in range(4):
-        both = dot(features, w[WIDTH * j : WIDTH * (j + 1), :])
+        w = (w_here, w_there)[j // 2]
+        both = dot(features, w[WIDTH * (j % 2) : WIDTH * (j % 2 + 1), :])
         g, u = both[:, :LANES], both[:, LANES:]
-        out[ROWS * 2 * j : ROWS * (2 * j + 1), :] = jnp.where(left, g, swap_halves(u)).astype(BF16)
-        out[ROWS * (2 * j + 1) : ROWS * (2 * j + 2), :] = jnp.where(left, swap_halves(g), u).astype(BF16)
+        expert = core if j % 2 == 0 else 1 - core
+        part = xh if j < 2 else 1 - xh
+        at = ROWS * 2 * (expert * NXH + part)
+        out[pl.ds(pl.multiple_of(at, ROWS), ROWS), :] = jnp.where(left, g, swap_halves(u)).astype(BF16)
+        at = at + ROWS
+        out[pl.ds(pl.multiple_of(at, ROWS), ROWS), :] = jnp.where(left, swap_halves(g), u).astype(BF16)
 
 
 def hidden_body(parts, gate, out):
@@ -147,17 +154,26 @@
         out[half * j : half * (j + 1), :] = h
 
 
-def down_body(hidden, w, place, out, acc):
+def down_body(place_ids, hidden, w0, w1, w2, w3, place, out, acc):
+    core, x = place_ids[0], place_ids[2]
     half = ROWS // 2
     left = left_half((half, LANES))
-    top, bottom = [], []
-    for j in range(0, 8, 2):
-        a = hidden[half * j : half * (j + 1), :].astype(F32)
-        b = hidden[half * (j + 1) : half * (j + 2), :].astype(F32)
-        top.append(jnp.where(left, a, swap_halves(b)).astype(BF16))
-        bottom.append(jnp.where(left, swap_halves(a), b).astype(BF16))
-    acc[0:half, :] = dot(jnp.concatenate(top, axis=1), w[...])
-    acc[half:ROWS, :] = dot(jnp.concatenate(bottom, axis=1), w[...])
+
+    def block(expert, source):
+        at = pl.multiple_of((expert * NX + source) * half, half)
+        return hidden[pl.ds(at, half), :].astype(F32)
+
+    for d, w in enumerate((w0, w1, w2, w3)):
+        source = lax.bitwise_xor(x, jnp.int32(d))
+        a, b = block(core, source), block(1 - core, source)
+        top = dot(jnp.where(left, a, swap_halves(b)).astype(BF16), w[...])
+        bottom = dot(jnp.where(left, swap_halves(a), b).astype(BF16), w[...])
+        if d == 0:
+            acc[0:half, :] = top
+            acc[half:ROWS, :] = bottom
+        else:
+            acc[0:half, :] += top
+            acc[half:ROWS, :] += bottom
     n = 2 * NX * OUT_ROWS
     a = lax.broadcasted_iota(jnp.int32, (n, EIGHTH * PAIR), 0)
     q = one_hot(a, place[...])
@@ -235,10 +251,63 @@
     return y.reshape(x.shape)
 
 
-def shards(tokens, node_ids, gates, w_in, w_out):
+def swapped(x, axis):
+    return lax.ppermute(x, axis, [(0, 1), (1, 0)])
+
+
+def x_swapped(x, mask):
+    return lax.ppermute(x, ("xh", "xl"), [(i, i ^ mask) for i in range(NX)])
+
+
+def rows_at(start, size):
+    return pl.ds(pl.multiple_of(start, size), size)
+
+
+def for_core_body(place_ids, w_in, w_out, up, down):
+    other = 1 - place_ids[0]
+    up[...] = w_in[rows_at(other * 2 * WIDTH, 2 * WIDTH), :]
+    down[...] = w_out[:, rows_at(other * NX * WIDTH, NX * WIDTH)]
+
+
+def for_row_body(place_ids, w_in, w_out, up, down, up_here, up_there, d0, d1, d2, d3):
+    core, xh, x = place_ids[0], place_ids[1], place_ids[2]
+    for out, side in ((up_here, xh), (up_there, 1 - xh)):
+        out[0:WIDTH, :] = w_in[rows_at((2 * core + side) * WIDTH, WIDTH), :]
+        out[WIDTH : 2 * WIDTH, :] = up[rows_at(side * WIDTH, WIDTH), :]
+    for d, out in enumerate((d0, d1, d2, d3)):
+        to = lax.bitwise_xor(x, jnp.int32(d))
+        out[0:BLOCK, :] = w_out[:, rows_at((core * NX + to) * WIDTH, WIDTH)]
+        out[BLOCK : 2 * BLOCK, :] = down[:, rows_at(to * WIDTH, WIDTH)]
+
+
+def spread_weights(place_ids, w_in, w_out):
+    shape = jax.ShapeDtypeStruct
+    up_shape, down_shape = shape((2 * WIDTH, 2 * LANES), BF16), shape((2 * BLOCK, WIDTH), BF16)
+    up, down = call(
+        for_core_body,
+        (up_shape, shape((BLOCK, NX * WIDTH), BF16)),
+        (place_ids, w_in, w_out),
+        smem=(0,),
+    )
+    up = swapped(up, "c")
+    down = swapped(down, "c")
+    up_here, up_there, *parts = call(
+        for_row_body,
+        (up_shape,) * 2 + (down_shape,) * NX,
+        (place_ids, w_in, w_out, up, down),
+        smem=(0,),
+    )
+    up_there = swapped(up_there, "xh")
+    for d in range(1, NX):
+        parts[d] = x_swapped(parts[d], d)
+    return (up_here, up_there), parts
+
+
+def layer(tokens, node_ids, gates, w_in, w_out):
     spread_pick, pack_key, up_place, down_place, unpack_key, finish_pick = tables()
     shape = jax.ShapeDtypeStruct
-    core = lax.axis_index("c").astype(jnp.int32).reshape(1)
+    core, xh, xl = (lax.axis_index(a).astype(jnp.int32) for a in ROW)
+    place_ids = jnp.stack([core, xh, xh * NXL + xl])
 
     sent = call(
         spread_body,
@@ -251,10 +320,9 @@
         ),
         smem=(0, 1),
     )
+    sent, w_in, w_out = lax.optimization_barrier((sent, w_in, w_out))
     arrived = exchange(sent, COLUMN, NZ * NC)
-    w_up = exchange(w_in.reshape(4 * WIDTH, 2 * LANES), ("c", "xh"), NC * NXH)
-    w_down = w_out.reshape(BLOCK, 8, WIDTH).transpose(1, 0, 2).reshape(8 * BLOCK, WIDTH)
-    w_down = exchange(w_down, ROW, 8)
+    w_up, w_down = spread_weights(place_ids, w_in.reshape(4 * WIDTH, 2 * LANES), w_out[0])
 
     packed, gate_rows = call(
         pack_body,
@@ -266,7 +334,7 @@
     partial_sums, gate, balance = call(
         up_body,
         (shape((8 * ROWS, LANES), BF16), shape((ROWS, LANES), F32), shape((8, LANES), F32)),
-        (core, rows, jnp.asarray(up_place), w_up),
+        (place_ids, rows, jnp.asarray(up_place), *w_up),
         scratch=(pltpu.VMEM((EIGHTH + 1, ROWS, LANES), F32),),
         smem=(0,),
         flops=10**9,
@@ -279,8 +347,9 @@
     down = call(
         down_body,
         shape((NY * NX * OUT_ROWS, LANES), BF16),
-        (every_hidden, w_down, jnp.asarray(down_place)),
+        (place_ids, every_hidden, *w_down, jnp.asarray(down_place)),
         scratch=(pltpu.VMEM((ROWS, WIDTH), F32),),
+        smem=(0,),
         flops=10**9,
     )
     returned = exchange(down, PLANE, NY * NX)
@@ -304,7 +373,7 @@
     fine = Mesh(mesh.devices.reshape(NZ, NC, NY, NXH, NXL), AXES)
     token_spec = P(PLANE, COLUMN, None)
     return jax.shard_map(
-        shards,
+        layer,
         mesh=fine,
         in_specs=(
             token_spec,

time: 198 us -> 192 us (0.970)
  blocking collectives: 73 us -> 35.6 us
  starting transfers between devices: 28.5 us -> 58.3 us
  waiting for transfers between devices: 82.3 us -> 72.1 us
  local copies, waits for them, and re-layouts: 3.73 us -> 10.9 us
  Pallas kernels: 7.58 us -> 11.9 us
    all_to_all x5 -> x4, waiting for transfers between devices: 82.3 us -> 34.6 us  [exchange(): lax.all_to_all(x.reshape(members, rows, x.shape[1]), axes, split_axis=0,...]
    ppermute x0 -> x6, waiting for transfers between devices: none -> 37.6 us  [the longest x3 25 us: swapped(): return lax.ppermute(x, axis, [(0, 1), (1, 0)])]
    all_to_all x3 -> x2, blocking collectives: 73 us -> 35.6 us  [exchange(): lax.all_to_all(x.reshape(members, rows, x.shape[1]), axes, split_axis=0,...]
    ppermute x0 -> x6, starting transfers between devices: none -> 18.5 us  [the longest x3 9.57 us: x_swapped(): return lax.ppermute(x, ('xh', 'xl'), [(i, i ^ mask) for i in range(NX)])]
    all_to_all x5 -> x4, starting transfers between devices: 28.5 us -> 39.8 us  [exchange(): lax.all_to_all(x.reshape(members, rows, x.shape[1]), axes, split_axis=0,...]
    unnamed x17 -> x44, local copies, waits for them, and re-layouts: 1.54 us -> 9.74 us
    pallas_call x7 -> x9, Pallas kernels: 7.58 us -> 11.9 us  [call(): pl.pallas_call(body, out_shape=outs, in_specs=[pl.BlockSpec(memory_space=...]
  transfers between devices with their start and end apart: 5 -> 10, of which waited for: 5 -> 6; matrix products, arithmetic and copies ran while one was open for 1% -> 0% of each run, Pallas kernels for 1% -> 2%
where the time goes in v2:
time: 192 us; the launch traced here: 191 us
  waiting for transfers between devices  72.1 us (38%)
  starting transfers between devices  58.3 us (30%)
  blocking collectives  35.6 us (19%)
  Pallas kernels  11.9 us (6%)
  local copies, waits for them, and re-layouts  10.9 us (6%)
    all_to_all x4, starting transfers between devices, exchange(): lax.all_to_all(x.reshape(members, rows, x.shape[1]), axes, split_axis=0,...  39.8 us
    all_to_all x2, blocking collectives, exchange(): lax.all_to_all(x.reshape(members, rows, x.shape[1]), axes, split_axis=0,...  35.6 us
    all_to_all x4, waiting for transfers between devices, exchange(): lax.all_to_all(x.reshape(members, rows, x.shape[1]), axes, split_axis=0,...  34.6 us
    ppermute x3, waiting for transfers between devices, swapped(): return lax.ppermute(x, axis, [(0, 1), (1, 0)])  25 us
    ppermute x3, waiting for transfers between devices, x_swapped(): return lax.ppermute(x, ('xh', 'xl'), [(i, i ^ mask) for i in range(NX)])  12.6 us
    pallas_call x9, Pallas kernels, call(): pl.pallas_call(body, out_shape=outs, in_specs=[pl.BlockSpec(memory_space=...  11.9 us
    unnamed x44, local copies, waits for them, and re-layouts  9.74 us
    ppermute x3, starting transfers between devices, x_swapped(): return lax.ppermute(x, ('xh', 'xl'), [(i, i ^ mask) for i in range(NX)])  9.57 us
  transfers between devices with their start and end apart: 10, of which 6 were waited for; matrix products, arithmetic and copies ran while one was open for 0% of the time, Pallas kernels for 2%

profile of v2, /device:TPU:1, one launch (start us, length us, event | category | flops | bytes accessed | tf_op | source)
XLA Modules:
  0.0 191.3 jit_solution(10636459506466706595)
XLA Ops:
  0.6 0.7 bitcast_convert_fusion.gates
  1.3 0.8 reduce
  2.1 0.0 copy-start.17
  2.1 0.6 copy-done.17
  2.8 0.7 copy-done.18
  3.5 1.4 shard_map.122
  4.9 20.4 %all-to-all-start = ((bf16[32,32,128]{2,1,0:T(8,128)(2,1)}), bf16[32,32,128]{2,1,0:T(8,128)(2,1)S(1)}, u32[]{:S(2)}, u32[]{:S(2)}) async-start(bf16[32,32,128]{2,1,0:T(8,128)(2,1)} %bitcast.5), calls=%async_computation | async-start | bytes 524288 | tf_op jit(solution)/shard_map/all_to_all | solution.py:248
  25.3 0.1 pad_add_fusion.place_ids
  25.4 1.5 copy-done
  26.9 1.2 copy-done.2
  28.1 1.7 shard_map.124
  29.8 2.1 %collective-permute-start = (bf16[1792,256]{1,0:T(8,128)(2,1)}, bf16[1792,256]{1,0:T(8,128)(2,1)}, u32[]{:S(2)}, u32[]{:S(2)}) collective-permute-start(bf16[1792,256]{1,0:T(8,128)(2,1)} %get-tuple-element.22), channel_id=1, source_target_pairs={{0,32},{32,0},{1,33},{33,1},{2,34},{34,2},{3,35},{35,3},{4,36},{36... | collective-permute-start | bytes 2752520 | tf_op jit(solution)/shard_map/ppermute | solution.py:255
  32.0 2.2 %collective-permute-start.1 = (bf16[64,3584]{1,0:T(8,128)(2,1)}, bf16[64,3584]{1,0:T(8,128)(2,1)}, u32[]{:S(2)}, u32[]{:S(2)}) collective-permute-start(bf16[64,3584]{1,0:T(8,128)(2,1)} %get-tuple-element.23), channel_id=1, source_target_pairs={{0,32},{32,0},{1,33},{33,1},{2,34},{34,2},{3,35},{35,3},{4,36},{36... | collective-permute-start | bytes 1376264 | tf_op jit(solution)/shard_map/ppermute | solution.py:255
  34.2 13.4 %all-to-all-done = bf16[32,32,128]{2,1,0:T(8,128)(2,1)S(1)} async-done(((bf16[32,32,128]{2,1,0:T(8,128)(2,1)}), bf16[32,32,128]{2,1,0:T(8,128)(2,1)S(1)}, u32[]{:S(2)}, u32[]{:S(2)}) %all-to-all-start) | async-done | bytes 262176 | tf_op jit(solution)/shard_map/all_to_all | solution.py:248
  47.6 0.0 copy-done.5
  47.6 0.8 shard_map.123
  48.4 0.0 copy-start.4
  48.4 0.8 copy-done.4
  49.2 9.7 %all-to-all-start.1 = ((bf16[32,72,128]{2,1,0:T(8,128)(2,1)}), bf16[32,72,128]{2,1,0:T(8,128)(2,1)S(1)}, u32[]{:S(2)}, u32[]{:S(2)}) async-start(bf16[32,72,128]{2,1,0:T(8,128)(2,1)} %bitcast.31), calls=%async_computation.1 | async-start | bytes 1179648 | tf_op jit(solution)/shard_map/all_to_all | solution.py:248
  58.9 0.0 copy-start.20
  58.9 0.0 collective-permute-done.1.down
  58.9 0.0 collective-permute-done.up
  58.9 0.0 copy-done.1
  59.0 0.0 copy-done.3
  59.0 1.5 shard_map.125
  60.5 0.0 copy-start.7
  60.5 0.9 copy-done.7
  61.4 0.7 copy-done.9
  62.1 0.7 copy-done.11
  62.8 0.7 copy-done.13
  63.5 0.7 copy-done.15
  64.1 4.6 %collective-permute-start.2 = (bf16[1792,256]{1,0:T(8,128)(2,1)S(1)}, bf16[1792,256]{1,0:T(8,128)(2,1)S(1)}, u32[]{:S(2)}, u32[]{:S(2)}) collective-permute-start(bf16[1792,256]{1,0:T(8,128)(2,1)S(1)} %get-tuple-element.25), channel_id=1, source_target_pairs={{0,2},{2,0},{1,3},{3,1},{4,6},{6,4},{5,7},{7,5},{8,10},{10,8},{9,1... | collective-permute-start | bytes 2752520 | tf_op jit(solution)/shard_map/ppermute | solution.py:255
  68.8 25.0 %collective-permute-done.2.w_there = bf16[1792,256]{1,0:T(8,128)(2,1)S(1)} collective-permute-done((bf16[1792,256]{1,0:T(8,128)(2,1)S(1)}, bf16[1792,256]{1,0:T(8,128)(2,1)S(1)}, u32[]{:S(2)}, u32[]{:S(2)}) %collective-permute-start.2) | collective-permute-done | bytes 917536 | tf_op jit(solution)/shard_map/ppermute | solution.py:255
  93.8 0.0 all-to-all-done.1
  93.8 0.0 copy-done.20
  93.8 1.2 copy-done.8
  95.0 2.2 %shard_map.126 = (bf16[2304,128]{1,0:T(8,128)(2,1)S(1)}, f32[288,128]{1,0:T(8,128)S(1)}, f32[8,128]{1,0:T(8,128)S(1)}) custom-call(s32[3]{0:T(128)S(1)} %pad_add_fusion.place_ids, bf16[2304,128]{1,0:T(8,128)(2,1)S(1)} %bitcast.30, s32[1,576]{1,0:T(1,128)S(1)} %copy-done.20, bf16[1792,256]{1,0:T(8,128)(2,1)S(1)} %copy-done.8, ...), custom_call_target="tpu_custom_call" | custom-call | flops 1000000000 | bytes 1000000 | tf_op jit(solution)/shard_map/pallas_call | solution.py:57
  97.2 0.0 copy-start.16
  97.2 0.0 copy-start.14
  97.2 0.0 copy-start.12
  97.2 0.0 copy-start.10
  97.2 0.0 copy-start.21
  97.2 13.5 %all_to_all.30 = bf16[8,288,128]{2,1,0:T(8,128)(2,1)S(1)} all-to-all(bf16[8,288,128]{2,1,0:T(8,128)(2,1)S(1)} %bitcast.32), channel_id=1, replica_groups=mesh['z'=16,'c'=2,'y'=8,'xh'=2,'xl'=2] {'c','xh','xl'}, dimensions={0} | all-to-all | bytes 1179648 | tf_op jit(solution)/shard_map/all_to_all | solution.py:248
  110.7 0.9 shard_map.127
  111.6 3.7 %all-to-all-start.3 = ((bf16[8,144,128]{2,1,0:T(8,128)(2,1)}), bf16[8,144,128]{2,1,0:T(8,128)(2,1)S(1)}, u32[]{:S(2)}, u32[]{:S(2)}) async-start(bf16[8,144,128]{2,1,0:T(8,128)(2,1)} %bitcast.13), calls=%async_computation.3 | async-start | bytes 589824 | tf_op jit(solution)/shard_map/all_to_all | solution.py:248
  115.3 0.0 copy-done.16
  115.3 3.3 %collective-permute-start.3 = (bf16[128,896]{1,0:T(8,128)(2,1)S(1)}, bf16[128,896]{1,0:T(8,128)(2,1)S(1)}, u32[]{:S(2)}, u32[]{:S(2)}) collective-permute-start(bf16[128,896]{1,0:T(8,128)(2,1)S(1)} %copy-done.16), channel_id=1, source_target_pairs={{0,1},{1,0},{2,3},{3,2},{4,5},{5,4},{6,7},{7,6},{8,9},{9,8},{10,11... | collective-permute-start | bytes 688136 | tf_op jit(solution)/shard_map/ppermute | solution.py:259
  118.6 4.3 %collective-permute-start.4 = (bf16[128,896]{1,0:T(8,128)(2,1)S(1)}, bf16[128,896]{1,0:T(8,128)(2,1)S(1)}, u32[]{:S(2)}, u32[]{:S(2)}) collective-permute-start(bf16[128,896]{1,0:T(8,128)(2,1)S(1)} %copy-done.14), channel_id=1, source_target_pairs={{0,2},{1,3},{2,0},{3,1},{4,6},{5,7},{6,4},{7,5},{8,10},{9,11},{10,... | collective-permute-start | bytes 688136 | tf_op jit(solution)/shard_map/ppermute | solution.py:259
  122.9 2.0 %collective-permute-start.5 = (bf16[128,896]{1,0:T(8,128)(2,1)S(1)}, bf16[128,896]{1,0:T(8,128)(2,1)S(1)}, u32[]{:S(2)}, u32[]{:S(2)}) collective-permute-start(bf16[128,896]{1,0:T(8,128)(2,1)S(1)} %copy-done.12), channel_id=1, source_target_pairs={{0,3},{1,2},{2,1},{3,0},{4,7},{5,6},{6,5},{7,4},{8,11},{9,10},{10,... | collective-permute-start | bytes 688136 | tf_op jit(solution)/shard_map/ppermute | solution.py:259
  125.0 0.7 collective-permute-done.3.w1
  125.7 6.5 %collective-permute-done.4.w2 = bf16[128,896]{1,0:T(8,128)(2,1)S(1)} collective-permute-done((bf16[128,896]{1,0:T(8,128)(2,1)S(1)}, bf16[128,896]{1,0:T(8,128)(2,1)S(1)}, u32[]{:S(2)}, u32[]{:S(2)}) %collective-permute-start.4) | collective-permute-done | bytes 229408 | tf_op jit(solution)/shard_map/ppermute | solution.py:259
  132.2 5.3 %collective-permute-done.5.w3 = bf16[128,896]{1,0:T(8,128)(2,1)S(1)} collective-permute-done((bf16[128,896]{1,0:T(8,128)(2,1)S(1)}, bf16[128,896]{1,0:T(8,128)(2,1)S(1)}, u32[]{:S(2)}, u32[]{:S(2)}) %collective-permute-start.5) | collective-permute-done | bytes 229408 | tf_op jit(solution)/shard_map/ppermute | solution.py:259
  137.5 0.0 all-to-all-done.3
  137.5 0.0 copy-start.6
  137.5 1.9 %shard_map.128 = bf16[2048,128]{1,0:T(8,128)(2,1)S(1)} custom-call(s32[3]{0:T(128)S(1)} %pad_add_fusion.place_ids, bf16[1152,128]{1,0:T(8,128)(2,1)S(1)} %bitcast.34, bf16[128,896]{1,0:T(8,128)(2,1)S(1)} %copy-done.10, bf16[128,896]{1,0:T(8,128)(2,1)S(1)} %collective-permute-done.3.w1, bf16[128,896]{1,0:T(8,128)(2,1)S(1)} %collective-permute-done.4.w2, ...), custom_call_target="tpu_custom_call" | custom-call | flops 1000000000 | bytes 1000000 | tf_op jit(solution)/shard_map/pallas_call | solution.py:57
  139.5 0.0 copy-start.19
  139.5 22.1 %all_to_all.31 = bf16[32,64,128]{2,1,0:T(8,128)(2,1)S(1)} all-to-all(bf16[32,64,128]{2,1,0:T(8,128)(2,1)S(1)} %bitcast.33), channel_id=1, replica_groups=mesh['z'=16,'c'=2,'y'=8,'xh'=2,'xl'=2] {'y','xh','xl'}, dimensions={0} | all-to-all | bytes 1048576 | tf_op jit(solution)/shard_map/all_to_all | solution.py:248
  161.6 1.3 shard_map.129
  162.9 5.9 %all-to-all-start.5 = ((bf16[32,32,128]{2,1,0:T(8,128)(2,1)}), bf16[32,32,128]{2,1,0:T(8,128)(2,1)S(1)}, u32[]{:S(2)}, u32[]{:S(2)}) async-start(bf16[32,32,128]{2,1,0:T(8,128)(2,1)} %bitcast.17), calls=%async_computation.5 | async-start | bytes 524288 | tf_op jit(solution)/shard_map/all_to_all | solution.py:248
  168.9 0.5 slice.3
  169.4 21.1 %all-to-all-done.5 = bf16[32,32,128]{2,1,0:T(8,128)(2,1)S(1)} async-done(((bf16[32,32,128]{2,1,0:T(8,128)(2,1)}), bf16[32,32,128]{2,1,0:T(8,128)(2,1)S(1)}, u32[]{:S(2)}, u32[]{:S(2)}) %all-to-all-start.5) | async-done | bytes 262176 | tf_op jit(solution)/shard_map/all_to_all | solution.py:248
  190.5 0.0 copy-done.19
  190.5 0.2 shard_map.130
  190.7 0.6 reshape.70
  (16 shorter events, 0.0 us)
Async XLA Ops:
  2.1 0.7 copy-start.17
  2.8 0.7 copy-start.18
  3.5 44.1 %copy-start.5 = (f32[288,1]{1,0:T(8,128)S(1)}, f32[288,1]{1,0:T(8,128)}, u32[]{:S(2)}) copy-start(f32[288,1]{1,0:T(8,128)} %constant.25.clone.row_key) | copy-start | bytes 3460
  4.9 42.7 %all-to-all-start = ((bf16[32,32,128]{2,1,0:T(8,128)(2,1)}), bf16[32,32,128]{2,1,0:T(8,128)(2,1)S(1)}, u32[]{:S(2)}, u32[]{:S(2)}) async-start(bf16[32,32,128]{2,1,0:T(8,128)(2,1)} %bitcast.5), calls=%async_computation | async-start | bytes 524288 | tf_op jit(solution)/shard_map/all_to_all | solution.py:248
  25.4 1.5 copy-start
  26.9 1.2 copy-start.2
  28.1 30.8 %copy-start.1 = (bf16[1,3584,256]{2,1,0:T(8,128)(2,1)S(1)}, bf16[1,3584,256]{2,1,0:T(8,128)(2,1)}, u32[]{:S(2)}) copy-start(bf16[1,3584,256]{2,1,0:T(8,128)(2,1)} %param.14) | copy-start | bytes 5505028
  28.1 30.9 %copy-start.3 = (bf16[1,64,7168]{2,1,0:T(8,128)(2,1)S(1)}, bf16[1,64,7168]{2,1,0:T(8,128)(2,1)}, u32[]{:S(2)}) copy-start(bf16[1,64,7168]{2,1,0:T(8,128)(2,1)} %param.15) | copy-start | bytes 2752516
  29.8 29.1 %collective-permute-start = (bf16[1792,256]{1,0:T(8,128)(2,1)}, bf16[1792,256]{1,0:T(8,128)(2,1)}, u32[]{:S(2)}, u32[]{:S(2)}) collective-permute-start(bf16[1792,256]{1,0:T(8,128)(2,1)} %get-tuple-element.22), channel_id=1, source_target_pairs={{0,32},{32,0},{1,33},{33,1},{2,34},{34,2},{3,35},{35,3},{4,36},{36... | collective-permute-start | bytes 2752520 | tf_op jit(solution)/shard_map/ppermute | solution.py:255
  32.0 26.9 %collective-permute-start.1 = (bf16[64,3584]{1,0:T(8,128)(2,1)}, bf16[64,3584]{1,0:T(8,128)(2,1)}, u32[]{:S(2)}, u32[]{:S(2)}) collective-permute-start(bf16[64,3584]{1,0:T(8,128)(2,1)} %get-tuple-element.23), channel_id=1, source_target_pairs={{0,32},{32,0},{1,33},{33,1},{2,34},{34,2},{3,35},{35,3},{4,36},{36... | collective-permute-start | bytes 1376264 | tf_op jit(solution)/shard_map/ppermute | solution.py:255
  48.4 0.8 copy-start.4
  49.2 44.6 %all-to-all-start.1 = ((bf16[32,72,128]{2,1,0:T(8,128)(2,1)}), bf16[32,72,128]{2,1,0:T(8,128)(2,1)S(1)}, u32[]{:S(2)}, u32[]{:S(2)}) async-start(bf16[32,72,128]{2,1,0:T(8,128)(2,1)} %bitcast.31), calls=%async_computation.1 | async-start | bytes 1179648 | tf_op jit(solution)/shard_map/all_to_all | solution.py:248
  58.9 34.9 %copy-start.20 = (s32[1,576]{1,0:T(1,128)S(1)}, s32[1,576]{1,0:T(1,128)}, u32[]{:S(2)}) copy-start(s32[1,576]{1,0:T(1,128)} %constant.26.clone.place) | copy-start | bytes 6916
  60.5 0.9 copy-start.7
  61.4 0.7 copy-start.9
  62.1 0.7 copy-start.11
  62.8 0.7 copy-start.13
  63.5 0.7 copy-start.15
  64.1 29.7 %collective-permute-start.2 = (bf16[1792,256]{1,0:T(8,128)(2,1)S(1)}, bf16[1792,256]{1,0:T(8,128)(2,1)S(1)}, u32[]{:S(2)}, u32[]{:S(2)}) collective-permute-start(bf16[1792,256]{1,0:T(8,128)(2,1)S(1)} %get-tuple-element.25), channel_id=1, source_target_pairs={{0,2},{2,0},{1,3},{3,1},{4,6},{6,4},{5,7},{7,5},{8,10},{10,8},{9,1... | collective-permute-start | bytes 2752520 | tf_op jit(solution)/shard_map/ppermute | solution.py:255
  93.8 1.2 copy-start.8
  97.2 18.2 %copy-start.16 = (bf16[128,896]{1,0:T(8,128)(2,1)S(1)}, bf16[128,896]{1,0:T(8,128)(2,1)}, u32[]{:S(2)}) copy-start(bf16[128,896]{1,0:T(8,128)(2,1)} %copy-done.15) | copy-start | bytes 688132
  97.2 21.4 %copy-start.14 = (bf16[128,896]{1,0:T(8,128)(2,1)S(1)}, bf16[128,896]{1,0:T(8,128)(2,1)}, u32[]{:S(2)}) copy-start(bf16[128,896]{1,0:T(8,128)(2,1)} %copy-done.13) | copy-start | bytes 688132
  97.2 25.8 %copy-start.12 = (bf16[128,896]{1,0:T(8,128)(2,1)S(1)}, bf16[128,896]{1,0:T(8,128)(2,1)}, u32[]{:S(2)}) copy-start(bf16[128,896]{1,0:T(8,128)(2,1)} %copy-done.11) | copy-start | bytes 688132
  97.2 40.3 %copy-start.10 = (bf16[128,896]{1,0:T(8,128)(2,1)S(1)}, bf16[128,896]{1,0:T(8,128)(2,1)}, u32[]{:S(2)}) copy-start(bf16[128,896]{1,0:T(8,128)(2,1)} %copy-done.9) | copy-start | bytes 688132
  97.2 40.3 %copy-start.21 = (s32[1,504]{1,0:T(1,128)S(1)}, s32[1,504]{1,0:T(1,128)}, u32[]{:S(2)}) copy-start(s32[1,504]{1,0:T(1,128)} %constant.27.clone.place) | copy-start | bytes 6052
  111.6 25.9 %all-to-all-start.3 = ((bf16[8,144,128]{2,1,0:T(8,128)(2,1)}), bf16[8,144,128]{2,1,0:T(8,128)(2,1)S(1)}, u32[]{:S(2)}, u32[]{:S(2)}) async-start(bf16[8,144,128]{2,1,0:T(8,128)(2,1)} %bitcast.13), calls=%async_computation.3 | async-start | bytes 589824 | tf_op jit(solution)/shard_map/all_to_all | solution.py:248
  115.3 10.3 %collective-permute-start.3 = (bf16[128,896]{1,0:T(8,128)(2,1)S(1)}, bf16[128,896]{1,0:T(8,128)(2,1)S(1)}, u32[]{:S(2)}, u32[]{:S(2)}) collective-permute-start(bf16[128,896]{1,0:T(8,128)(2,1)S(1)} %copy-done.16), channel_id=1, source_target_pairs={{0,1},{1,0},{2,3},{3,2},{4,5},{5,4},{6,7},{7,6},{8,9},{9,8},{10,11... | collective-permute-start | bytes 688136 | tf_op jit(solution)/shard_map/ppermute | solution.py:259
  118.6 13.6 %collective-permute-start.4 = (bf16[128,896]{1,0:T(8,128)(2,1)S(1)}, bf16[128,896]{1,0:T(8,128)(2,1)S(1)}, u32[]{:S(2)}, u32[]{:S(2)}) collective-permute-start(bf16[128,896]{1,0:T(8,128)(2,1)S(1)} %copy-done.14), channel_id=1, source_target_pairs={{0,2},{1,3},{2,0},{3,1},{4,6},{5,7},{6,4},{7,5},{8,10},{9,11},{10,... | collective-permute-start | bytes 688136 | tf_op jit(solution)/shard_map/ppermute | solution.py:259
  122.9 14.6 %collective-permute-start.5 = (bf16[128,896]{1,0:T(8,128)(2,1)S(1)}, bf16[128,896]{1,0:T(8,128)(2,1)S(1)}, u32[]{:S(2)}, u32[]{:S(2)}) collective-permute-start(bf16[128,896]{1,0:T(8,128)(2,1)S(1)} %copy-done.12), channel_id=1, source_target_pairs={{0,3},{1,2},{2,1},{3,0},{4,7},{5,6},{6,5},{7,4},{8,11},{9,10},{10,... | collective-permute-start | bytes 688136 | tf_op jit(solution)/shard_map/ppermute | solution.py:259
  137.5 24.1 %copy-start.6 = (f32[1,256]{1,0:T(1,128)S(1)}, f32[1,256]{1,0:T(1,128)}, u32[]{:S(2)}) copy-start(f32[1,256]{1,0:T(1,128)} %constant.28.clone.col_key) | copy-start | bytes 3076
  139.5 51.1 %copy-start.19 = (bf16[56,64]{1,0:T(8,128)(2,1)S(1)}, bf16[56,64]{1,0:T(8,128)(2,1)}, u32[]{:S(2)}) copy-start(bf16[56,64]{1,0:T(8,128)(2,1)} %constant.29.clone.pick) | copy-start | bytes 21508
  162.9 27.6 %all-to-all-start.5 = ((bf16[32,32,128]{2,1,0:T(8,128)(2,1)}), bf16[32,32,128]{2,1,0:T(8,128)(2,1)S(1)}, u32[]{:S(2)}, u32[]{:S(2)}) async-start(bf16[32,32,128]{2,1,0:T(8,128)(2,1)} %bitcast.17), calls=%async_computation.5 | async-start | bytes 524288 | tf_op jit(solution)/shard_map/all_to_all | solution.py:248

commit v3 on v2

v3 whole, which is shorter than its diff:
```python
import jax
import jax.numpy as jnp
from jax import lax
from jax.experimental import pallas as pl
from jax.experimental.pallas import tpu as pltpu
from jax.sharding import Mesh
from jax.sharding import PartitionSpec as P


F32 = jnp.float32
BF16 = jnp.bfloat16

NZ, NC, NY, NXH, NXL = 16, 2, 8, 2, 2
NX = NXH * NXL
AXES = ("z", "c", "y", "xh", "xl")
COLUMN = ("z", "c")
PLANE = ("y", "xh", "xl")
ROW = ("c", "xh", "xl")

LANES = 128
SLOTS = 9
EIGHTH = 7
HALF = NX * EIGHTH
TOK = 32
BLOCK_ROWS = 64
ROWS = NY * NX * SLOTS
PAIR = ROWS // 4
BLOCK = 64
WIDTH = EIGHTH * LANES


def swap_halves(v):
    return pltpu.roll(v, LANES // 2, 1)


def left_half(shape):
    return lax.broadcasted_iota(jnp.int32, shape, 1) < LANES // 2


def one_hot(row_key, col_key):
    return (row_key == col_key).astype(F32).astype(BF16)


def iota(shape, axis):
    return lax.broadcasted_iota(jnp.int32, shape, axis).astype(F32)


def divided(value, by):
    quotient = jnp.floor((value + 0.5) * (1.0 / by))
    return quotient, value - by * quotient


def dot(a, b):
    return jnp.dot(a, b, preferred_element_type=F32)


def dot_t(a, b):
    return lax.dot_general(a, b, (((1,), (1,)), ((), ())), preferred_element_type=F32)


def call(body, outs, ins, scratch=(), smem=(), smem_out=(), far=False, flops=10**8, limit=24 * 2**20):
    def spec(in_smem):
        return pl.BlockSpec(memory_space=pltpu.SMEM if in_smem else pltpu.VMEM)

    far_spec = pl.BlockSpec(memory_space=pltpu.HBM)

    if far:
        ins = [pltpu.with_memory_space_constraint(x, pltpu.HBM) for x in ins]
    several = isinstance(outs, tuple)
    return pl.pallas_call(
        body,
        out_shape=outs,
        in_specs=[far_spec if far else spec(i in smem) for i in range(len(ins))],
        out_specs=tuple(spec(i in smem_out) for i in range(len(outs))) if several else spec(False),
        scratch_shapes=list(scratch),
        compiler_params=pltpu.CompilerParams(vmem_limit_bytes=limit),
        cost_estimate=pl.CostEstimate(flops=flops, bytes_accessed=10**6, transcendentals=0),
    )(*ins)


def spread_body(far_ids, far_gates, far_token, out, ids, gates, token, base, arrived):
    copies = [
        pltpu.make_async_copy(far, near, arrived.at[i])
        for i, (far, near) in enumerate(((far_token, token), (far_ids, ids), (far_gates, gates)))
    ]
    for copy in copies:
        copy.start()
    for copy in copies:
        copy.wait()
    for c in range(NC):
        for xh in range(NXH):
            for xl in range(NXL):
                for k in range(EIGHTH):
                    row = c * TOK + (xh * NXL + xl) * EIGHTH + k
                    i = xl * HALF + (c * NXH + xh) * EIGHTH + k
                    base[row : row + 1, :] = token[:, i * LANES : (i + 1) * LANES].astype(F32)
        base[c * TOK + HALF : (c + 1) * TOK, :] = jnp.zeros((TOK - HALF, LANES), F32)
    tile = (8, LANES)
    left = left_half(tile)
    gate_row = lax.broadcasted_iota(jnp.int32, tile, 0) == HALF % 8
    every_gate = gates[...].astype(F32)
    nodes, pairs = [], []
    for m in range(4):
        nodes.append(jnp.broadcast_to(ids[:, m : m + 1], tile))
        first = jnp.broadcast_to(every_gate[:, 2 * m : 2 * m + 1], tile)
        second = jnp.broadcast_to(every_gate[:, 2 * m + 1 : 2 * m + 2], tile)
        pairs.append(jnp.where(left, first, second))
    blocks = [base[8 * b : 8 * (b + 1), :] for b in range(2 * TOK // 8)]
    for z in range(NZ):
        gate = jnp.zeros(tile, F32)
        for node, pair in zip(nodes, pairs):
            gate = jnp.where(node == z, pair, gate)
        live = gate > 0
        rows = [jnp.where(live, block, 0.0) for block in blocks]
        for b in (HALF // 8, (TOK + HALF) // 8):
            rows[b] = jnp.where(gate_row, gate, rows[b])
        out[2 * TOK * z : 2 * TOK * (z + 1), :] = jnp.concatenate(rows, axis=0).astype(BF16)


def slot_of(gate_rows):
    live = (gate_rows > 0).astype(F32)
    a = lax.broadcasted_iota(jnp.int32, (TOK, TOK), 0)
    b = lax.broadcasted_iota(jnp.int32, (TOK, TOK), 1)
    order = dot((b <= a).astype(F32).astype(BF16), live.astype(BF16)) - 1.0
    return jnp.where(live > 0, order, 15.0)


def chunk_and_slot(at):
    x, row = divided(at, BLOCK_ROWS)
    k, r = divided(row, SLOTS)
    return jnp.where(k < EIGHTH, (x * EIGHTH + k) * 16.0 + r, -1.0)


def pack_body(arrived, out, gate_out):
    a = lax.broadcasted_iota(jnp.int32, (TOK, TOK * TOK), 0)
    b = lax.broadcasted_iota(jnp.int32, (TOK, TOK * TOK), 1)
    gate_rows = dot(one_hot(a * TOK + HALF, b), arrived[...])
    gate_out[...] = gate_rows
    slot = slot_of(gate_rows)
    lane = lax.broadcasted_iota(jnp.int32, (8, LANES), 1)
    by_token = dot_t(one_hot(lane, 0), slot.astype(BF16))
    token_of = lax.shift_right_logical(b, 5)
    spread = dot(by_token.astype(BF16), one_hot(a, token_of))
    chunk = lax.bitwise_and(b[0:1], TOK - 1).astype(F32)
    col_key = chunk * 16.0 + spread[0:1]
    row_key = chunk_and_slot(iota((NX * BLOCK_ROWS, 1), 0))
    packed = dot(one_hot(row_key, col_key), arrived[...])
    lane = lax.broadcasted_iota(jnp.int32, (TOK, LANES), 1)
    wanted = lax.bitwise_and(lane, 15).astype(F32) == slot
    value = jnp.where(lane < 16, gate_rows, jnp.where(lane < 32, swap_halves(gate_rows), 0.0))
    gate_line = jnp.sum(jnp.where(wanted, value, 0.0), axis=0, keepdims=True)
    row = lax.broadcasted_iota(jnp.int32, packed.shape, 0)
    last = lax.bitwise_and(row, BLOCK_ROWS - 1) == BLOCK_ROWS - 1
    packed = jnp.where(last, gate_line, packed).astype(BF16)
    for y in range(NY):
        out[y * NX * BLOCK_ROWS : (y + 1) * NX * BLOCK_ROWS, :] = packed


def up_body(place_ids, rows, w_here, w_there, out, gate_out, balance_out, x):
    core, xh = place_ids[0], place_ids[1]
    n = 2 * NX * BLOCK_ROWS
    column, row = divided(iota((1, n), 1), BLOCK_ROWS)
    k, r = divided(row, SLOTS)
    of_pair, _ = divided(iota((PAIR, 1), 0), SLOTS)
    p = jnp.concatenate(
        [
            one_hot(iota((EIGHTH * PAIR, n), 0), k * PAIR + column * SLOTS + r),
            one_hot((of_pair + 1.0) * BLOCK_ROWS - 1.0, iota((PAIR, n), 1)),
        ],
        axis=0,
    )
    for g in range(4):
        moved = dot(p, rows[n * g : n * (g + 1), :])
        for k in range(EIGHTH + 1):
            x[k, PAIR * g : PAIR * (g + 1), :] = moved[PAIR * k : PAIR * (k + 1), :]
    _, slot = divided(iota((ROWS, 1), 0), SLOTS)
    wanted = iota((ROWS, LANES), 1) == slot + 16.0 * core.astype(F32)
    gate = jnp.sum(jnp.where(wanted, x[EIGHTH], 0.0), axis=1, keepdims=True)
    gate_out[...] = jnp.broadcast_to(gate, (ROWS, LANES))
    scale = jnp.float32(1.0 / 256.0)
    count, total = jnp.sum((gate > 0).astype(F32)), jnp.sum(gate)
    balance_out[0] = (count * scale) * (total * scale)
    features = jnp.concatenate([x[k].astype(BF16) for k in range(EIGHTH)], axis=1)
    left = left_half((ROWS, LANES))
    for j in range(4):
        w = (w_here, w_there)[j // 2]
        both = dot(features, w[WIDTH * (j % 2) : WIDTH * (j % 2 + 1), :])
        g, u = both[:, :LANES], both[:, LANES:]
        expert = core if j % 2 == 0 else 1 - core
        part = xh if j < 2 else 1 - xh
        at = ROWS * 2 * (expert * NXH + part)
        out[pl.ds(pl.multiple_of(at, ROWS), ROWS), :] = jnp.where(left, g, swap_halves(u)).astype(BF16)
        at = at + ROWS
        out[pl.ds(pl.multiple_of(at, ROWS), ROWS), :] = jnp.where(left, swap_halves(g), u).astype(BF16)


def hidden_body(parts, gate, out):
    total = parts[0:ROWS, :].astype(F32)
    for j in range(1, 8):
        total = total + parts[ROWS * j : ROWS * (j + 1), :].astype(F32)
    up = swap_halves(total)
    h = gate[...] * (total / (1.0 + jnp.exp(-total))) * up
    half = ROWS // 2
    h = jnp.where(left_half((half, LANES)), h[:half], swap_halves(h[half:])).astype(BF16)
    for j in range(8):
        out[half * j : half * (j + 1), :] = h


def down_body(place_ids, hidden, w0, w1, w2, w3, out, acc):
    core, x = place_ids[0], place_ids[2]
    half = ROWS // 2
    left = left_half((half, LANES))

    def block(expert, source):
        at = pl.multiple_of((expert * NX + source) * half, half)
        return hidden[pl.ds(at, half), :].astype(F32)

    for d, w in enumerate((w0, w1, w2, w3)):
        source = lax.bitwise_xor(x, jnp.int32(d))
        a, b = block(core, source), block(1 - core, source)
        top = dot(jnp.where(left, a, swap_halves(b)).astype(BF16), w[...])
        bottom = dot(jnp.where(left, swap_halves(a), b).astype(BF16), w[...])
        if d == 0:
            acc[0:half, :] = top
            acc[half:ROWS, :] = bottom
        else:
            acc[0:half, :] += top
            acc[half:ROWS, :] += bottom
    n = 2 * NX * BLOCK_ROWS
    k, row = divided(iota((1, EIGHTH * PAIR), 1), PAIR)
    column, r = divided(row, SLOTS)
    q = one_hot(iota((n, EIGHTH * PAIR), 0), column * BLOCK_ROWS + k * SLOTS + r)
    for g in range(4):
        stacked = jnp.concatenate(
            [acc[PAIR * g : PAIR * (g + 1), LANES * k : LANES * (k + 1)] for k in range(EIGHTH)],
            axis=0,
        ).astype(BF16)
        out[n * g : n * (g + 1), :] = dot(q, stacked).astype(BF16)


def unpack_body(parts, gate_rows, out):
    n = NX * BLOCK_ROWS
    total = parts[0:n, :].astype(F32)
    for y in range(1, NY):
        total = total + parts[n * y : n * (y + 1), :].astype(F32)
    slot = slot_of(gate_rows[...])
    a = lax.broadcasted_iota(jnp.int32, (TOK * TOK, TOK), 0)
    b = lax.broadcasted_iota(jnp.int32, (TOK * TOK, TOK), 1)
    spread = dot(one_hot(lax.shift_right_logical(a, 5), b), slot.astype(BF16))
    chunk = lax.bitwise_and(lax.broadcasted_iota(jnp.int32, (TOK * TOK, LANES), 0), TOK - 1)
    key = (chunk.astype(F32) * 16.0 + spread)[:, 0:1]
    out[...] = dot(one_hot(key, chunk_and_slot(iota((1, n), 1))), total.astype(BF16)).astype(BF16)


def finish_body(parts, out, total):
    n = 2 * TOK
    value = parts[0:n, :].astype(F32)
    for z in range(1, NZ):
        value = value + parts[n * z : n * (z + 1), :].astype(F32)
    total[...] = value
    for c in range(NC):
        for j in range(HALF):
            at = (c * HALF + j) * LANES
            row = c * TOK + j
            out[:, at : at + LANES] = total[row : row + 1, :].astype(BF16)


def exchange(x, axes, members):
    rows = x.shape[0] // members
    y = lax.all_to_all(
        x.reshape(members, rows, x.shape[1]), axes, split_axis=0, concat_axis=0, tiled=True
    )
    return y.reshape(x.shape)


def swapped(x, axis):
    return lax.ppermute(x, axis, [(0, 1), (1, 0)])


def x_swapped(x, mask):
    return lax.ppermute(x, ("xh", "xl"), [(i, i ^ mask) for i in range(NX)])


def rows_at(start, size):
    return pl.ds(pl.multiple_of(start, size), size)


def core_body(place_ids, w_in, w_out, up, down):
    other = 1 - place_ids[0]
    up[...] = w_in[rows_at(other * 2 * WIDTH, 2 * WIDTH), :]
    down[...] = w_out[:, rows_at(other * NX * WIDTH, NX * WIDTH)]


def up_row_body(place_ids, w_in, up, here, there):
    core, xh = place_ids[0], place_ids[1]
    for out, side in ((here, xh), (there, 1 - xh)):
        out[0:WIDTH, :] = w_in[rows_at((2 * core + side) * WIDTH, WIDTH), :]
        out[WIDTH : 2 * WIDTH, :] = up[rows_at(side * WIDTH, WIDTH), :]


def down_row_body(place_ids, w_out, down, *outs):
    core, x = place_ids[0], place_ids[2]
    for d, out in enumerate(outs):
        to = lax.bitwise_xor(x, jnp.int32(d))
        out[0:BLOCK, :] = w_out[:, rows_at((core * NX + to) * WIDTH, WIDTH)]
        out[BLOCK : 2 * BLOCK, :] = down[:, rows_at(to * WIDTH, WIDTH)]


def spread_weights(place_ids, w_in, w_out):
    shape = jax.ShapeDtypeStruct
    up_shape, down_shape = shape((2 * WIDTH, 2 * LANES), BF16), shape((2 * BLOCK, WIDTH), BF16)
    up, down = call(
        core_body,
        (up_shape, shape((BLOCK, NX * WIDTH), BF16)),
        (place_ids, w_in, w_out),
        smem=(0,),
    )
    up = swapped(up, "c")
    down = swapped(down, "c")
    up_here, up_there = call(
        up_row_body, (up_shape,) * 2, (place_ids, w_in, up), smem=(0,)
    )
    up_there = swapped(up_there, "xh")
    parts = call(
        down_row_body, (down_shape,) * NX, (place_ids, w_out, down), smem=(0,)
    )
    parts = list(parts)
    for d in range(1, NX):
        parts[d] = x_swapped(parts[d], d)
    return (up_here, up_there), parts


def layer(tokens, node_ids, gates, w_in, w_out):
    shape = jax.ShapeDtypeStruct
    core, xh, xl = (lax.axis_index(a).astype(jnp.int32) for a in ROW)
    place_ids = jnp.stack([core, xh, xh * NXL + xl])

    sent = call(
        spread_body,
        shape((TOK * TOK, LANES), BF16),
        (node_ids[0], gates[0], tokens[0]),
        scratch=(
            pltpu.VMEM((1, 4), jnp.int32),
            pltpu.VMEM((1, 8), BF16),
            pltpu.VMEM((1, 2 * HALF * LANES), BF16),
            pltpu.VMEM((2 * TOK, LANES), F32),
            pltpu.SemaphoreType.DMA((3,)),
        ),
        far=True,
    )
    sent, w_in, w_out = lax.optimization_barrier((sent, w_in, w_out))
    arrived = exchange(sent, COLUMN, NZ * NC)
    w_up, w_down = spread_weights(place_ids, w_in.reshape(4 * WIDTH, 2 * LANES), w_out[0])

    packed, gate_rows = call(
        pack_body,
        (shape((NY * NX * BLOCK_ROWS, LANES), BF16), shape((TOK, LANES), F32)),
        (arrived,),
    )
    rows = exchange(packed, PLANE, NY * NX)

    partial_sums, gate, balance = call(
        up_body,
        (shape((8 * ROWS, LANES), BF16), shape((ROWS, LANES), F32), shape((1,), F32)),
        (place_ids, rows, *w_up),
        scratch=(pltpu.VMEM((EIGHTH + 1, ROWS, LANES), F32),),
        smem=(0,),
        smem_out=(2,),
        flops=10**9,
    )
    summands = exchange(partial_sums, ROW, 8)

    hidden = call(hidden_body, shape((4 * ROWS, LANES), BF16), (summands, gate))
    every_hidden = exchange(hidden, ROW, 8)

    down = call(
        down_body,
        shape((NY * NX * BLOCK_ROWS, LANES), BF16),
        (place_ids, every_hidden, *w_down),
        scratch=(pltpu.VMEM((ROWS, WIDTH), F32),),
        smem=(0,),
        flops=10**9,
    )
    returned = exchange(down, PLANE, NY * NX)

    unpacked = call(
        unpack_body,
        shape((TOK * TOK, LANES), BF16),
        (returned, gate_rows),
    )
    back = exchange(unpacked, COLUMN, NZ * NC)

    mixed = call(
        finish_body,
        shape((1, 2 * HALF * LANES), BF16),
        (back,),
        scratch=(pltpu.VMEM((2 * TOK, LANES), F32),),
    )
    return mixed[None], balance


def solution(mesh):
    fine = Mesh(mesh.devices.reshape(NZ, NC, NY, NXH, NXL), AXES)
    token_spec = P(PLANE, COLUMN, None)
    return jax.shard_map(
        layer,
        mesh=fine,
        in_specs=(
            token_spec,
            token_spec,
            token_spec,
            P(AXES, None, None),
            P(COLUMN, PLANE, None),
        ),
        out_specs=(token_spec, P(COLUMN)),
        check_vma=False,
    )
```

time: 192 us -> 186 us (0.969)
  blocking collectives: 35.6 us -> 48.9 us
  waiting for transfers between devices: 72.1 us -> 59.6 us
  local copies, waits for them, and re-layouts: 10.9 us -> 6.41 us
    all_to_all x2, blocking collectives: 35.6 us -> 48.9 us  [exchange(): lax.all_to_all(x.reshape(members, rows, x.shape[1]), axes, split_axis=0,...]
    all_to_all x4, waiting for transfers between devices: 34.6 us -> 23 us  [exchange(): lax.all_to_all(x.reshape(members, rows, x.shape[1]), axes, split_axis=0,...]
    unnamed x44 -> x18, local copies, waits for them, and re-layouts: 9.74 us -> 6.41 us
    pallas_call x9 -> x10, Pallas kernels: 11.9 us -> 12.3 us  [call(): pl.pallas_call(body, out_shape=outs, in_specs=[far_spec if far else spec(...]
where the time goes in v3:
time: 186 us; the launch traced here: 185 us
  waiting for transfers between devices  59.6 us (32%)
  starting transfers between devices  57.2 us (31%)
  blocking collectives  48.9 us (26%)
  Pallas kernels  12.3 us (7%)
  local copies, waits for them, and re-layouts  6.41 us (3%)
    all_to_all x2, blocking collectives, exchange(): lax.all_to_all(x.reshape(members, rows, x.shape[1]), axes, split_axis=0,...  48.9 us
    all_to_all x4, starting transfers between devices, exchange(): lax.all_to_all(x.reshape(members, rows, x.shape[1]), axes, split_axis=0,...  38.8 us
    ppermute x3, waiting for transfers between devices, swapped(): return lax.ppermute(x, axis, [(0, 1), (1, 0)])  24.6 us
    all_to_all x4, waiting for transfers between devices, exchange(): lax.all_to_all(x.reshape(members, rows, x.shape[1]), axes, split_axis=0,...  23 us
    pallas_call x10, Pallas kernels, call(): pl.pallas_call(body, out_shape=outs, in_specs=[far_spec if far else spec(...  12.3 us
    ppermute x3, waiting for transfers between devices, x_swapped(): return lax.ppermute(x, ('xh', 'xl'), [(i, i ^ mask) for i in range(NX)])  11.9 us
    ppermute x3, starting transfers between devices, x_swapped(): return lax.ppermute(x, ('xh', 'xl'), [(i, i ^ mask) for i in range(NX)])  9.58 us
    ppermute x3, starting transfers between devices, swapped(): return lax.ppermute(x, axis, [(0, 1), (1, 0)])  8.76 us
  transfers between devices with their start and end apart: 10, of which 6 were waited for; matrix products, arithmetic and copies ran while one was open for 0% of the time, Pallas kernels for 2%

profile of v3, /device:TPU:1, one launch (start us, length us, event | category | flops | bytes accessed | tf_op | source)
XLA Modules:
  0.0 185.3 jit_solution(14612222579844332156)
XLA Ops:
  0.6 1.7 shard_map.68
  2.3 20.4 %all-to-all-start = ((bf16[32,32,128]{2,1,0:T(8,128)(2,1)}), bf16[32,32,128]{2,1,0:T(8,128)(2,1)S(1)}, u32[]{:S(2)}, u32[]{:S(2)}) async-start(bf16[32,32,128]{2,1,0:T(8,128)(2,1)} %bitcast.6), calls=%async_computation | async-start | bytes 524288 | tf_op jit(solution)/shard_map/all_to_all | solution.py:270
  22.7 0.1 pad_add_fusion.place_ids
  22.8 0.0 copy-start
  22.8 1.5 copy-done
  24.3 0.0 copy-start.2
  24.3 1.2 copy-done.2
  25.5 0.0 copy-start.1
  25.5 1.6 shard_map.70
  27.1 0.0 copy-start.7
  27.1 0.8 copy-done.7
  27.8 2.1 %collective-permute-start = (bf16[1792,256]{1,0:T(8,128)(2,1)}, bf16[1792,256]{1,0:T(8,128)(2,1)S(1)}, u32[]{:S(2)}, u32[]{:S(2)}) collective-permute-start(bf16[1792,256]{1,0:T(8,128)(2,1)} %get-tuple-element.22), channel_id=1, source_target_pairs={{0,32},{32,0},{1,33},{33,1},{2,34},{34,2},{3,35},{35,3},{4,36},{36... | collective-permute-start | bytes 2752520 | tf_op jit(solution)/shard_map/ppermute | solution.py:277
  30.0 15.0 %all-to-all-done = bf16[32,32,128]{2,1,0:T(8,128)(2,1)S(1)} async-done(((bf16[32,32,128]{2,1,0:T(8,128)(2,1)}), bf16[32,32,128]{2,1,0:T(8,128)(2,1)S(1)}, u32[]{:S(2)}, u32[]{:S(2)}) %all-to-all-start) | async-done | bytes 262176 | tf_op jit(solution)/shard_map/all_to_all | solution.py:270
  45.0 0.8 shard_map.69
  45.8 0.0 copy-start.4
  45.8 0.8 copy-done.4
  46.6 9.7 %all-to-all-start.1 = ((bf16[32,64,128]{2,1,0:T(8,128)(2,1)}), bf16[32,64,128]{2,1,0:T(8,128)(2,1)S(1)}, u32[]{:S(2)}, u32[]{:S(2)}) async-start(bf16[32,64,128]{2,1,0:T(8,128)(2,1)} %bitcast.29), calls=%async_computation.1 | async-start | bytes 1048576 | tf_op jit(solution)/shard_map/all_to_all | solution.py:270
  56.3 0.0 collective-permute-done.up
  56.3 0.0 copy-done.1
  56.3 0.7 shard_map.71
  57.0 0.0 copy-start.5
  57.0 0.9 copy-done.5
  57.9 4.6 %collective-permute-start.1 = (bf16[1792,256]{1,0:T(8,128)(2,1)S(1)}, bf16[1792,256]{1,0:T(8,128)(2,1)S(1)}, u32[]{:S(2)}, u32[]{:S(2)}) collective-permute-start(bf16[1792,256]{1,0:T(8,128)(2,1)S(1)} %get-tuple-element.24), channel_id=1, source_target_pairs={{0,2},{2,0},{1,3},{3,1},{4,6},{6,4},{5,7},{7,5},{8,10},{10,8},{9,1... | collective-permute-start | bytes 2752520 | tf_op jit(solution)/shard_map/ppermute | solution.py:277
  62.6 24.6 %collective-permute-done.1.w_there = bf16[1792,256]{1,0:T(8,128)(2,1)S(1)} collective-permute-done((bf16[1792,256]{1,0:T(8,128)(2,1)S(1)}, bf16[1792,256]{1,0:T(8,128)(2,1)S(1)}, u32[]{:S(2)}, u32[]{:S(2)}) %collective-permute-start.1) | collective-permute-done | bytes 917536 | tf_op jit(solution)/shard_map/ppermute | solution.py:277
  87.1 0.0 all-to-all-done.1
  87.1 0.0 copy-start.6
  87.1 1.2 copy-done.6
  88.3 0.0 copy-start.8
  88.3 2.9 %shard_map.72 = (bf16[2304,128]{1,0:T(8,128)(2,1)}, f32[288,128]{1,0:T(8,128)S(1)}, f32[1]{0:T(128)}) custom-call(s32[3]{0:T(128)S(1)} %pad_add_fusion.place_ids, bf16[2048,128]{1,0:T(8,128)(2,1)S(1)} %bitcast.28, bf16[1792,256]{1,0:T(8,128)(2,1)S(1)} %copy-done.6, bf16[1792,256]{1,0:T(8,128)(2,1)S(1)} %collective-permute-done.1.w_there), custom_call_target="tpu_custom_call" | custom-call | flops 1000000000 | bytes 1000000 | tf_op jit(solution)/shard_map/pallas_call | solution.py:70
  91.2 0.0 copy-start.3
  91.2 5.1 %all-to-all-start.2 = ((bf16[8,288,128]{2,1,0:T(8,128)(2,1)}), bf16[8,288,128]{2,1,0:T(8,128)(2,1)S(1)}, u32[]{:S(2)}, u32[]{:S(2)}) async-start(bf16[8,288,128]{2,1,0:T(8,128)(2,1)} %bitcast.12), calls=%async_computation.2 | async-start | bytes 1179648 | tf_op jit(solution)/shard_map/all_to_all | solution.py:270
  96.3 0.0 copy-done.8
  96.3 2.0 %collective-permute-start.2 = (bf16[64,3584]{1,0:T(8,128)(2,1)S(1)}, bf16[64,3584]{1,0:T(8,128)(2,1)S(1)}, u32[]{:S(2)}, u32[]{:S(2)}) collective-permute-start(bf16[64,3584]{1,0:T(8,128)(2,1)S(1)} %copy-done.8), channel_id=1, source_target_pairs={{0,32},{32,0},{1,33},{33,1},{2,34},{34,2},{3,35},{35,3},{4,36},{36... | collective-permute-start | bytes 1376264 | tf_op jit(solution)/shard_map/ppermute | solution.py:277
  98.3 8.0 %all-to-all-done.2 = bf16[8,288,128]{2,1,0:T(8,128)(2,1)S(1)} async-done(((bf16[8,288,128]{2,1,0:T(8,128)(2,1)}), bf16[8,288,128]{2,1,0:T(8,128)(2,1)S(1)}, u32[]{:S(2)}, u32[]{:S(2)}) %all-to-all-start.2) | async-done | bytes 589856 | tf_op jit(solution)/shard_map/all_to_all | solution.py:270
  106.4 0.9 shard_map.73
  107.3 3.6 %all-to-all-start.3 = ((bf16[8,144,128]{2,1,0:T(8,128)(2,1)}), bf16[8,144,128]{2,1,0:T(8,128)(2,1)S(1)}, u32[]{:S(2)}, u32[]{:S(2)}) async-start(bf16[8,144,128]{2,1,0:T(8,128)(2,1)} %bitcast.14), calls=%async_computation.3 | async-start | bytes 589824 | tf_op jit(solution)/shard_map/all_to_all | solution.py:270
  110.9 0.0 collective-permute-done.2.down
  110.9 0.0 copy-done.3
  110.9 0.6 shard_map.74
  111.6 3.3 %collective-permute-start.3 = (bf16[128,896]{1,0:T(8,128)(2,1)S(1)}, bf16[128,896]{1,0:T(8,128)(2,1)S(1)}, u32[]{:S(2)}, u32[]{:S(2)}) collective-permute-start(bf16[128,896]{1,0:T(8,128)(2,1)S(1)} %get-tuple-element.29), channel_id=1, source_target_pairs={{0,1},{1,0},{2,3},{3,2},{4,5},{5,4},{6,7},{7,6},{8,9},{9,8},{10,11... | collective-permute-start | bytes 688136 | tf_op jit(solution)/shard_map/ppermute | solution.py:281
  114.8 4.3 %collective-permute-start.4 = (bf16[128,896]{1,0:T(8,128)(2,1)S(1)}, bf16[128,896]{1,0:T(8,128)(2,1)S(1)}, u32[]{:S(2)}, u32[]{:S(2)}) collective-permute-start(bf16[128,896]{1,0:T(8,128)(2,1)S(1)} %get-tuple-element.30), channel_id=1, source_target_pairs={{0,2},{1,3},{2,0},{3,1},{4,6},{5,7},{6,4},{7,5},{8,10},{9,11},{10,... | collective-permute-start | bytes 688136 | tf_op jit(solution)/shard_map/ppermute | solution.py:281
  119.2 2.0 %collective-permute-start.5 = (bf16[128,896]{1,0:T(8,128)(2,1)S(1)}, bf16[128,896]{1,0:T(8,128)(2,1)S(1)}, u32[]{:S(2)}, u32[]{:S(2)}) collective-permute-start(bf16[128,896]{1,0:T(8,128)(2,1)S(1)} %get-tuple-element.31), channel_id=1, source_target_pairs={{0,3},{1,2},{2,1},{3,0},{4,7},{5,6},{6,5},{7,4},{8,11},{9,10},{10,... | collective-permute-start | bytes 688136 | tf_op jit(solution)/shard_map/ppermute | solution.py:281
  121.2 0.1 collective-permute-done.3.w1
  121.3 6.2 %collective-permute-done.4.w2 = bf16[128,896]{1,0:T(8,128)(2,1)S(1)} collective-permute-done((bf16[128,896]{1,0:T(8,128)(2,1)S(1)}, bf16[128,896]{1,0:T(8,128)(2,1)S(1)}, u32[]{:S(2)}, u32[]{:S(2)}) %collective-permute-start.4) | collective-permute-done | bytes 229408 | tf_op jit(solution)/shard_map/ppermute | solution.py:281
  127.5 5.6 %collective-permute-done.5.w3 = bf16[128,896]{1,0:T(8,128)(2,1)S(1)} collective-permute-done((bf16[128,896]{1,0:T(8,128)(2,1)S(1)}, bf16[128,896]{1,0:T(8,128)(2,1)S(1)}, u32[]{:S(2)}, u32[]{:S(2)}) %collective-permute-start.5) | collective-permute-done | bytes 229408 | tf_op jit(solution)/shard_map/ppermute | solution.py:281
  133.1 0.0 all-to-all-done.3
  133.1 1.9 %shard_map.75 = bf16[2048,128]{1,0:T(8,128)(2,1)S(1)} custom-call(s32[3]{0:T(128)S(1)} %pad_add_fusion.place_ids, bf16[1152,128]{1,0:T(8,128)(2,1)S(1)} %bitcast.31, bf16[128,896]{1,0:T(8,128)(2,1)S(1)} %get-tuple-element.28.w0, bf16[128,896]{1,0:T(8,128)(2,1)S(1)} %collective-permute-done.3.w1, bf16[128,896]{1,0:T(8,128)(2,1)S(1)} %collective-permute-done.4.w2, ...), custom_call_target="tpu_custom_call" | custom-call | flops 1000000000 | bytes 1000000 | tf_op jit(solution)/shard_map/pallas_call | solution.py:70
  135.0 22.5 %all_to_all.30 = bf16[32,64,128]{2,1,0:T(8,128)(2,1)S(1)} all-to-all(bf16[32,64,128]{2,1,0:T(8,128)(2,1)S(1)} %bitcast.30), channel_id=1, replica_groups=mesh['z'=16,'c'=2,'y'=8,'xh'=2,'xl'=2] {'y','xh','xl'}, dimensions={0} | all-to-all | bytes 1048576 | tf_op jit(solution)/shard_map/all_to_all | solution.py:270
  157.6 0.6 shard_map.76
  158.2 26.4 %all_to_all.31 = bf16[32,32,128]{2,1,0:T(8,128)(2,1)S(1)} all-to-all(bf16[32,32,128]{2,1,0:T(8,128)(2,1)S(1)} %bitcast.27), channel_id=1, replica_groups=mesh['z'=16,'c'=2,'y'=8,'xh'=2,'xl'=2] {'z','c'}, dimensions={0} | all-to-all | bytes 524288 | tf_op jit(solution)/shard_map/all_to_all | solution.py:270
  184.6 0.7 shard_map.77
Async XLA Ops:
  2.3 42.7 %all-to-all-start = ((bf16[32,32,128]{2,1,0:T(8,128)(2,1)}), bf16[32,32,128]{2,1,0:T(8,128)(2,1)S(1)}, u32[]{:S(2)}, u32[]{:S(2)}) async-start(bf16[32,32,128]{2,1,0:T(8,128)(2,1)} %bitcast.6), calls=%async_computation | async-start | bytes 524288 | tf_op jit(solution)/shard_map/all_to_all | solution.py:270
  22.8 1.5 copy-start
  24.3 1.2 copy-start.2
  25.5 30.8 %copy-start.1 = (bf16[1,3584,256]{2,1,0:T(8,128)(2,1)S(1)}, bf16[1,3584,256]{2,1,0:T(8,128)(2,1)}, u32[]{:S(2)}) copy-start(bf16[1,3584,256]{2,1,0:T(8,128)(2,1)} %param.8) | copy-start | bytes 5505028
  27.1 0.8 copy-start.7
  27.8 28.4 %collective-permute-start = (bf16[1792,256]{1,0:T(8,128)(2,1)}, bf16[1792,256]{1,0:T(8,128)(2,1)S(1)}, u32[]{:S(2)}, u32[]{:S(2)}) collective-permute-start(bf16[1792,256]{1,0:T(8,128)(2,1)} %get-tuple-element.22), channel_id=1, source_target_pairs={{0,32},{32,0},{1,33},{33,1},{2,34},{34,2},{3,35},{35,3},{4,36},{36... | collective-permute-start | bytes 2752520 | tf_op jit(solution)/shard_map/ppermute | solution.py:277
  45.8 0.8 copy-start.4
  46.6 40.5 %all-to-all-start.1 = ((bf16[32,64,128]{2,1,0:T(8,128)(2,1)}), bf16[32,64,128]{2,1,0:T(8,128)(2,1)S(1)}, u32[]{:S(2)}, u32[]{:S(2)}) async-start(bf16[32,64,128]{2,1,0:T(8,128)(2,1)} %bitcast.29), calls=%async_computation.1 | async-start | bytes 1048576 | tf_op jit(solution)/shard_map/all_to_all | solution.py:270
  57.0 0.9 copy-start.5
  57.9 29.2 %collective-permute-start.1 = (bf16[1792,256]{1,0:T(8,128)(2,1)S(1)}, bf16[1792,256]{1,0:T(8,128)(2,1)S(1)}, u32[]{:S(2)}, u32[]{:S(2)}) collective-permute-start(bf16[1792,256]{1,0:T(8,128)(2,1)S(1)} %get-tuple-element.24), channel_id=1, source_target_pairs={{0,2},{2,0},{1,3},{3,1},{4,6},{6,4},{5,7},{7,5},{8,10},{10,8},{9,1... | collective-permute-start | bytes 2752520 | tf_op jit(solution)/shard_map/ppermute | solution.py:277
  87.1 1.2 copy-start.6
  88.3 8.0 %copy-start.8 = (bf16[64,3584]{1,0:T(8,128)(2,1)S(1)}, bf16[64,3584]{1,0:T(8,128)(2,1)}, u32[]{:S(2)}) copy-start(bf16[64,3584]{1,0:T(8,128)(2,1)} %copy-done.7) | copy-start | bytes 1376260
  91.2 19.7 %copy-start.3 = (bf16[1,64,7168]{2,1,0:T(8,128)(2,1)S(1)}, bf16[1,64,7168]{2,1,0:T(8,128)(2,1)}, u32[]{:S(2)}) copy-start(bf16[1,64,7168]{2,1,0:T(8,128)(2,1)} %param.9) | copy-start | bytes 2752516
  91.2 15.2 %all-to-all-start.2 = ((bf16[8,288,128]{2,1,0:T(8,128)(2,1)}), bf16[8,288,128]{2,1,0:T(8,128)(2,1)S(1)}, u32[]{:S(2)}, u32[]{:S(2)}) async-start(bf16[8,288,128]{2,1,0:T(8,128)(2,1)} %bitcast.12), calls=%async_computation.2 | async-start | bytes 1179648 | tf_op jit(solution)/shard_map/all_to_all | solution.py:270
  96.3 14.6 %collective-permute-start.2 = (bf16[64,3584]{1,0:T(8,128)(2,1)S(1)}, bf16[64,3584]{1,0:T(8,128)(2,1)S(1)}, u32[]{:S(2)}, u32[]{:S(2)}) collective-permute-start(bf16[64,3584]{1,0:T(8,128)(2,1)S(1)} %copy-done.8), channel_id=1, source_target_pairs={{0,32},{32,0},{1,33},{33,1},{2,34},{34,2},{3,35},{35,3},{4,36},{36... | collective-permute-start | bytes 1376264 | tf_op jit(solution)/shard_map/ppermute | solution.py:277
  107.3 25.8 %all-to-all-start.3 = ((bf16[8,144,128]{2,1,0:T(8,128)(2,1)}), bf16[8,144,128]{2,1,0:T(8,128)(2,1)S(1)}, u32[]{:S(2)}, u32[]{:S(2)}) async-start(bf16[8,144,128]{2,1,0:T(8,128)(2,1)} %bitcast.14), calls=%async_computation.3 | async-start | bytes 589824 | tf_op jit(solution)/shard_map/all_to_all | solution.py:270
  111.6 9.7 %collective-permute-start.3 = (bf16[128,896]{1,0:T(8,128)(2,1)S(1)}, bf16[128,896]{1,0:T(8,128)(2,1)S(1)}, u32[]{:S(2)}, u32[]{:S(2)}) collective-permute-start(bf16[128,896]{1,0:T(8,128)(2,1)S(1)} %get-tuple-element.29), channel_id=1, source_target_pairs={{0,1},{1,0},{2,3},{3,2},{4,5},{5,4},{6,7},{7,6},{8,9},{9,8},{10,11... | collective-permute-start | bytes 688136 | tf_op jit(solution)/shard_map/ppermute | solution.py:281
  114.8 12.7 %collective-permute-start.4 = (bf16[128,896]{1,0:T(8,128)(2,1)S(1)}, bf16[128,896]{1,0:T(8,128)(2,1)S(1)}, u32[]{:S(2)}, u32[]{:S(2)}) collective-permute-start(bf16[128,896]{1,0:T(8,128)(2,1)S(1)} %get-tuple-element.30), channel_id=1, source_target_pairs={{0,2},{1,3},{2,0},{3,1},{4,6},{5,7},{6,4},{7,5},{8,10},{9,11},{10,... | collective-permute-start | bytes 688136 | tf_op jit(solution)/shard_map/ppermute | solution.py:281
  119.2 14.0 %collective-permute-start.5 = (bf16[128,896]{1,0:T(8,128)(2,1)S(1)}, bf16[128,896]{1,0:T(8,128)(2,1)S(1)}, u32[]{:S(2)}, u32[]{:S(2)}) collective-permute-start(bf16[128,896]{1,0:T(8,128)(2,1)S(1)} %get-tuple-element.31), channel_id=1, source_target_pairs={{0,3},{1,2},{2,1},{3,0},{4,7},{5,6},{6,5},{7,4},{8,11},{9,10},{10,... | collective-permute-start | bytes 688136 | tf_op jit(solution)/shard_map/ppermute | solution.py:281

commit v4 on v3

--- a/solution.py
+++ b/solution.py
@@ -10,20 +10,23 @@
 F32 = jnp.float32
 BF16 = jnp.bfloat16
 
-NZ, NC, NY, NXH, NXL = 16, 2, 8, 2, 2
-NX = NXH * NXL
-AXES = ("z", "c", "y", "xh", "xl")
+NZ, NC, NYH, NYL, NXH, NXL = 16, 2, 4, 2, 2, 2
+COLUMNS = NYH * NYL * NXH * NXL
+NQ = NYL * NXL
+AXES = ("z", "c", "yh", "yl", "xh", "xl")
 COLUMN = ("z", "c")
-PLANE = ("y", "xh", "xl")
-ROW = ("c", "xh", "xl")
+PLANE = ("yh", "yl", "xh", "xl")
+QUAD = ("yl", "xl")
+TEAM = ("c", "yl", "xl")
+
 
 LANES = 128
 SLOTS = 9
 EIGHTH = 7
-HALF = NX * EIGHTH
+HALF = NQ * EIGHTH
 TOK = 32
 BLOCK_ROWS = 64
-ROWS = NY * NX * SLOTS
+ROWS = COLUMNS * SLOTS
 PAIR = ROWS // 4
 BLOCK = 64
 WIDTH = EIGHTH * LANES
@@ -88,11 +91,11 @@
     for copy in copies:
         copy.wait()
     for c in range(NC):
-        for xh in range(NXH):
+        for yl in range(NYL):
             for xl in range(NXL):
                 for k in range(EIGHTH):
-                    row = c * TOK + (xh * NXL + xl) * EIGHTH + k
-                    i = xl * HALF + (c * NXH + xh) * EIGHTH + k
+                    row = c * TOK + (yl * NXL + xl) * EIGHTH + k
+                    i = xl * HALF + (c * NYL + yl) * EIGHTH + k
                     base[row : row + 1, :] = token[:, i * LANES : (i + 1) * LANES].astype(F32)
         base[c * TOK + HALF : (c + 1) * TOK, :] = jnp.zeros((TOK - HALF, LANES), F32)
     tile = (8, LANES)
@@ -143,7 +146,7 @@
     spread = dot(by_token.astype(BF16), one_hot(a, token_of))
     chunk = lax.bitwise_and(b[0:1], TOK - 1).astype(F32)
     col_key = chunk * 16.0 + spread[0:1]
-    row_key = chunk_and_slot(iota((NX * BLOCK_ROWS, 1), 0))
+    row_key = chunk_and_slot(iota((NQ * BLOCK_ROWS, 1), 0))
     packed = dot(one_hot(row_key, col_key), arrived[...])
     lane = lax.broadcasted_iota(jnp.int32, (TOK, LANES), 1)
     wanted = lax.bitwise_and(lane, 15).astype(F32) == slot
@@ -152,13 +155,14 @@
     row = lax.broadcasted_iota(jnp.int32, packed.shape, 0)
     last = lax.bitwise_and(row, BLOCK_ROWS - 1) == BLOCK_ROWS - 1
     packed = jnp.where(last, gate_line, packed).astype(BF16)
-    for y in range(NY):
-        out[y * NX * BLOCK_ROWS : (y + 1) * NX * BLOCK_ROWS, :] = packed
+    for t in range(COLUMNS):
+        v = t // (NXH * NXL) % NYL * NXL + t % NXL
+        out[t * BLOCK_ROWS : (t + 1) * BLOCK_ROWS, :] = packed[v * BLOCK_ROWS : (v + 1) * BLOCK_ROWS]
 
 
 def up_body(place_ids, rows, w_here, w_there, out, gate_out, balance_out, x):
-    core, xh = place_ids[0], place_ids[1]
-    n = 2 * NX * BLOCK_ROWS
+    core, yl = place_ids[0], place_ids[1]
+    n = COLUMNS // 4 * BLOCK_ROWS
     column, row = divided(iota((1, n), 1), BLOCK_ROWS)
     k, r = divided(row, SLOTS)
     of_pair, _ = divided(iota((PAIR, 1), 0), SLOTS)
@@ -187,8 +191,8 @@
         both = dot(features, w[WIDTH * (j % 2) : WIDTH * (j % 2 + 1), :])
         g, u = both[:, :LANES], both[:, LANES:]
         expert = core if j % 2 == 0 else 1 - core
-        part = xh if j < 2 else 1 - xh
-        at = ROWS * 2 * (expert * NXH + part)
+        part = yl if j < 2 else 1 - yl
+        at = ROWS * 2 * (expert * NYL + part)
         out[pl.ds(pl.multiple_of(at, ROWS), ROWS), :] = jnp.where(left, g, swap_halves(u)).astype(BF16)
         at = at + ROWS
         out[pl.ds(pl.multiple_of(at, ROWS), ROWS), :] = jnp.where(left, swap_halves(g), u).astype(BF16)
@@ -207,16 +211,16 @@
 
 
 def down_body(place_ids, hidden, w0, w1, w2, w3, out, acc):
-    core, x = place_ids[0], place_ids[2]
+    core, quad = place_ids[0], place_ids[2]
     half = ROWS // 2
     left = left_half((half, LANES))
 
     def block(expert, source):
-        at = pl.multiple_of((expert * NX + source) * half, half)
+        at = pl.multiple_of((expert * NQ + source) * half, half)
         return hidden[pl.ds(at, half), :].astype(F32)
 
     for d, w in enumerate((w0, w1, w2, w3)):
-        source = lax.bitwise_xor(x, jnp.int32(d))
+        source = lax.bitwise_xor(quad, jnp.int32(d))
         a, b = block(core, source), block(1 - core, source)
         top = dot(jnp.where(left, a, swap_halves(b)).astype(BF16), w[...])
         bottom = dot(jnp.where(left, swap_halves(a), b).astype(BF16), w[...])
@@ -226,7 +230,7 @@
         else:
             acc[0:half, :] += top
             acc[half:ROWS, :] += bottom
-    n = 2 * NX * BLOCK_ROWS
+    n = COLUMNS // 4 * BLOCK_ROWS
     k, row = divided(iota((1, EIGHTH * PAIR), 1), PAIR)
     column, r = divided(row, SLOTS)
     q = one_hot(iota((n, EIGHTH * PAIR), 0), column * BLOCK_ROWS + k * SLOTS + r)
@@ -239,10 +243,17 @@
 
 
 def unpack_body(parts, gate_rows, out):
-    n = NX * BLOCK_ROWS
-    total = parts[0:n, :].astype(F32)
-    for y in range(1, NY):
-        total = total + parts[n * y : n * (y + 1), :].astype(F32)
+    n = NQ * BLOCK_ROWS
+    blocks = []
+    for yl in range(NYL):
+        for xl in range(NXL):
+            block = jnp.zeros((BLOCK_ROWS, LANES), F32)
+            for yh in range(NYH):
+                for xh in range(NXH):
+                    t = ((yh * NYL + yl) * NXH + xh) * NXL + xl
+                    block = block + parts[t * BLOCK_ROWS : (t + 1) * BLOCK_ROWS, :].astype(F32)
+            blocks.append(block)
+    total = jnp.concatenate(blocks, axis=0)
     slot = slot_of(gate_rows[...])
     a = lax.broadcasted_iota(jnp.int32, (TOK * TOK, TOK), 0)
     b = lax.broadcasted_iota(jnp.int32, (TOK * TOK, TOK), 1)
@@ -277,63 +288,63 @@
     return lax.ppermute(x, axis, [(0, 1), (1, 0)])
 
 
-def x_swapped(x, mask):
-    return lax.ppermute(x, ("xh", "xl"), [(i, i ^ mask) for i in range(NX)])
+def quad_swapped(x, mask):
+    return lax.ppermute(x, QUAD, [(i, i ^ mask) for i in range(NQ)])
 
 
 def rows_at(start, size):
     return pl.ds(pl.multiple_of(start, size), size)
 
 
-def core_body(place_ids, w_in, w_out, up, down):
-    other = 1 - place_ids[0]
-    up[...] = w_in[rows_at(other * 2 * WIDTH, 2 * WIDTH), :]
-    down[...] = w_out[:, rows_at(other * NX * WIDTH, NX * WIDTH)]
-
-
-def up_row_body(place_ids, w_in, up, here, there):
-    core, xh = place_ids[0], place_ids[1]
-    for out, side in ((here, xh), (there, 1 - xh)):
+def up_core_body(place_ids, w_in, up):
+    up[...] = w_in[rows_at((1 - place_ids[0]) * 2 * WIDTH, 2 * WIDTH), :]
+
+
+def down_core_body(place_ids, w_out, down):
+    down[...] = w_out[:, rows_at((1 - place_ids[0]) * NQ * WIDTH, NQ * WIDTH)]
+
+
+def up_quad_body(place_ids, w_in, up, here, there):
+    core, yl = place_ids[0], place_ids[1]
+    for out, side in ((here, yl), (there, 1 - yl)):
         out[0:WIDTH, :] = w_in[rows_at((2 * core + side) * WIDTH, WIDTH), :]
         out[WIDTH : 2 * WIDTH, :] = up[rows_at(side * WIDTH, WIDTH), :]
 
 
-def down_row_body(place_ids, w_out, down, *outs):
-    core, x = place_ids[0], place_ids[2]
+def down_quad_body(place_ids, w_out, down, *outs):
+    core, quad = place_ids[0], place_ids[2]
     for d, out in enumerate(outs):
-        to = lax.bitwise_xor(x, jnp.int32(d))
-        out[0:BLOCK, :] = w_out[:, rows_at((core * NX + to) * WIDTH, WIDTH)]
+        to = lax.bitwise_xor(quad, jnp.int32(d))
+        out[0:BLOCK, :] = w_out[:, rows_at((core * NQ + to) * WIDTH, WIDTH)]
         out[BLOCK : 2 * BLOCK, :] = down[:, rows_at(to * WIDTH, WIDTH)]
 
 
 def spread_weights(place_ids, w_in, w_out):
     shape = jax.ShapeDtypeStruct
     up_shape, down_shape = shape((2 * WIDTH, 2 * LANES), BF16), shape((2 * BLOCK, WIDTH), BF16)
-    up, down = call(
-        core_body,
-        (up_shape, shape((BLOCK, NX * WIDTH), BF16)),
-        (place_ids, w_in, w_out),
-        smem=(0,),
-    )
+    up = call(up_core_body, up_shape, (place_ids, w_in), smem=(0,))
     up = swapped(up, "c")
+    up_here, up_there = call(
+        up_quad_body, (up_shape,) * 2, (place_ids, w_in, up), smem=(0,)
+    )
+    up_there = swapped(up_there, "yl")
+    down = call(
+        down_core_body, shape((BLOCK, NQ * WIDTH), BF16), (place_ids, w_out), smem=(0,)
+    )
     down = swapped(down, "c")
-    up_here, up_there = call(
-        up_row_body, (up_shape,) * 2, (place_ids, w_in, up), smem=(0,)
-    )
-    up_there = swapped(up_there, "xh")
     parts = call(
-        down_row_body, (down_shape,) * NX, (place_ids, w_out, down), smem=(0,)
+        down_quad_body, (down_shape,) * NQ, (place_ids, w_out, down), smem=(0,)
     )
     parts = list(parts)
-    for d in range(1, NX):
-        parts[d] = x_swapped(parts[d], d)
+    for d in range(1, NQ):
+        parts[d] = quad_swapped(parts[d], d)
     return (up_here, up_there), parts
 
 
 def layer(tokens, node_ids, gates, w_in, w_out):
     shape = jax.ShapeDtypeStruct
-    core, xh, xl = (lax.axis_index(a).astype(jnp.int32) for a in ROW)
-    place_ids = jnp.stack([core, xh, xh * NXL + xl])
+    core, yl, xl = (lax.axis_index(a).astype(jnp.int32) for a in TEAM)
+    place_ids = jnp.stack([core, yl, yl * NXL + xl])
 
     sent = call(
         spread_body,
@@ -354,10 +365,10 @@
 
     packed, gate_rows = call(
         pack_body,
-        (shape((NY * NX * BLOCK_ROWS, LANES), BF16), shape((TOK, LANES), F32)),
+        (shape((COLUMNS * BLOCK_ROWS, LANES), BF16), shape((TOK, LANES), F32)),
         (arrived,),
     )
-    rows = exchange(packed, PLANE, NY * NX)
+    rows = exchange(packed, PLANE, COLUMNS)
 
     partial_sums, gate, balance = call(
         up_body,
@@ -368,20 +379,20 @@
         smem_out=(2,),
         flops=10**9,
     )
-    summands = exchange(partial_sums, ROW, 8)
+    summands = exchange(partial_sums, TEAM, 8)
 
     hidden = call(hidden_body, shape((4 * ROWS, LANES), BF16), (summands, gate))
-    every_hidden = exchange(hidden, ROW, 8)
+    every_hidden = exchange(hidden, TEAM, 8)
 
     down = call(
         down_body,
-        shape((NY * NX * BLOCK_ROWS, LANES), BF16),
+        shape((COLUMNS * BLOCK_ROWS, LANES), BF16),
         (place_ids, every_hidden, *w_down),
         scratch=(pltpu.VMEM((ROWS, WIDTH), F32),),
         smem=(0,),
         flops=10**9,
     )
-    returned = exchange(down, PLANE, NY * NX)
+    returned = exchange(down, PLANE, COLUMNS)
 
     unpacked = call(
         unpack_body,
@@ -400,7 +411,7 @@
 
 
 def solution(mesh):
-    fine = Mesh(mesh.devices.reshape(NZ, NC, NY, NXH, NXL), AXES)
+    fine = Mesh(mesh.devices.reshape(NZ, NC, NYH, NYL, NXH, NXL), AXES)
     token_spec = P(PLANE, COLUMN, None)
     return jax.shard_map(
         layer,

time: 186 us -> 187 us (level)
  starting transfers between devices: 57.2 us -> 54.2 us
  blocking collectives: 48.9 us -> 51.1 us
    ppermute x3, waiting for transfers between devices: 11.9 us -> 8.4 us  [quad_swapped(): return lax.ppermute(x, QUAD, [(i, i ^ mask) for i in range(NQ)])]
    ppermute x3, waiting for transfers between devices: 24.6 us -> 27.5 us  [swapped(): return lax.ppermute(x, axis, [(0, 1), (1, 0)])]
    all_to_all x2, blocking collectives: 48.9 us -> 51.1 us  [exchange(): lax.all_to_all(x.reshape(members, rows, x.shape[1]), axes, split_axis=0,...]
    pallas_call x10 -> x11, Pallas kernels: 12.3 us -> 12.9 us  [call(): pl.pallas_call(body, out_shape=outs, in_specs=[far_spec if far else spec(...]
    unnamed x18 -> x16, local copies, waits for them, and re-layouts: 6.41 us -> 6.57 us
  transfers between devices with their start and end apart: 10 -> 10, of which waited for: 6 -> 6; matrix products, arithmetic and copies ran while one was open for 0% -> 0% of each run, Pallas kernels for 2% -> 3%
where the time goes in v4:
time: 187 us; the launch traced here: 186 us
  waiting for transfers between devices  60.1 us (32%)
  starting transfers between devices  54.2 us (29%)
  blocking collectives  51.1 us (27%)
  Pallas kernels  12.9 us (7%)
  local copies, waits for them, and re-layouts  6.57 us (4%)
    all_to_all x2, blocking collectives, exchange(): lax.all_to_all(x.reshape(members, rows, x.shape[1]), axes, split_axis=0,...  51.1 us
    all_to_all x4, starting transfers between devices, exchange(): lax.all_to_all(x.reshape(members, rows, x.shape[1]), axes, split_axis=0,...  38.6 us
    ppermute x3, waiting for transfers between devices, swapped(): return lax.ppermute(x, axis, [(0, 1), (1, 0)])  27.5 us
    all_to_all x4, waiting for transfers between devices, exchange(): lax.all_to_all(x.reshape(members, rows, x.shape[1]), axes, split_axis=0,...  24.1 us
    pallas_call x11, Pallas kernels, call(): pl.pallas_call(body, out_shape=outs, in_specs=[far_spec if far else spec(...  12.9 us
    ppermute x3, waiting for transfers between devices, quad_swapped(): return lax.ppermute(x, QUAD, [(i, i ^ mask) for i in range(NQ)])  8.4 us
    ppermute x3, starting transfers between devices, quad_swapped(): return lax.ppermute(x, QUAD, [(i, i ^ mask) for i in range(NQ)])  8.37 us
    ppermute x3, starting transfers between devices, swapped(): return lax.ppermute(x, axis, [(0, 1), (1, 0)])  7.26 us
  transfers between devices with their start and end apart: 10, of which 6 were waited for; matrix products, arithmetic and copies ran while one was open for 0% of the time, Pallas kernels for 3%

profile of v4, /device:TPU:1, one launch (start us, length us, event | category | flops | bytes accessed | tf_op | source)
XLA Modules:
  0.0 185.8 jit_solution(11156940180612028819)
XLA Ops:
  0.6 1.6 shard_map.68
  2.3 20.4 %all-to-all-start = ((bf16[32,32,128]{2,1,0:T(8,128)(2,1)}), bf16[32,32,128]{2,1,0:T(8,128)(2,1)S(1)}, u32[]{:S(2)}, u32[]{:S(2)}) async-start(bf16[32,32,128]{2,1,0:T(8,128)(2,1)} %bitcast.6), calls=%async_computation | async-start | bytes 524288 | tf_op jit(solution)/shard_map/all_to_all | solution.py:281
  22.7 0.1 pad_add_fusion.place_ids
  22.8 0.0 copy-start
  22.8 1.5 copy-done
  24.3 0.0 copy-start.1
  24.3 1.6 shard_map.70
  25.8 2.1 %collective-permute-start = (bf16[1792,256]{1,0:T(8,128)(2,1)}, bf16[1792,256]{1,0:T(8,128)(2,1)S(1)}, u32[]{:S(2)}, u32[]{:S(2)}) collective-permute-start(bf16[1792,256]{1,0:T(8,128)(2,1)} %shard_map.70), channel_id=1, source_target_pairs={{0,32},{32,0},{1,33},{33,1},{2,34},{34,2},{3,35},{35,3},{4,36},{36... | collective-permute-start | bytes 2752520 | tf_op jit(solution)/shard_map/ppermute | solution.py:288
  28.0 17.0 %all-to-all-done = bf16[32,32,128]{2,1,0:T(8,128)(2,1)S(1)} async-done(((bf16[32,32,128]{2,1,0:T(8,128)(2,1)}), bf16[32,32,128]{2,1,0:T(8,128)(2,1)S(1)}, u32[]{:S(2)}, u32[]{:S(2)}) %all-to-all-start) | async-done | bytes 262176 | tf_op jit(solution)/shard_map/all_to_all | solution.py:281
  45.0 0.8 shard_map.69
  45.8 0.0 copy-start.3
  45.8 0.8 copy-done.3
  46.6 9.7 %all-to-all-start.1 = ((bf16[32,64,128]{2,1,0:T(8,128)(2,1)}), bf16[32,64,128]{2,1,0:T(8,128)(2,1)S(1)}, u32[]{:S(2)}, u32[]{:S(2)}) async-start(bf16[32,64,128]{2,1,0:T(8,128)(2,1)} %bitcast.29), calls=%async_computation.1 | async-start | bytes 1048576 | tf_op jit(solution)/shard_map/all_to_all | solution.py:281
  56.3 0.0 collective-permute-done.up
  56.3 0.0 copy-done.1
  56.3 0.7 shard_map.71
  57.0 0.0 copy-start.4
  57.0 0.9 copy-done.4
  57.9 3.1 %collective-permute-start.1 = (bf16[1792,256]{1,0:T(8,128)(2,1)S(1)}, bf16[1792,256]{1,0:T(8,128)(2,1)S(1)}, u32[]{:S(2)}, u32[]{:S(2)}) collective-permute-start(bf16[1792,256]{1,0:T(8,128)(2,1)S(1)} %get-tuple-element.20), channel_id=1, source_target_pairs={{0,4},{4,0},{1,5},{5,1},{2,6},{6,2},{3,7},{7,3},{8,12},{12,8},{9,1... | collective-permute-start | bytes 2752520 | tf_op jit(solution)/shard_map/ppermute | solution.py:288
  61.0 27.5 %collective-permute-done.1.w_there = bf16[1792,256]{1,0:T(8,128)(2,1)S(1)} collective-permute-done((bf16[1792,256]{1,0:T(8,128)(2,1)S(1)}, bf16[1792,256]{1,0:T(8,128)(2,1)S(1)}, u32[]{:S(2)}, u32[]{:S(2)}) %collective-permute-start.1) | collective-permute-done | bytes 917536 | tf_op jit(solution)/shard_map/ppermute | solution.py:288
  88.6 0.0 copy-start.6
  88.6 1.0 copy-done.6
  89.5 0.0 all-to-all-done.1
  89.5 0.0 copy-start.5
  89.5 1.2 copy-done.5
  90.7 0.0 copy-start.7
  90.7 1.2 copy-done.7
  91.9 0.0 copy-start.2
  91.9 2.9 %shard_map.72 = (bf16[2304,128]{1,0:T(8,128)(2,1)}, f32[288,128]{1,0:T(8,128)S(1)}, f32[1]{0:T(128)}) custom-call(s32[3]{0:T(128)S(1)} %pad_add_fusion.place_ids, bf16[2048,128]{1,0:T(8,128)(2,1)S(1)} %bitcast.28, bf16[1792,256]{1,0:T(8,128)(2,1)S(1)} %copy-done.5, bf16[1792,256]{1,0:T(8,128)(2,1)S(1)} %copy-done.7), custom_call_target="tpu_custom_call" | custom-call | flops 1000000000 | bytes 1000000 | tf_op jit(solution)/shard_map/pallas_call | solution.py:73
  94.8 5.0 %all-to-all-start.2 = ((bf16[8,288,128]{2,1,0:T(8,128)(2,1)}), bf16[8,288,128]{2,1,0:T(8,128)(2,1)S(1)}, u32[]{:S(2)}, u32[]{:S(2)}) async-start(bf16[8,288,128]{2,1,0:T(8,128)(2,1)} %bitcast.11), calls=%async_computation.2 | async-start | bytes 1179648 | tf_op jit(solution)/shard_map/all_to_all | solution.py:281
  99.8 0.0 copy-done.2
  99.8 0.6 shard_map.74
  100.4 2.0 %collective-permute-start.2 = (bf16[64,3584]{1,0:T(8,128)(2,1)S(1)}, bf16[64,3584]{1,0:T(8,128)(2,1)S(1)}, u32[]{:S(2)}, u32[]{:S(2)}) collective-permute-start(bf16[64,3584]{1,0:T(8,128)(2,1)S(1)} %shard_map.74), channel_id=1, source_target_pairs={{0,32},{32,0},{1,33},{33,1},{2,34},{34,2},{3,35},{35,3},{4,36},{36... | collective-permute-start | bytes 1376264 | tf_op jit(solution)/shard_map/ppermute | solution.py:288
  102.4 7.1 %all-to-all-done.2 = bf16[8,288,128]{2,1,0:T(8,128)(2,1)S(1)} async-done(((bf16[8,288,128]{2,1,0:T(8,128)(2,1)}), bf16[8,288,128]{2,1,0:T(8,128)(2,1)S(1)}, u32[]{:S(2)}, u32[]{:S(2)}) %all-to-all-start.2) | async-done | bytes 589856 | tf_op jit(solution)/shard_map/all_to_all | solution.py:281
  109.6 0.9 shard_map.73
  110.5 3.5 %all-to-all-start.3 = ((bf16[8,144,128]{2,1,0:T(8,128)(2,1)}), bf16[8,144,128]{2,1,0:T(8,128)(2,1)S(1)}, u32[]{:S(2)}, u32[]{:S(2)}) async-start(bf16[8,144,128]{2,1,0:T(8,128)(2,1)} %bitcast.13), calls=%async_computation.3 | async-start | bytes 589824 | tf_op jit(solution)/shard_map/all_to_all | solution.py:281
  114.0 0.0 collective-permute-done.2.down
  114.0 0.6 shard_map.75
  114.6 3.3 %collective-permute-start.3 = (bf16[128,896]{1,0:T(8,128)(2,1)S(1)}, bf16[128,896]{1,0:T(8,128)(2,1)S(1)}, u32[]{:S(2)}, u32[]{:S(2)}) collective-permute-start(bf16[128,896]{1,0:T(8,128)(2,1)S(1)} %get-tuple-element.25), channel_id=1, source_target_pairs={{0,1},{1,0},{4,5},{5,4},{2,3},{3,2},{6,7},{7,6},{8,9},{9,8},{12,13... | collective-permute-start | bytes 688136 | tf_op jit(solution)/shard_map/ppermute | solution.py:292
  117.9 3.1 %collective-permute-start.4 = (bf16[128,896]{1,0:T(8,128)(2,1)S(1)}, bf16[128,896]{1,0:T(8,128)(2,1)S(1)}, u32[]{:S(2)}, u32[]{:S(2)}) collective-permute-start(bf16[128,896]{1,0:T(8,128)(2,1)S(1)} %get-tuple-element.26), channel_id=1, source_target_pairs={{0,4},{1,5},{4,0},{5,1},{2,6},{3,7},{6,2},{7,3},{8,12},{9,13},{12,... | collective-permute-start | bytes 688136 | tf_op jit(solution)/shard_map/ppermute | solution.py:292
  121.0 2.0 %collective-permute-start.5 = (bf16[128,896]{1,0:T(8,128)(2,1)S(1)}, bf16[128,896]{1,0:T(8,128)(2,1)S(1)}, u32[]{:S(2)}, u32[]{:S(2)}) collective-permute-start(bf16[128,896]{1,0:T(8,128)(2,1)S(1)} %get-tuple-element.27), channel_id=1, source_target_pairs={{0,5},{1,4},{4,1},{5,0},{2,7},{3,6},{6,3},{7,2},{8,13},{9,12},{12,... | collective-permute-start | bytes 688136 | tf_op jit(solution)/shard_map/ppermute | solution.py:292
  123.0 2.2 %collective-permute-done.3.w1 = bf16[128,896]{1,0:T(8,128)(2,1)S(1)} collective-permute-done((bf16[128,896]{1,0:T(8,128)(2,1)S(1)}, bf16[128,896]{1,0:T(8,128)(2,1)S(1)}, u32[]{:S(2)}, u32[]{:S(2)}) %collective-permute-start.3) | collective-permute-done | bytes 229408 | tf_op jit(solution)/shard_map/ppermute | solution.py:292
  125.2 1.1 collective-permute-done.4.w2
  126.3 5.1 %collective-permute-done.5.w3 = bf16[128,896]{1,0:T(8,128)(2,1)S(1)} collective-permute-done((bf16[128,896]{1,0:T(8,128)(2,1)S(1)}, bf16[128,896]{1,0:T(8,128)(2,1)S(1)}, u32[]{:S(2)}, u32[]{:S(2)}) %collective-permute-start.5) | collective-permute-done | bytes 229408 | tf_op jit(solution)/shard_map/ppermute | solution.py:292
  131.4 0.0 all-to-all-done.3
  131.4 1.9 %shard_map.76 = bf16[2048,128]{1,0:T(8,128)(2,1)S(1)} custom-call(s32[3]{0:T(128)S(1)} %pad_add_fusion.place_ids, bf16[1152,128]{1,0:T(8,128)(2,1)S(1)} %bitcast.31, bf16[128,896]{1,0:T(8,128)(2,1)S(1)} %get-tuple-element.24.w0, bf16[128,896]{1,0:T(8,128)(2,1)S(1)} %collective-permute-done.3.w1, bf16[128,896]{1,0:T(8,128)(2,1)S(1)} %collective-permute-done.4.w2, ...), custom_call_target="tpu_custom_call" | custom-call | flops 1000000000 | bytes 1000000 | tf_op jit(solution)/shard_map/pallas_call | solution.py:73
  133.3 23.5 %all_to_all.30 = bf16[32,64,128]{2,1,0:T(8,128)(2,1)S(1)} all-to-all(bf16[32,64,128]{2,1,0:T(8,128)(2,1)S(1)} %bitcast.30), channel_id=1, replica_groups=mesh['z'=16,'c'=2,'yh'=4,'yl'=2,'xh'=2,'xl'=2] {'yh','yl','xh','xl'}, dimensions={0} | all-to-all | bytes 1048576 | tf_op jit(solution)/shard_map/all_to_all | solution.py:281
  156.8 0.6 shard_map.77
  157.5 27.6 %all_to_all.31 = bf16[32,32,128]{2,1,0:T(8,128)(2,1)S(1)} all-to-all(bf16[32,32,128]{2,1,0:T(8,128)(2,1)S(1)} %bitcast.27), channel_id=1, replica_groups=mesh['z'=16,'c'=2,'yh'=4,'yl'=2,'xh'=2,'xl'=2] {'z','c'}, dimensions={0} | all-to-all | bytes 524288 | tf_op jit(solution)/shard_map/all_to_all | solution.py:281
  185.1 0.7 shard_map.78
Async XLA Ops:
  2.3 42.7 %all-to-all-start = ((bf16[32,32,128]{2,1,0:T(8,128)(2,1)}), bf16[32,32,128]{2,1,0:T(8,128)(2,1)S(1)}, u32[]{:S(2)}, u32[]{:S(2)}) async-start(bf16[32,32,128]{2,1,0:T(8,128)(2,1)} %bitcast.6), calls=%async_computation | async-start | bytes 524288 | tf_op jit(solution)/shard_map/all_to_all | solution.py:281
  22.8 1.5 copy-start
  24.3 32.0 %copy-start.1 = (bf16[1,3584,256]{2,1,0:T(8,128)(2,1)S(1)}, bf16[1,3584,256]{2,1,0:T(8,128)(2,1)}, u32[]{:S(2)}) copy-start(bf16[1,3584,256]{2,1,0:T(8,128)(2,1)} %param.8) | copy-start | bytes 5505028
  25.8 30.4 %collective-permute-start = (bf16[1792,256]{1,0:T(8,128)(2,1)}, bf16[1792,256]{1,0:T(8,128)(2,1)S(1)}, u32[]{:S(2)}, u32[]{:S(2)}) collective-permute-start(bf16[1792,256]{1,0:T(8,128)(2,1)} %shard_map.70), channel_id=1, source_target_pairs={{0,32},{32,0},{1,33},{33,1},{2,34},{34,2},{3,35},{35,3},{4,36},{36... | collective-permute-start | bytes 2752520 | tf_op jit(solution)/shard_map/ppermute | solution.py:288
  45.8 0.8 copy-start.3
  46.6 42.9 %all-to-all-start.1 = ((bf16[32,64,128]{2,1,0:T(8,128)(2,1)}), bf16[32,64,128]{2,1,0:T(8,128)(2,1)S(1)}, u32[]{:S(2)}, u32[]{:S(2)}) async-start(bf16[32,64,128]{2,1,0:T(8,128)(2,1)} %bitcast.29), calls=%async_computation.1 | async-start | bytes 1048576 | tf_op jit(solution)/shard_map/all_to_all | solution.py:281
  57.0 0.9 copy-start.4
  57.9 30.6 %collective-permute-start.1 = (bf16[1792,256]{1,0:T(8,128)(2,1)S(1)}, bf16[1792,256]{1,0:T(8,128)(2,1)S(1)}, u32[]{:S(2)}, u32[]{:S(2)}) collective-permute-start(bf16[1792,256]{1,0:T(8,128)(2,1)S(1)} %get-tuple-element.20), channel_id=1, source_target_pairs={{0,4},{4,0},{1,5},{5,1},{2,6},{6,2},{3,7},{7,3},{8,12},{12,8},{9,1... | collective-permute-start | bytes 2752520 | tf_op jit(solution)/shard_map/ppermute | solution.py:288
  88.6 1.0 copy-start.6
  89.5 1.2 copy-start.5
  90.7 1.2 copy-start.7
  91.9 8.0 %copy-start.2 = (bf16[1,64,7168]{2,1,0:T(8,128)(2,1)S(1)}, bf16[1,64,7168]{2,1,0:T(8,128)(2,1)}, u32[]{:S(2)}) copy-start(bf16[1,64,7168]{2,1,0:T(8,128)(2,1)} %param.9) | copy-start | bytes 2752516
  94.8 14.8 %all-to-all-start.2 = ((bf16[8,288,128]{2,1,0:T(8,128)(2,1)}), bf16[8,288,128]{2,1,0:T(8,128)(2,1)S(1)}, u32[]{:S(2)}, u32[]{:S(2)}) async-start(bf16[8,288,128]{2,1,0:T(8,128)(2,1)} %bitcast.11), calls=%async_computation.2 | async-start | bytes 1179648 | tf_op jit(solution)/shard_map/all_to_all | solution.py:281
  100.4 13.5 %collective-permute-start.2 = (bf16[64,3584]{1,0:T(8,128)(2,1)S(1)}, bf16[64,3584]{1,0:T(8,128)(2,1)S(1)}, u32[]{:S(2)}, u32[]{:S(2)}) collective-permute-start(bf16[64,3584]{1,0:T(8,128)(2,1)S(1)} %shard_map.74), channel_id=1, source_target_pairs={{0,32},{32,0},{1,33},{33,1},{2,34},{34,2},{3,35},{35,3},{4,36},{36... | collective-permute-start | bytes 1376264 | tf_op jit(solution)/shard_map/ppermute | solution.py:288
  110.5 20.9 %all-to-all-start.3 = ((bf16[8,144,128]{2,1,0:T(8,128)(2,1)}), bf16[8,144,128]{2,1,0:T(8,128)(2,1)S(1)}, u32[]{:S(2)}, u32[]{:S(2)}) async-start(bf16[8,144,128]{2,1,0:T(8,128)(2,1)} %bitcast.13), calls=%async_computation.3 | async-start | bytes 589824 | tf_op jit(solution)/shard_map/all_to_all | solution.py:281
  114.6 10.6 %collective-permute-start.3 = (bf16[128,896]{1,0:T(8,128)(2,1)S(1)}, bf16[128,896]{1,0:T(8,128)(2,1)S(1)}, u32[]{:S(2)}, u32[]{:S(2)}) collective-permute-start(bf16[128,896]{1,0:T(8,128)(2,1)S(1)} %get-tuple-element.25), channel_id=1, source_target_pairs={{0,1},{1,0},{4,5},{5,4},{2,3},{3,2},{6,7},{7,6},{8,9},{9,8},{12,13... | collective-permute-start | bytes 688136 | tf_op jit(solution)/shard_map/ppermute | solution.py:292
  117.9 8.4 %collective-permute-start.4 = (bf16[128,896]{1,0:T(8,128)(2,1)S(1)}, bf16[128,896]{1,0:T(8,128)(2,1)S(1)}, u32[]{:S(2)}, u32[]{:S(2)}) collective-permute-start(bf16[128,896]{1,0:T(8,128)(2,1)S(1)} %get-tuple-element.26), channel_id=1, source_target_pairs={{0,4},{1,5},{4,0},{5,1},{2,6},{3,7},{6,2},{7,3},{8,12},{9,13},{12,... | collective-permute-start | bytes 688136 | tf_op jit(solution)/shard_map/ppermute | solution.py:292
  121.0 10.4 %collective-permute-start.5 = (bf16[128,896]{1,0:T(8,128)(2,1)S(1)}, bf16[128,896]{1,0:T(8,128)(2,1)S(1)}, u32[]{:S(2)}, u32[]{:S(2)}) collective-permute-start(bf16[128,896]{1,0:T(8,128)(2,1)S(1)} %get-tuple-element.27), channel_id=1, source_target_pairs={{0,5},{1,4},{4,1},{5,0},{2,7},{3,6},{6,3},{7,2},{8,13},{9,12},{12,... | collective-permute-start | bytes 688136 | tf_op jit(solution)/shard_map/ppermute | solution.py:292

commit v5 on v3

--- a/solution.py
+++ b/solution.py
@@ -16,6 +16,9 @@
 COLUMN = ("z", "c")
 PLANE = ("y", "xh", "xl")
 ROW = ("c", "xh", "xl")
+
+FIRST_PLANE_IN, FIRST_PLANE_OUT = 10, 8
+FIRST_COLUMN_IN, FIRST_COLUMN_OUT = 16, 16
 
 LANES = 128
 SLOTS = 9
@@ -50,6 +53,10 @@
     return quotient, value - by * quotient
 
 
+def rows_at(start, size):
+    return pl.ds(pl.multiple_of(start, size), size)
+
+
 def dot(a, b):
     return jnp.dot(a, b, preferred_element_type=F32)
 
@@ -58,19 +65,18 @@
     return lax.dot_general(a, b, (((1,), (1,)), ((), ())), preferred_element_type=F32)
 
 
-def call(body, outs, ins, scratch=(), smem=(), smem_out=(), far=False, flops=10**8, limit=24 * 2**20):
+def call(body, outs, ins, scratch=(), smem=(), smem_out=(), far=(), flops=10**8, limit=24 * 2**20):
     def spec(in_smem):
         return pl.BlockSpec(memory_space=pltpu.SMEM if in_smem else pltpu.VMEM)
 
     far_spec = pl.BlockSpec(memory_space=pltpu.HBM)
 
-    if far:
-        ins = [pltpu.with_memory_space_constraint(x, pltpu.HBM) for x in ins]
+    ins = [pltpu.with_memory_space_constraint(x, pltpu.HBM) if i in far else x for i, x in enumerate(ins)]
     several = isinstance(outs, tuple)
     return pl.pallas_call(
         body,
         out_shape=outs,
-        in_specs=[far_spec if far else spec(i in smem) for i in range(len(ins))],
+        in_specs=[far_spec if i in far else spec(i in smem) for i in range(len(ins))],
         out_specs=tuple(spec(i in smem_out) for i in range(len(outs))) if several else spec(False),
         scratch_shapes=list(scratch),
         compiler_params=pltpu.CompilerParams(vmem_limit_bytes=limit),
@@ -109,7 +115,7 @@
     for z in range(NZ):
         gate = jnp.zeros(tile, F32)
         for node, pair in zip(nodes, pairs):
-            gate = jnp.where(node == z, pair, gate)
+            gate = jnp.where(node == (z + FIRST_PLANE_IN) % NZ, pair, gate)
         live = gate > 0
         rows = [jnp.where(live, block, 0.0) for block in blocks]
         for b in (HALF // 8, (TOK + HALF) // 8):
@@ -156,8 +162,10 @@
         out[y * NX * BLOCK_ROWS : (y + 1) * NX * BLOCK_ROWS, :] = packed
 
 
-def up_body(place_ids, rows, w_here, w_there, out, gate_out, balance_out, x):
+def up_body(place_ids, far_w, rows, w_core, w_row, w_both, out, gate_out, balance_out, x, w_own, done):
     core, xh = place_ids[0], place_ids[1]
+    own = pltpu.make_async_copy(far_w.at[rows_at((2 * core + xh) * WIDTH, WIDTH)], w_own, done.at[0])
+    own.start()
     n = 2 * NX * BLOCK_ROWS
     column, row = divided(iota((1, n), 1), BLOCK_ROWS)
     k, r = divided(row, SLOTS)
@@ -182,16 +190,21 @@
     balance_out[0] = (count * scale) * (total * scale)
     features = jnp.concatenate([x[k].astype(BF16) for k in range(EIGHTH)], axis=1)
     left = left_half((ROWS, LANES))
-    for j in range(4):
-        w = (w_here, w_there)[j // 2]
-        both = dot(features, w[WIDTH * (j % 2) : WIDTH * (j % 2 + 1), :])
+    for w, other_core, other_row in (
+        (w_core, True, False),
+        (w_row, False, True),
+        (w_both, True, True),
+        (w_own, False, False),
+    ):
+        if w is w_own:
+            own.wait()
+        both = dot(features, w[...])
         g, u = both[:, :LANES], both[:, LANES:]
-        expert = core if j % 2 == 0 else 1 - core
-        part = xh if j < 2 else 1 - xh
+        expert = 1 - core if other_core else core
+        part = 1 - xh if other_row else xh
         at = ROWS * 2 * (expert * NXH + part)
-        out[pl.ds(pl.multiple_of(at, ROWS), ROWS), :] = jnp.where(left, g, swap_halves(u)).astype(BF16)
-        at = at + ROWS
-        out[pl.ds(pl.multiple_of(at, ROWS), ROWS), :] = jnp.where(left, swap_halves(g), u).astype(BF16)
+        out[rows_at(at, ROWS), :] = jnp.where(left, g, swap_halves(u)).astype(BF16)
+        out[rows_at(at + ROWS, ROWS), :] = jnp.where(left, swap_halves(g), u).astype(BF16)
 
 
 def hidden_body(parts, gate, out):
@@ -246,7 +259,8 @@
     slot = slot_of(gate_rows[...])
     a = lax.broadcasted_iota(jnp.int32, (TOK * TOK, TOK), 0)
     b = lax.broadcasted_iota(jnp.int32, (TOK * TOK, TOK), 1)
-    spread = dot(one_hot(lax.shift_right_logical(a, 5), b), slot.astype(BF16))
+    token = lax.shift_right_logical(a, 5) + NC * (FIRST_PLANE_OUT - FIRST_PLANE_IN)
+    spread = dot(one_hot(lax.bitwise_and(token, TOK - 1), b), slot.astype(BF16))
     chunk = lax.bitwise_and(lax.broadcasted_iota(jnp.int32, (TOK * TOK, LANES), 0), TOK - 1)
     key = (chunk.astype(F32) * 16.0 + spread)[:, 0:1]
     out[...] = dot(one_hot(key, chunk_and_slot(iota((1, n), 1))), total.astype(BF16)).astype(BF16)
@@ -265,69 +279,69 @@
             out[:, at : at + LANES] = total[row : row + 1, :].astype(BF16)
 
 
-def exchange(x, axes, members):
+def exchange(x, axes, members, turn=0):
     rows = x.shape[0] // members
+    order = [[(i + turn) % members for i in range(members)]] if turn else None
     y = lax.all_to_all(
-        x.reshape(members, rows, x.shape[1]), axes, split_axis=0, concat_axis=0, tiled=True
+        x.reshape(members, rows, x.shape[1]),
+        axes,
+        split_axis=0,
+        concat_axis=0,
+        axis_index_groups=order,
+        tiled=True,
     )
     return y.reshape(x.shape)
 
 
-def swapped(x, axis):
-    return lax.ppermute(x, axis, [(0, 1), (1, 0)])
-
-
-def x_swapped(x, mask):
-    return lax.ppermute(x, ("xh", "xl"), [(i, i ^ mask) for i in range(NX)])
-
-
-def rows_at(start, size):
-    return pl.ds(pl.multiple_of(start, size), size)
-
-
-def core_body(place_ids, w_in, w_out, up, down):
-    other = 1 - place_ids[0]
-    up[...] = w_in[rows_at(other * 2 * WIDTH, 2 * WIDTH), :]
-    down[...] = w_out[:, rows_at(other * NX * WIDTH, NX * WIDTH)]
-
-
-def up_row_body(place_ids, w_in, up, here, there):
+def up_parts_body(place_ids, far_w, core_out, row_out, both_out, done):
     core, xh = place_ids[0], place_ids[1]
-    for out, side in ((here, xh), (there, 1 - xh)):
-        out[0:WIDTH, :] = w_in[rows_at((2 * core + side) * WIDTH, WIDTH), :]
-        out[WIDTH : 2 * WIDTH, :] = up[rows_at(side * WIDTH, WIDTH), :]
-
-
-def down_row_body(place_ids, w_out, down, *outs):
+    to = (2 * (1 - core) + xh, 2 * core + 1 - xh, 2 * (1 - core) + 1 - xh)
+    copies = [
+        pltpu.make_async_copy(far_w.at[rows_at(eighth * WIDTH, WIDTH)], out, done.at[i])
+        for i, (eighth, out) in enumerate(zip(to, (core_out, row_out, both_out)))
+    ]
+    for copy in copies:
+        copy.start()
+    for copy in copies:
+        copy.wait()
+
+
+def down_row_body(place_ids, w_out, other, *outs):
     core, x = place_ids[0], place_ids[2]
     for d, out in enumerate(outs):
-        to = lax.bitwise_xor(x, jnp.int32(d))
-        out[0:BLOCK, :] = w_out[:, rows_at((core * NX + to) * WIDTH, WIDTH)]
-        out[BLOCK : 2 * BLOCK, :] = down[:, rows_at(to * WIDTH, WIDTH)]
-
-
-def spread_weights(place_ids, w_in, w_out):
-    shape = jax.ShapeDtypeStruct
-    up_shape, down_shape = shape((2 * WIDTH, 2 * LANES), BF16), shape((2 * BLOCK, WIDTH), BF16)
-    up, down = call(
-        core_body,
-        (up_shape, shape((BLOCK, NX * WIDTH), BF16)),
-        (place_ids, w_in, w_out),
+        to = (core * NX + lax.bitwise_xor(x, jnp.int32(d))) * WIDTH
+        out[0:BLOCK, :] = w_out[:, rows_at(to, WIDTH)]
+        out[BLOCK : 2 * BLOCK, :] = other[:, rows_at(to, WIDTH)]
+
+
+def up_weights(place_ids, w_in):
+    parts = call(
+        up_parts_body,
+        (jax.ShapeDtypeStruct((WIDTH, 2 * LANES), BF16),) * 3,
+        (place_ids, w_in),
+        scratch=(pltpu.SemaphoreType.DMA((3,)),),
         smem=(0,),
-    )
-    up = swapped(up, "c")
-    down = swapped(down, "c")
-    up_here, up_there = call(
-        up_row_body, (up_shape,) * 2, (place_ids, w_in, up), smem=(0,)
-    )
-    up_there = swapped(up_there, "xh")
+        far=(1,),
+    )
+    swaps = ("c", [(0, 1), (1, 0)]), ("xh", [(0, 1), (1, 0)]), (("c", "xh"), [(i, 3 - i) for i in range(4)])
+    out = []
+    for i in (1, 2, 0):
+        out.append(lax.ppermute(parts[i], *swaps[i]))
+    return out[2], out[0], out[1]
+
+
+def down_weights(place_ids, w_out):
+    other = lax.ppermute(w_out, "c", [(0, 1), (1, 0)])
     parts = call(
-        down_row_body, (down_shape,) * NX, (place_ids, w_out, down), smem=(0,)
+        down_row_body,
+        (jax.ShapeDtypeStruct((2 * BLOCK, WIDTH), BF16),) * NX,
+        (place_ids, w_out, other),
+        smem=(0,),
     )
     parts = list(parts)
     for d in range(1, NX):
-        parts[d] = x_swapped(parts[d], d)
-    return (up_here, up_there), parts
+        parts[d] = lax.ppermute(parts[d], ("xh", "xl"), [(i, i ^ d) for i in range(NX)])
+    return parts
 
 
 def layer(tokens, node_ids, gates, w_in, w_out):
@@ -346,26 +360,33 @@
             pltpu.VMEM((2 * TOK, LANES), F32),
             pltpu.SemaphoreType.DMA((3,)),
         ),
-        far=True,
+        far=(0, 1, 2),
     )
     sent, w_in, w_out = lax.optimization_barrier((sent, w_in, w_out))
-    arrived = exchange(sent, COLUMN, NZ * NC)
-    w_up, w_down = spread_weights(place_ids, w_in.reshape(4 * WIDTH, 2 * LANES), w_out[0])
+    arrived = exchange(sent, COLUMN, NZ * NC, NC * FIRST_PLANE_IN)
+    w_in = w_in.reshape(4 * WIDTH, 2 * LANES)
+    w_up = up_weights(place_ids, w_in)
+    w_down = down_weights(place_ids, w_out[0])
 
     packed, gate_rows = call(
         pack_body,
         (shape((NY * NX * BLOCK_ROWS, LANES), BF16), shape((TOK, LANES), F32)),
         (arrived,),
     )
-    rows = exchange(packed, PLANE, NY * NX)
+    rows = exchange(packed, PLANE, NY * NX, FIRST_COLUMN_IN)
 
     partial_sums, gate, balance = call(
         up_body,
         (shape((8 * ROWS, LANES), BF16), shape((ROWS, LANES), F32), shape((1,), F32)),
-        (place_ids, rows, *w_up),
-        scratch=(pltpu.VMEM((EIGHTH + 1, ROWS, LANES), F32),),
+        (place_ids, w_in, rows, *w_up),
+        scratch=(
+            pltpu.VMEM((EIGHTH + 1, ROWS, LANES), F32),
+            pltpu.VMEM((WIDTH, 2 * LANES), BF16),
+            pltpu.SemaphoreType.DMA((1,)),
+        ),
         smem=(0,),
         smem_out=(2,),
+        far=(1,),
         flops=10**9,
     )
     summands = exchange(partial_sums, ROW, 8)
@@ -381,14 +402,14 @@
         smem=(0,),
         flops=10**9,
     )
-    returned = exchange(down, PLANE, NY * NX)
+    returned = exchange(down, PLANE, NY * NX, FIRST_COLUMN_OUT)
 
     unpacked = call(
         unpack_body,
         shape((TOK * TOK, LANES), BF16),
         (returned, gate_rows),
     )
-    back = exchange(unpacked, COLUMN, NZ * NC)
+    back = exchange(unpacked, COLUMN, NZ * NC, NC * FIRST_PLANE_OUT)
 
     mixed = call(
         finish_body,

time: 186 us -> 181 us (0.973)
  blocking collectives: 48.9 us -> 100 us
  waiting for transfers between devices: 59.6 us -> 30.6 us
  starting transfers between devices: 57.2 us -> 34.7 us
  local copies, waits for them, and re-layouts: 6.41 us -> 1.8 us
    all_to_all x2 -> x4, blocking collectives: 48.9 us -> 100 us  [exchange(): lax.all_to_all(x.reshape(members, rows, x.shape[1]), axes, split_axis=0,...]
    all_to_all x4 -> x2, starting transfers between devices: 38.8 us -> 13.8 us  [exchange(): lax.all_to_all(x.reshape(members, rows, x.shape[1]), axes, split_axis=0,...]
    all_to_all x4 -> x2, waiting for transfers between devices: 23 us -> 0.01 us  [exchange(): lax.all_to_all(x.reshape(members, rows, x.shape[1]), axes, split_axis=0,...]
    ppermute x6 -> x7, waiting for transfers between devices: 36.5 us -> 30.6 us  [the longest x3 18.6 us: up_weights(): out.append(lax.ppermute(parts[i], *swaps[i]))]
    unnamed x18 -> x6, local copies, waits for them, and re-layouts: 6.41 us -> 1.8 us
    ppermute x6 -> x7, starting transfers between devices: 18.3 us -> 20.9 us  [the longest x3 9.58 us: down_weights(): lax.ppermute(parts[d], ('xh', 'xl'), [(i, i ^ d) for i in range(NX)])]
    pallas_call x10 -> x9, Pallas kernels: 12.3 us -> 12.4 us  [call(): pl.pallas_call(body, out_shape=outs, in_specs=[far_spec if i in far else...]
  transfers between devices with their start and end apart: 10 -> 9, of which waited for: 6 -> 5; matrix products, arithmetic and copies ran while one was open for 0% -> 0% of each run, Pallas kernels for 2% -> 4%
where the time goes in v5:
time: 181 us; the launch traced here: 180 us
  blocking collectives  100 us (55%)
  starting transfers between devices  34.7 us (19%)
  waiting for transfers between devices  30.6 us (17%)
  Pallas kernels  12.4 us (7%)
    all_to_all x4, blocking collectives, exchange(): lax.all_to_all(x.reshape(members, rows, x.shape[1]), axes, split_axis=0,...  100 us
    ppermute x3, waiting for transfers between devices, up_weights(): out.append(lax.ppermute(parts[i], *swaps[i]))  18.6 us
    all_to_all x2, starting transfers between devices, exchange(): lax.all_to_all(x.reshape(members, rows, x.shape[1]), axes, split_axis=0,...  13.8 us
    pallas_call x9, Pallas kernels, call(): pl.pallas_call(body, out_shape=outs, in_specs=[far_spec if i in far else...  12.4 us
    ppermute x3, waiting for transfers between devices, down_weights(): lax.ppermute(parts[d], ('xh', 'xl'), [(i, i ^ d) for i in range(NX)])  11.9 us
    ppermute x3, starting transfers between devices, down_weights(): lax.ppermute(parts[d], ('xh', 'xl'), [(i, i ^ d) for i in range(NX)])  9.58 us
    ppermute x3, starting transfers between devices, up_weights(): out.append(lax.ppermute(parts[i], *swaps[i]))  9.37 us
  transfers between devices with their start and end apart: 9, of which 5 were waited for; matrix products, arithmetic and copies ran while one was open for 0% of the time, Pallas kernels for 4%

profile of v5, /device:TPU:1, one launch (start us, length us, event | category | flops | bytes accessed | tf_op | source)
XLA Modules:
  0.0 180.4 jit_solution(12286415548479116921)
XLA Ops:
  0.6 0.9 shard_map.68
  1.6 0.0 copy-start
  1.6 39.2 %all_to_all.30 = bf16[32,32,128]{2,1,0:T(8,128)(2,1)S(1)} all-to-all(bf16[32,32,128]{2,1,0:T(8,128)(2,1)S(1)} %bitcast.32), channel_id=1, replica_groups={{640,672,704,736,768,800,832,864,896,928,960,992,0,32,64,96,128,160,192..., dimensions={0} | all-to-all | bytes 524288 | tf_op jit(solution)/shard_map/all_to_all | solution.py:285
  40.8 1.6 shard_map.69
  42.4 10.1 %all-to-all-start.1 = ((bf16[32,64,128]{2,1,0:T(8,128)(2,1)}), bf16[32,64,128]{2,1,0:T(8,128)(2,1)S(1)}, u32[]{:S(2)}, u32[]{:S(2)}) async-start(bf16[32,64,128]{2,1,0:T(8,128)(2,1)} %bitcast.9), calls=%async_computation.1 | async-start | bytes 1048576 | tf_op jit(solution)/shard_map/all_to_all | solution.py:285
  52.5 0.1 pad_add_fusion.place_ids
  52.6 1.9 %shard_map.70 = (bf16[896,256]{1,0:T(8,128)(2,1)S(1)}, bf16[896,256]{1,0:T(8,128)(2,1)S(1)}, bf16[896,256]{1,0:T(8,128)(2,1)S(1)}) custom-call(s32[3]{0:T(128)S(1)} %pad_add_fusion.place_ids, bf16[3584,256]{1,0:T(8,128)(2,1)} %bitcast.33), custom_call_target="tpu_custom_call" | custom-call | flops 100000000 | bytes 1000000 | tf_op jit(solution)/shard_map/pallas_call | solution.py:76
  54.5 2.2 %collective-permute-start = (bf16[896,256]{1,0:T(8,128)(2,1)S(1)}, bf16[896,256]{1,0:T(8,128)(2,1)S(1)}, u32[]{:S(2)}, u32[]{:S(2)}) collective-permute-start(bf16[896,256]{1,0:T(8,128)(2,1)S(1)} %get-tuple-element.20), channel_id=1, source_target_pairs={{0,32},{32,0},{1,33},{33,1},{2,34},{34,2},{3,35},{35,3},{4,36},{36... | collective-permute-start | bytes 1376264 | tf_op jit(solution)/shard_map/ppermute | solution.py:329
  56.7 4.6 %collective-permute-start.1 = (bf16[896,256]{1,0:T(8,128)(2,1)S(1)}, bf16[896,256]{1,0:T(8,128)(2,1)S(1)}, u32[]{:S(2)}, u32[]{:S(2)}) collective-permute-start(bf16[896,256]{1,0:T(8,128)(2,1)S(1)} %get-tuple-element.21), channel_id=1, source_target_pairs={{0,2},{2,0},{1,3},{3,1},{4,6},{6,4},{5,7},{7,5},{8,10},{10,8},{9,1... | collective-permute-start | bytes 1376264 | tf_op jit(solution)/shard_map/ppermute | solution.py:329
  61.3 2.5 %collective-permute-start.2 = (bf16[896,256]{1,0:T(8,128)(2,1)S(1)}, bf16[896,256]{1,0:T(8,128)(2,1)S(1)}, u32[]{:S(2)}, u32[]{:S(2)}) collective-permute-start(bf16[896,256]{1,0:T(8,128)(2,1)S(1)} %get-tuple-element.22), channel_id=1, source_target_pairs={{0,34},{2,32},{32,2},{34,0},{1,35},{3,33},{33,3},{35,1},{4,38},{6,... | collective-permute-start | bytes 1376264 | tf_op jit(solution)/shard_map/ppermute | solution.py:329
  63.9 0.0 copy-done
  63.9 2.0 %collective-permute-start.3 = (bf16[64,7168]{1,0:T(8,128)(2,1)S(1)}, bf16[64,7168]{1,0:T(8,128)(2,1)S(1)}, u32[]{:S(2)}, u32[]{:S(2)}) collective-permute-start(bf16[64,7168]{1,0:T(8,128)(2,1)S(1)} %bitcast.25), channel_id=1, source_target_pairs={{0,32},{32,0},{1,33},{33,1},{2,34},{34,2},{3,35},{35,3},{4,36},{36... | collective-permute-start | bytes 2752520 | tf_op jit(solution)/shard_map/ppermute | solution.py:334
  65.8 0.0 collective-permute-done.w_core
  65.8 8.6 %collective-permute-done.1.w_row = bf16[896,256]{1,0:T(8,128)(2,1)S(1)} collective-permute-done((bf16[896,256]{1,0:T(8,128)(2,1)S(1)}, bf16[896,256]{1,0:T(8,128)(2,1)S(1)}, u32[]{:S(2)}, u32[]{:S(2)}) %collective-permute-start.1) | collective-permute-done | bytes 458784 | tf_op jit(solution)/shard_map/ppermute | solution.py:329
  74.4 10.0 %collective-permute-done.2.w_both = bf16[896,256]{1,0:T(8,128)(2,1)S(1)} collective-permute-done((bf16[896,256]{1,0:T(8,128)(2,1)S(1)}, bf16[896,256]{1,0:T(8,128)(2,1)S(1)}, u32[]{:S(2)}, u32[]{:S(2)}) %collective-permute-start.2) | collective-permute-done | bytes 458784 | tf_op jit(solution)/shard_map/ppermute | solution.py:329
  84.4 0.0 copy-start.1
  84.5 0.8 copy-done.1
  85.2 0.0 all-to-all-done.1
  85.2 0.0 copy-start.2
  85.2 1.0 copy-done.2
  86.2 3.3 %shard_map.71 = (bf16[2304,128]{1,0:T(8,128)(2,1)S(1)}, f32[288,128]{1,0:T(8,128)S(1)}, f32[1]{0:T(128)}) custom-call(s32[3]{0:T(128)S(1)} %pad_add_fusion.place_ids, bf16[3584,256]{1,0:T(8,128)(2,1)} %bitcast.34, bf16[2048,128]{1,0:T(8,128)(2,1)S(1)} %bitcast.23, bf16[896,256]{1,0:T(8,128)(2,1)S(1)} %collective-permute-done.w_core, ...), custom_call_target="tpu_custom_call" | custom-call | flops 1000000000 | bytes 1000000 | tf_op jit(solution)/shard_map/pallas_call | solution.py:76
  89.5 13.6 %all_to_all.31 = bf16[8,288,128]{2,1,0:T(8,128)(2,1)S(1)} all-to-all(bf16[8,288,128]{2,1,0:T(8,128)(2,1)S(1)} %bitcast.27), channel_id=1, replica_groups=mesh['z'=16,'c'=2,'y'=8,'xh'=2,'xl'=2] {'c','xh','xl'}, dimensions={0} | all-to-all | bytes 1179648 | tf_op jit(solution)/shard_map/all_to_all | solution.py:285
  103.1 0.9 shard_map.72
  104.0 3.7 %all-to-all-start.3 = ((bf16[8,144,128]{2,1,0:T(8,128)(2,1)}), bf16[8,144,128]{2,1,0:T(8,128)(2,1)S(1)}, u32[]{:S(2)}, u32[]{:S(2)}) async-start(bf16[8,144,128]{2,1,0:T(8,128)(2,1)} %bitcast.13), calls=%async_computation.3 | async-start | bytes 589824 | tf_op jit(solution)/shard_map/all_to_all | solution.py:285
  107.7 0.0 collective-permute-done.3.other
  107.7 0.6 shard_map.73
  108.4 3.3 %collective-permute-start.4 = (bf16[128,896]{1,0:T(8,128)(2,1)S(1)}, bf16[128,896]{1,0:T(8,128)(2,1)S(1)}, u32[]{:S(2)}, u32[]{:S(2)}) collective-permute-start(bf16[128,896]{1,0:T(8,128)(2,1)S(1)} %get-tuple-element.27), channel_id=1, source_target_pairs={{0,1},{1,0},{2,3},{3,2},{4,5},{5,4},{6,7},{7,6},{8,9},{9,8},{10,11... | collective-permute-start | bytes 688136 | tf_op jit(solution)/shard_map/ppermute | solution.py:343
  111.6 4.3 %collective-permute-start.5 = (bf16[128,896]{1,0:T(8,128)(2,1)S(1)}, bf16[128,896]{1,0:T(8,128)(2,1)S(1)}, u32[]{:S(2)}, u32[]{:S(2)}) collective-permute-start(bf16[128,896]{1,0:T(8,128)(2,1)S(1)} %get-tuple-element.28), channel_id=1, source_target_pairs={{0,2},{1,3},{2,0},{3,1},{4,6},{5,7},{6,4},{7,5},{8,10},{9,11},{10,... | collective-permute-start | bytes 688136 | tf_op jit(solution)/shard_map/ppermute | solution.py:343
  116.0 2.0 %collective-permute-start.6 = (bf16[128,896]{1,0:T(8,128)(2,1)S(1)}, bf16[128,896]{1,0:T(8,128)(2,1)S(1)}, u32[]{:S(2)}, u32[]{:S(2)}) collective-permute-start(bf16[128,896]{1,0:T(8,128)(2,1)S(1)} %get-tuple-element.29), channel_id=1, source_target_pairs={{0,3},{1,2},{2,1},{3,0},{4,7},{5,6},{6,5},{7,4},{8,11},{9,10},{10,... | collective-permute-start | bytes 688136 | tf_op jit(solution)/shard_map/ppermute | solution.py:343
  118.0 0.1 collective-permute-done.4.w1
  118.1 6.2 %collective-permute-done.5.w2 = bf16[128,896]{1,0:T(8,128)(2,1)S(1)} collective-permute-done((bf16[128,896]{1,0:T(8,128)(2,1)S(1)}, bf16[128,896]{1,0:T(8,128)(2,1)S(1)}, u32[]{:S(2)}, u32[]{:S(2)}) %collective-permute-start.5) | collective-permute-done | bytes 229408 | tf_op jit(solution)/shard_map/ppermute | solution.py:343
  124.3 5.6 %collective-permute-done.6.w3 = bf16[128,896]{1,0:T(8,128)(2,1)S(1)} collective-permute-done((bf16[128,896]{1,0:T(8,128)(2,1)S(1)}, bf16[128,896]{1,0:T(8,128)(2,1)S(1)}, u32[]{:S(2)}, u32[]{:S(2)}) %collective-permute-start.6) | collective-permute-done | bytes 229408 | tf_op jit(solution)/shard_map/ppermute | solution.py:343
  129.9 0.0 all-to-all-done.3
  129.9 1.9 %shard_map.74 = bf16[2048,128]{1,0:T(8,128)(2,1)S(1)} custom-call(s32[3]{0:T(128)S(1)} %pad_add_fusion.place_ids, bf16[1152,128]{1,0:T(8,128)(2,1)S(1)} %bitcast.29, bf16[128,896]{1,0:T(8,128)(2,1)S(1)} %get-tuple-element.26.w0, bf16[128,896]{1,0:T(8,128)(2,1)S(1)} %collective-permute-done.4.w1, bf16[128,896]{1,0:T(8,128)(2,1)S(1)} %collective-permute-done.5.w2, ...), custom_call_target="tpu_custom_call" | custom-call | flops 1000000000 | bytes 1000000 | tf_op jit(solution)/shard_map/pallas_call | solution.py:76
  131.9 21.0 %all_to_all.32 = bf16[32,64,128]{2,1,0:T(8,128)(2,1)S(1)} all-to-all(bf16[32,64,128]{2,1,0:T(8,128)(2,1)S(1)} %bitcast.28), channel_id=1, replica_groups={{16,17,18,19,20,21,22,23,24,25,26,27,28,29,30,31,0,1,2,3,4,5,6,7,8,9,10..., dimensions={0} | all-to-all | bytes 1048576 | tf_op jit(solution)/shard_map/all_to_all | solution.py:285
  152.8 0.6 shard_map.75
  153.5 26.2 %all_to_all.33 = bf16[32,32,128]{2,1,0:T(8,128)(2,1)S(1)} all-to-all(bf16[32,32,128]{2,1,0:T(8,128)(2,1)S(1)} %bitcast.24), channel_id=1, replica_groups={{512,544,576,608,640,672,704,736,768,800,832,864,896,928,960,992,0,32,6..., dimensions={0} | all-to-all | bytes 524288 | tf_op jit(solution)/shard_map/all_to_all | solution.py:285
  179.7 0.7 shard_map.76
Async XLA Ops:
  1.6 62.3 %copy-start = (bf16[1,64,7168]{2,1,0:T(8,128)(2,1)S(1)}, bf16[1,64,7168]{2,1,0:T(8,128)(2,1)}, u32[]{:S(2)}) copy-start(bf16[1,64,7168]{2,1,0:T(8,128)(2,1)} %param.9) | copy-start | bytes 2752516
  42.4 42.8 %all-to-all-start.1 = ((bf16[32,64,128]{2,1,0:T(8,128)(2,1)}), bf16[32,64,128]{2,1,0:T(8,128)(2,1)S(1)}, u32[]{:S(2)}, u32[]{:S(2)}) async-start(bf16[32,64,128]{2,1,0:T(8,128)(2,1)} %bitcast.9), calls=%async_computation.1 | async-start | bytes 1048576 | tf_op jit(solution)/shard_map/all_to_all | solution.py:285
  54.5 11.4 %collective-permute-start = (bf16[896,256]{1,0:T(8,128)(2,1)S(1)}, bf16[896,256]{1,0:T(8,128)(2,1)S(1)}, u32[]{:S(2)}, u32[]{:S(2)}) collective-permute-start(bf16[896,256]{1,0:T(8,128)(2,1)S(1)} %get-tuple-element.20), channel_id=1, source_target_pairs={{0,32},{32,0},{1,33},{33,1},{2,34},{34,2},{3,35},{35,3},{4,36},{36... | collective-permute-start | bytes 1376264 | tf_op jit(solution)/shard_map/ppermute | solution.py:329
  56.7 17.7 %collective-permute-start.1 = (bf16[896,256]{1,0:T(8,128)(2,1)S(1)}, bf16[896,256]{1,0:T(8,128)(2,1)S(1)}, u32[]{:S(2)}, u32[]{:S(2)}) collective-permute-start(bf16[896,256]{1,0:T(8,128)(2,1)S(1)} %get-tuple-element.21), channel_id=1, source_target_pairs={{0,2},{2,0},{1,3},{3,1},{4,6},{6,4},{5,7},{7,5},{8,10},{10,8},{9,1... | collective-permute-start | bytes 1376264 | tf_op jit(solution)/shard_map/ppermute | solution.py:329
  61.3 23.1 %collective-permute-start.2 = (bf16[896,256]{1,0:T(8,128)(2,1)S(1)}, bf16[896,256]{1,0:T(8,128)(2,1)S(1)}, u32[]{:S(2)}, u32[]{:S(2)}) collective-permute-start(bf16[896,256]{1,0:T(8,128)(2,1)S(1)} %get-tuple-element.22), channel_id=1, source_target_pairs={{0,34},{2,32},{32,2},{34,0},{1,35},{3,33},{33,3},{35,1},{4,38},{6,... | collective-permute-start | bytes 1376264 | tf_op jit(solution)/shard_map/ppermute | solution.py:329
  63.9 43.9 %collective-permute-start.3 = (bf16[64,7168]{1,0:T(8,128)(2,1)S(1)}, bf16[64,7168]{1,0:T(8,128)(2,1)S(1)}, u32[]{:S(2)}, u32[]{:S(2)}) collective-permute-start(bf16[64,7168]{1,0:T(8,128)(2,1)S(1)} %bitcast.25), channel_id=1, source_target_pairs={{0,32},{32,0},{1,33},{33,1},{2,34},{34,2},{3,35},{35,3},{4,36},{36... | collective-permute-start | bytes 2752520 | tf_op jit(solution)/shard_map/ppermute | solution.py:334
  84.4 0.8 copy-start.1
  85.2 1.0 copy-start.2
  104.0 25.9 %all-to-all-start.3 = ((bf16[8,144,128]{2,1,0:T(8,128)(2,1)}), bf16[8,144,128]{2,1,0:T(8,128)(2,1)S(1)}, u32[]{:S(2)}, u32[]{:S(2)}) async-start(bf16[8,144,128]{2,1,0:T(8,128)(2,1)} %bitcast.13), calls=%async_computation.3 | async-start | bytes 589824 | tf_op jit(solution)/shard_map/all_to_all | solution.py:285
  108.4 9.7 %collective-permute-start.4 = (bf16[128,896]{1,0:T(8,128)(2,1)S(1)}, bf16[128,896]{1,0:T(8,128)(2,1)S(1)}, u32[]{:S(2)}, u32[]{:S(2)}) collective-permute-start(bf16[128,896]{1,0:T(8,128)(2,1)S(1)} %get-tuple-element.27), channel_id=1, source_target_pairs={{0,1},{1,0},{2,3},{3,2},{4,5},{5,4},{6,7},{7,6},{8,9},{9,8},{10,11... | collective-permute-start | bytes 688136 | tf_op jit(solution)/shard_map/ppermute | solution.py:343
  111.6 12.7 %collective-permute-start.5 = (bf16[128,896]{1,0:T(8,128)(2,1)S(1)}, bf16[128,896]{1,0:T(8,128)(2,1)S(1)}, u32[]{:S(2)}, u32[]{:S(2)}) collective-permute-start(bf16[128,896]{1,0:T(8,128)(2,1)S(1)} %get-tuple-element.28), channel_id=1, source_target_pairs={{0,2},{1,3},{2,0},{3,1},{4,6},{5,7},{6,4},{7,5},{8,10},{9,11},{10,... | collective-permute-start | bytes 688136 | tf_op jit(solution)/shard_map/ppermute | solution.py:343
  116.0 14.0 %collective-permute-start.6 = (bf16[128,896]{1,0:T(8,128)(2,1)S(1)}, bf16[128,896]{1,0:T(8,128)(2,1)S(1)}, u32[]{:S(2)}, u32[]{:S(2)}) collective-permute-start(bf16[128,896]{1,0:T(8,128)(2,1)S(1)} %get-tuple-element.29), channel_id=1, source_target_pairs={{0,3},{1,2},{2,1},{3,0},{4,7},{5,6},{6,5},{7,4},{8,11},{9,10},{10,... | collective-permute-start | bytes 688136 | tf_op jit(solution)/shard_map/ppermute | solution.py:343

commit v6 on v5

--- a/solution.py
+++ b/solution.py
@@ -17,14 +17,15 @@
 PLANE = ("y", "xh", "xl")
 ROW = ("c", "xh", "xl")
 
-FIRST_PLANE_IN, FIRST_PLANE_OUT = 10, 8
-FIRST_COLUMN_IN, FIRST_COLUMN_OUT = 16, 16
+FIRST_PLANE_IN, FIRST_PLANE_OUT = 13, 8
+FIRST_COLUMN = 18
 
 LANES = 128
 SLOTS = 9
 EIGHTH = 7
 HALF = NX * EIGHTH
 TOK = 32
+TOKEN_ROWS = 30
 BLOCK_ROWS = 64
 ROWS = NY * NX * SLOTS
 PAIR = ROWS // 4
@@ -93,17 +94,20 @@
         copy.start()
     for copy in copies:
         copy.wait()
+    pair_rows = NC * TOKEN_ROWS
+    base[...] = jnp.zeros(base.shape, F32)
     for c in range(NC):
         for xh in range(NXH):
             for xl in range(NXL):
                 for k in range(EIGHTH):
-                    row = c * TOK + (xh * NXL + xl) * EIGHTH + k
+                    row = c * TOKEN_ROWS + (xh * NXL + xl) * EIGHTH + k
                     i = xl * HALF + (c * NXH + xh) * EIGHTH + k
-                    base[row : row + 1, :] = token[:, i * LANES : (i + 1) * LANES].astype(F32)
-        base[c * TOK + HALF : (c + 1) * TOK, :] = jnp.zeros((TOK - HALF, LANES), F32)
+                    piece = token[:, i * LANES : (i + 1) * LANES].astype(F32)
+                    base[row : row + 1, :] = piece
+                    base[pair_rows + row : pair_rows + row + 1, :] = piece
     tile = (8, LANES)
     left = left_half(tile)
-    gate_row = lax.broadcasted_iota(jnp.int32, tile, 0) == HALF % 8
+    sub = lax.broadcasted_iota(jnp.int32, tile, 0)
     every_gate = gates[...].astype(F32)
     nodes, pairs = [], []
     for m in range(4):
@@ -111,16 +115,27 @@
         first = jnp.broadcast_to(every_gate[:, 2 * m : 2 * m + 1], tile)
         second = jnp.broadcast_to(every_gate[:, 2 * m + 1 : 2 * m + 2], tile)
         pairs.append(jnp.where(left, first, second))
-    blocks = [base[8 * b : 8 * (b + 1), :] for b in range(2 * TOK // 8)]
-    for z in range(NZ):
+
+    def gate_of(place):
         gate = jnp.zeros(tile, F32)
         for node, pair in zip(nodes, pairs):
-            gate = jnp.where(node == (z + FIRST_PLANE_IN) % NZ, pair, gate)
-        live = gate > 0
-        rows = [jnp.where(live, block, 0.0) for block in blocks]
-        for b in (HALF // 8, (TOK + HALF) // 8):
-            rows[b] = jnp.where(gate_row, gate, rows[b])
-        out[2 * TOK * z : 2 * TOK * (z + 1), :] = jnp.concatenate(rows, axis=0).astype(BF16)
+            gate = jnp.where(node == (place + FIRST_PLANE_IN) % NZ, pair, gate)
+        return gate
+
+    blocks = [base[8 * b : 8 * (b + 1), :] for b in range(2 * pair_rows // 8)]
+    for z in range(0, NZ, 2):
+        both = gate_of(z), gate_of(z + 1)
+        rows = []
+        for b, block in enumerate(blocks):
+            split = min(max(pair_rows - 8 * b, 0), 8)
+            gate = both[1] if split == 0 else both[0] if split == 8 else jnp.where(sub < split, *both)
+            block = jnp.where(gate > 0, block, 0.0)
+            for half in range(2 * NC):
+                at = half * TOKEN_ROWS + HALF - 8 * b
+                if 0 <= at < 8:
+                    block = jnp.where(sub == at, gate, block)
+            rows.append(block)
+        out[pair_rows * z : pair_rows * (z + 2), :] = jnp.concatenate(rows, axis=0).astype(BF16)
 
 
 def slot_of(gate_rows):
@@ -133,21 +148,21 @@
 
 def chunk_and_slot(at):
     x, row = divided(at, BLOCK_ROWS)
+    x = jnp.where(x < NXL, x + NXL, x - NXL)
     k, r = divided(row, SLOTS)
     return jnp.where(k < EIGHTH, (x * EIGHTH + k) * 16.0 + r, -1.0)
 
 
 def pack_body(arrived, out, gate_out):
-    a = lax.broadcasted_iota(jnp.int32, (TOK, TOK * TOK), 0)
-    b = lax.broadcasted_iota(jnp.int32, (TOK, TOK * TOK), 1)
-    gate_rows = dot(one_hot(a * TOK + HALF, b), arrived[...])
+    n = TOK * TOKEN_ROWS
+    token, at = iota((TOK, n), 0), iota((1, n), 1)
+    token_of, chunk = divided(at, TOKEN_ROWS)
+    gate_rows = dot(one_hot(token * TOKEN_ROWS + HALF, at), arrived[...])
     gate_out[...] = gate_rows
     slot = slot_of(gate_rows)
     lane = lax.broadcasted_iota(jnp.int32, (8, LANES), 1)
     by_token = dot_t(one_hot(lane, 0), slot.astype(BF16))
-    token_of = lax.shift_right_logical(b, 5)
-    spread = dot(by_token.astype(BF16), one_hot(a, token_of))
-    chunk = lax.bitwise_and(b[0:1], TOK - 1).astype(F32)
+    spread = dot(by_token.astype(BF16), one_hot(token, token_of))
     col_key = chunk * 16.0 + spread[0:1]
     row_key = chunk_and_slot(iota((NX * BLOCK_ROWS, 1), 0))
     packed = dot(one_hot(row_key, col_key), arrived[...])
@@ -177,10 +192,12 @@
         ],
         axis=0,
     )
-    for g in range(4):
-        moved = dot(p, rows[n * g : n * (g + 1), :])
-        for k in range(EIGHTH + 1):
-            x[k, PAIR * g : PAIR * (g + 1), :] = moved[PAIR * k : PAIR * (k + 1), :]
+    for g in range(0, 4, 2):
+        moved = dot(p, jnp.concatenate([rows[n * (g + i) : n * (g + i + 1), :] for i in range(2)], axis=1))
+        for i in range(2):
+            at = PAIR * (g + i)
+            for k in range(EIGHTH + 1):
+                x[k, at : at + PAIR, :] = moved[PAIR * k : PAIR * (k + 1), LANES * i : LANES * (i + 1)]
     _, slot = divided(iota((ROWS, 1), 0), SLOTS)
     wanted = iota((ROWS, LANES), 1) == slot + 16.0 * core.astype(F32)
     gate = jnp.sum(jnp.where(wanted, x[EIGHTH], 0.0), axis=1, keepdims=True)
@@ -201,7 +218,7 @@
         both = dot(features, w[...])
         g, u = both[:, :LANES], both[:, LANES:]
         expert = 1 - core if other_core else core
-        part = 1 - xh if other_row else xh
+        part = xh if other_row else 1 - xh
         at = ROWS * 2 * (expert * NXH + part)
         out[rows_at(at, ROWS), :] = jnp.where(left, g, swap_halves(u)).astype(BF16)
         out[rows_at(at + ROWS, ROWS), :] = jnp.where(left, swap_halves(g), u).astype(BF16)
@@ -225,30 +242,29 @@
     left = left_half((half, LANES))
 
     def block(expert, source):
-        at = pl.multiple_of((expert * NX + source) * half, half)
-        return hidden[pl.ds(at, half), :].astype(F32)
-
-    for d, w in enumerate((w0, w1, w2, w3)):
-        source = lax.bitwise_xor(x, jnp.int32(d))
+        return hidden[rows_at((expert * NX + source) * half, half), :].astype(F32)
+
+    pairs = []
+    for d in range(NX):
+        source = lax.bitwise_xor(x, jnp.int32(d ^ 2))
         a, b = block(core, source), block(1 - core, source)
-        top = dot(jnp.where(left, a, swap_halves(b)).astype(BF16), w[...])
-        bottom = dot(jnp.where(left, swap_halves(a), b).astype(BF16), w[...])
-        if d == 0:
-            acc[0:half, :] = top
-            acc[half:ROWS, :] = bottom
-        else:
-            acc[0:half, :] += top
-            acc[half:ROWS, :] += bottom
+        top, bottom = jnp.where(left, a, swap_halves(b)), jnp.where(left, swap_halves(a), b)
+        pairs.append(jnp.concatenate([top, bottom], axis=0).astype(BF16))
+    w = jnp.concatenate([w0[...], w1[...], w2[...], w3[...]], axis=0)
+    acc[...] = dot(jnp.concatenate(pairs, axis=1), w)
     n = 2 * NX * BLOCK_ROWS
     k, row = divided(iota((1, EIGHTH * PAIR), 1), PAIR)
     column, r = divided(row, SLOTS)
     q = one_hot(iota((n, EIGHTH * PAIR), 0), column * BLOCK_ROWS + k * SLOTS + r)
-    for g in range(4):
-        stacked = jnp.concatenate(
-            [acc[PAIR * g : PAIR * (g + 1), LANES * k : LANES * (k + 1)] for k in range(EIGHTH)],
-            axis=0,
-        ).astype(BF16)
-        out[n * g : n * (g + 1), :] = dot(q, stacked).astype(BF16)
+
+    def stacked(g):
+        pieces = [acc[PAIR * g : PAIR * (g + 1), LANES * k : LANES * (k + 1)] for k in range(EIGHTH)]
+        return jnp.concatenate(pieces, axis=0).astype(BF16)
+
+    for g in range(0, 4, 2):
+        both = dot(q, jnp.concatenate([stacked(g), stacked(g + 1)], axis=1)).astype(BF16)
+        for i in range(2):
+            out[n * (g + i) : n * (g + i + 1), :] = both[:, LANES * i : LANES * (i + 1)]
 
 
 def unpack_body(parts, gate_rows, out):
@@ -257,37 +273,39 @@
     for y in range(1, NY):
         total = total + parts[n * y : n * (y + 1), :].astype(F32)
     slot = slot_of(gate_rows[...])
-    a = lax.broadcasted_iota(jnp.int32, (TOK * TOK, TOK), 0)
-    b = lax.broadcasted_iota(jnp.int32, (TOK * TOK, TOK), 1)
-    token = lax.shift_right_logical(a, 5) + NC * (FIRST_PLANE_OUT - FIRST_PLANE_IN)
-    spread = dot(one_hot(lax.bitwise_and(token, TOK - 1), b), slot.astype(BF16))
-    chunk = lax.bitwise_and(lax.broadcasted_iota(jnp.int32, (TOK * TOK, LANES), 0), TOK - 1)
-    key = (chunk.astype(F32) * 16.0 + spread)[:, 0:1]
+    place, chunk = divided(iota((TOK * HALF, 1), 0), HALF)
+    place = place + NC * (FIRST_PLANE_OUT - FIRST_PLANE_IN)
+    token = place - TOK * jnp.floor((place + 0.5) * (1.0 / TOK))
+    spread = dot(one_hot(token, iota((TOK * HALF, TOK), 1)), slot.astype(BF16))
+    key = chunk * 16.0 + spread[:, 0:1]
     out[...] = dot(one_hot(key, chunk_and_slot(iota((1, n), 1))), total.astype(BF16)).astype(BF16)
 
 
 def finish_body(parts, out, total):
-    n = 2 * TOK
+    n = NC * HALF
     value = parts[0:n, :].astype(F32)
     for z in range(1, NZ):
         value = value + parts[n * z : n * (z + 1), :].astype(F32)
     total[...] = value
-    for c in range(NC):
-        for j in range(HALF):
-            at = (c * HALF + j) * LANES
-            row = c * TOK + j
-            out[:, at : at + LANES] = total[row : row + 1, :].astype(BF16)
-
-
-def exchange(x, axes, members, turn=0):
+    for j in range(n):
+        out[:, j * LANES : (j + 1) * LANES] = total[j : j + 1, :].astype(BF16)
+
+
+def turned(members, first):
+    return [(i + first) % members for i in range(members)]
+
+
+ROW_ORDER = [i ^ 2 for i in range(NC * NX)]
+
+
+def exchange(x, axes, members, order, group=8):
     rows = x.shape[0] // members
-    order = [[(i + turn) % members for i in range(members)]] if turn else None
     y = lax.all_to_all(
-        x.reshape(members, rows, x.shape[1]),
+        x.reshape(members, rows // group, group, x.shape[1]),
         axes,
         split_axis=0,
         concat_axis=0,
-        axis_index_groups=order,
+        axis_index_groups=[order],
         tiled=True,
     )
     return y.reshape(x.shape)
@@ -351,19 +369,19 @@
 
     sent = call(
         spread_body,
-        shape((TOK * TOK, LANES), BF16),
+        shape((TOK * TOKEN_ROWS, LANES), BF16),
         (node_ids[0], gates[0], tokens[0]),
         scratch=(
             pltpu.VMEM((1, 4), jnp.int32),
             pltpu.VMEM((1, 8), BF16),
             pltpu.VMEM((1, 2 * HALF * LANES), BF16),
-            pltpu.VMEM((2 * TOK, LANES), F32),
+            pltpu.VMEM((2 * NC * TOKEN_ROWS, LANES), F32),
             pltpu.SemaphoreType.DMA((3,)),
         ),
         far=(0, 1, 2),
     )
     sent, w_in, w_out = lax.optimization_barrier((sent, w_in, w_out))
-    arrived = exchange(sent, COLUMN, NZ * NC, NC * FIRST_PLANE_IN)
+    arrived = exchange(sent, COLUMN, NZ * NC, turned(NZ * NC, NC * FIRST_PLANE_IN), 2)
     w_in = w_in.reshape(4 * WIDTH, 2 * LANES)
     w_up = up_weights(place_ids, w_in)
     w_down = down_weights(place_ids, w_out[0])
@@ -373,7 +391,7 @@
         (shape((NY * NX * BLOCK_ROWS, LANES), BF16), shape((TOK, LANES), F32)),
         (arrived,),
     )
-    rows = exchange(packed, PLANE, NY * NX, FIRST_COLUMN_IN)
+    rows = exchange(packed, PLANE, NY * NX, turned(NY * NX, FIRST_COLUMN))
 
     partial_sums, gate, balance = call(
         up_body,
@@ -389,10 +407,10 @@
         far=(1,),
         flops=10**9,
     )
-    summands = exchange(partial_sums, ROW, 8)
+    summands = exchange(partial_sums, ROW, 8, ROW_ORDER)
 
     hidden = call(hidden_body, shape((4 * ROWS, LANES), BF16), (summands, gate))
-    every_hidden = exchange(hidden, ROW, 8)
+    every_hidden = exchange(hidden, ROW, 8, ROW_ORDER)
 
     down = call(
         down_body,
@@ -402,20 +420,20 @@
         smem=(0,),
         flops=10**9,
     )
-    returned = exchange(down, PLANE, NY * NX, FIRST_COLUMN_OUT)
+    returned = exchange(down, PLANE, NY * NX, turned(NY * NX, FIRST_COLUMN))
 
     unpacked = call(
         unpack_body,
-        shape((TOK * TOK, LANES), BF16),
+        shape((TOK * HALF, LANES), BF16),
         (returned, gate_rows),
     )
-    back = exchange(unpacked, COLUMN, NZ * NC, NC * FIRST_PLANE_OUT)
+    back = exchange(unpacked, COLUMN, NZ * NC, turned(NZ * NC, NC * FIRST_PLANE_OUT), 4)
 
     mixed = call(
         finish_body,
         shape((1, 2 * HALF * LANES), BF16),
         (back,),
-        scratch=(pltpu.VMEM((2 * TOK, LANES), F32),),
+        scratch=(pltpu.VMEM((2 * HALF, LANES), F32),),
     )
     return mixed[None], balance
 

time: 181 us -> 178 us (0.983)
  starting transfers between devices: 34.7 us -> 38.8 us
  waiting for transfers between devices: 30.6 us -> 26.9 us
  blocking collectives: 100 us -> 97.4 us
    all_to_all x2, starting transfers between devices: 13.8 us -> 17.9 us  [exchange(): lax.all_to_all(x.reshape(members, rows // group, group, x.shape[1]), axes...]
    all_to_all x4, blocking collectives: 100 us -> 97.4 us  [exchange(): lax.all_to_all(x.reshape(members, rows // group, group, x.shape[1]), axes...]
    ppermute x3, waiting for transfers between devices: 11.9 us -> 9.63 us  [down_weights(): lax.ppermute(parts[d], ('xh', 'xl'), [(i, i ^ d) for i in range(NX)])]
  transfers between devices with their start and end apart: 9 -> 9, of which waited for: 5 -> 4; matrix products, arithmetic and copies ran while one was open for 0% -> 0% of each run, Pallas kernels for 4% -> 4%
where the time goes in v6:
time: 178 us; the launch traced here: 177 us
  blocking collectives  97.4 us (55%)
  starting transfers between devices  38.8 us (22%)
  waiting for transfers between devices  26.9 us (15%)
  Pallas kernels  11.5 us (6%)
  local copies, waits for them, and re-layouts  1.8 us (1%)
    all_to_all x4, blocking collectives, exchange(): lax.all_to_all(x.reshape(members, rows // group, group, x.shape[1]), axes...  97.4 us
    all_to_all x2, starting transfers between devices, exchange(): lax.all_to_all(x.reshape(members, rows // group, group, x.shape[1]), axes...  17.9 us
    ppermute x3, waiting for transfers between devices, up_weights(): out.append(lax.ppermute(parts[i], *swaps[i]))  17.3 us
    pallas_call x9, Pallas kernels, call(): pl.pallas_call(body, out_shape=outs, in_specs=[far_spec if i in far else...  11.5 us
    ppermute x3, waiting for transfers between devices, down_weights(): lax.ppermute(parts[d], ('xh', 'xl'), [(i, i ^ d) for i in range(NX)])  9.63 us
    ppermute x3, starting transfers between devices, down_weights(): lax.ppermute(parts[d], ('xh', 'xl'), [(i, i ^ d) for i in range(NX)])  9.58 us
    ppermute x3, starting transfers between devices, up_weights(): out.append(lax.ppermute(parts[i], *swaps[i]))  9.37 us
  transfers between devices with their start and end apart: 9, of which 4 were waited for; matrix products, arithmetic and copies ran while one was open for 0% of the time, Pallas kernels for 4%

profile of v6, /device:TPU:1, one launch (start us, length us, event | category | flops | bytes accessed | tf_op | source)
XLA Modules:
  0.0 177.2 jit_solution(2505806946487058243)
XLA Ops:
  0.6 0.9 shard_map.68
  1.6 0.0 copy-start
  1.6 38.5 %all_to_all.30 = bf16[32,15,2,128]{3,2,1,0:T(2,128)(2,1)S(1)} all-to-all(bf16[32,15,2,128]{3,2,1,0:T(2,128)(2,1)S(1)} %bitcast.31), channel_id=1, replica_groups={{832,864,896,928,960,992,0,32,64,96,128,160,192,224,256,288,320,352,384..., dimensions={0} | all-to-all | bytes 491520 | tf_op jit(solution)/shard_map/all_to_all | solution.py:303
  40.1 1.6 shard_map.69
  41.7 11.6 %all-to-all-start.1 = ((bf16[32,8,8,128]{3,2,1,0:T(8,128)(2,1)}), bf16[32,8,8,128]{3,2,1,0:T(8,128)(2,1)S(1)}, u32[]{:S(2)}, u32[]{:S(2)}) async-start(bf16[32,8,8,128]{3,2,1,0:T(8,128)(2,1)} %bitcast.9), calls=%async_computation.1 | async-start | bytes 1048576 | tf_op jit(solution)/shard_map/all_to_all | solution.py:303
  53.4 0.1 pad_add_fusion.place_ids
  53.4 1.9 %shard_map.70 = (bf16[896,256]{1,0:T(8,128)(2,1)S(1)}, bf16[896,256]{1,0:T(8,128)(2,1)S(1)}, bf16[896,256]{1,0:T(8,128)(2,1)S(1)}) custom-call(s32[3]{0:T(128)S(1)} %pad_add_fusion.place_ids, bf16[3584,256]{1,0:T(8,128)(2,1)} %bitcast.33), custom_call_target="tpu_custom_call" | custom-call | flops 100000000 | bytes 1000000 | tf_op jit(solution)/shard_map/pallas_call | solution.py:77
  55.3 1.9 %collective-permute-start = (bf16[896,256]{1,0:T(8,128)(2,1)S(1)}, bf16[896,256]{1,0:T(8,128)(2,1)S(1)}, u32[]{:S(2)}, u32[]{:S(2)}) collective-permute-start(bf16[896,256]{1,0:T(8,128)(2,1)S(1)} %get-tuple-element.20), channel_id=1, source_target_pairs={{0,32},{32,0},{1,33},{33,1},{2,34},{34,2},{3,35},{35,3},{4,36},{36... | collective-permute-start | bytes 1376264 | tf_op jit(solution)/shard_map/ppermute | solution.py:347
  57.2 2.2 %collective-permute-start.1 = (bf16[896,256]{1,0:T(8,128)(2,1)S(1)}, bf16[896,256]{1,0:T(8,128)(2,1)S(1)}, u32[]{:S(2)}, u32[]{:S(2)}) collective-permute-start(bf16[896,256]{1,0:T(8,128)(2,1)S(1)} %get-tuple-element.21), channel_id=1, source_target_pairs={{0,2},{2,0},{1,3},{3,1},{4,6},{6,4},{5,7},{7,5},{8,10},{10,8},{9,1... | collective-permute-start | bytes 1376264 | tf_op jit(solution)/shard_map/ppermute | solution.py:347
  59.5 5.2 %collective-permute-start.2 = (bf16[896,256]{1,0:T(8,128)(2,1)S(1)}, bf16[896,256]{1,0:T(8,128)(2,1)S(1)}, u32[]{:S(2)}, u32[]{:S(2)}) collective-permute-start(bf16[896,256]{1,0:T(8,128)(2,1)S(1)} %get-tuple-element.22), channel_id=1, source_target_pairs={{0,34},{2,32},{32,2},{34,0},{1,35},{3,33},{33,3},{35,1},{4,38},{6,... | collective-permute-start | bytes 1376264 | tf_op jit(solution)/shard_map/ppermute | solution.py:347
  64.7 0.0 copy-done
  64.7 1.9 %collective-permute-start.3 = (bf16[64,7168]{1,0:T(8,128)(2,1)S(1)}, bf16[64,7168]{1,0:T(8,128)(2,1)S(1)}, u32[]{:S(2)}, u32[]{:S(2)}) collective-permute-start(bf16[64,7168]{1,0:T(8,128)(2,1)S(1)} %bitcast.25), channel_id=1, source_target_pairs={{0,32},{32,0},{1,33},{33,1},{2,34},{34,2},{3,35},{35,3},{4,36},{36... | collective-permute-start | bytes 2752520 | tf_op jit(solution)/shard_map/ppermute | solution.py:352
  66.6 0.0 collective-permute-done.w_core
  66.7 7.3 %collective-permute-done.1.w_row = bf16[896,256]{1,0:T(8,128)(2,1)S(1)} collective-permute-done((bf16[896,256]{1,0:T(8,128)(2,1)S(1)}, bf16[896,256]{1,0:T(8,128)(2,1)S(1)}, u32[]{:S(2)}, u32[]{:S(2)}) %collective-permute-start.1) | collective-permute-done | bytes 458784 | tf_op jit(solution)/shard_map/ppermute | solution.py:347
  74.0 9.9 %collective-permute-done.2.w_both = bf16[896,256]{1,0:T(8,128)(2,1)S(1)} collective-permute-done((bf16[896,256]{1,0:T(8,128)(2,1)S(1)}, bf16[896,256]{1,0:T(8,128)(2,1)S(1)}, u32[]{:S(2)}, u32[]{:S(2)}) %collective-permute-start.2) | collective-permute-done | bytes 458784 | tf_op jit(solution)/shard_map/ppermute | solution.py:347
  83.9 0.0 copy-start.1
  83.9 0.8 copy-done.1
  84.7 0.0 all-to-all-done.1
  84.7 0.0 copy-start.2
  84.7 1.0 copy-done.2
  85.7 3.0 %shard_map.71 = (bf16[2304,128]{1,0:T(8,128)(2,1)S(1)}, f32[288,128]{1,0:T(8,128)S(1)}, f32[1]{0:T(128)}) custom-call(s32[3]{0:T(128)S(1)} %pad_add_fusion.place_ids, bf16[3584,256]{1,0:T(8,128)(2,1)} %bitcast.34, bf16[2048,128]{1,0:T(8,128)(2,1)S(1)} %bitcast.23, bf16[896,256]{1,0:T(8,128)(2,1)S(1)} %collective-permute-done.w_core, ...), custom_call_target="tpu_custom_call" | custom-call | flops 1000000000 | bytes 1000000 | tf_op jit(solution)/shard_map/pallas_call | solution.py:77
  88.7 12.4 %all_to_all.31 = bf16[8,36,8,128]{3,2,1,0:T(8,128)(2,1)S(1)} all-to-all(bf16[8,36,8,128]{3,2,1,0:T(8,128)(2,1)S(1)} %bitcast.27), channel_id=1, replica_groups={{2,3,0,1,34,35,32,33},{6,7,4,5,38,39,36,37},{10,11,8,9,42,43,40,41},{14..., dimensions={0} | all-to-all | bytes 1179648 | tf_op jit(solution)/shard_map/all_to_all | solution.py:303
  101.1 0.9 shard_map.72
  101.9 6.3 %all-to-all-start.3 = ((bf16[8,18,8,128]{3,2,1,0:T(8,128)(2,1)}), bf16[8,18,8,128]{3,2,1,0:T(8,128)(2,1)S(1)}, u32[]{:S(2)}, u32[]{:S(2)}) async-start(bf16[8,18,8,128]{3,2,1,0:T(8,128)(2,1)} %bitcast.13), calls=%async_computation.3 | async-start | bytes 589824 | tf_op jit(solution)/shard_map/all_to_all | solution.py:303
  108.2 0.0 collective-permute-done.3.other
  108.2 0.6 shard_map.73
  108.9 1.9 %collective-permute-start.4 = (bf16[128,896]{1,0:T(8,128)(2,1)S(1)}, bf16[128,896]{1,0:T(8,128)(2,1)S(1)}, u32[]{:S(2)}, u32[]{:S(2)}) collective-permute-start(bf16[128,896]{1,0:T(8,128)(2,1)S(1)} %get-tuple-element.27), channel_id=1, source_target_pairs={{0,1},{1,0},{2,3},{3,2},{4,5},{5,4},{6,7},{7,6},{8,9},{9,8},{10,11... | collective-permute-start | bytes 688136 | tf_op jit(solution)/shard_map/ppermute | solution.py:361
  110.8 3.4 %collective-permute-start.5 = (bf16[128,896]{1,0:T(8,128)(2,1)S(1)}, bf16[128,896]{1,0:T(8,128)(2,1)S(1)}, u32[]{:S(2)}, u32[]{:S(2)}) collective-permute-start(bf16[128,896]{1,0:T(8,128)(2,1)S(1)} %get-tuple-element.28), channel_id=1, source_target_pairs={{0,2},{1,3},{2,0},{3,1},{4,6},{5,7},{6,4},{7,5},{8,10},{9,11},{10,... | collective-permute-start | bytes 688136 | tf_op jit(solution)/shard_map/ppermute | solution.py:361
  114.1 4.3 %collective-permute-start.6 = (bf16[128,896]{1,0:T(8,128)(2,1)S(1)}, bf16[128,896]{1,0:T(8,128)(2,1)S(1)}, u32[]{:S(2)}, u32[]{:S(2)}) collective-permute-start(bf16[128,896]{1,0:T(8,128)(2,1)S(1)} %get-tuple-element.29), channel_id=1, source_target_pairs={{0,3},{1,2},{2,1},{3,0},{4,7},{5,6},{6,5},{7,4},{8,11},{9,10},{10,... | collective-permute-start | bytes 688136 | tf_op jit(solution)/shard_map/ppermute | solution.py:361
  118.5 0.0 collective-permute-done.4.w1
  118.5 4.0 %collective-permute-done.5.w2 = bf16[128,896]{1,0:T(8,128)(2,1)S(1)} collective-permute-done((bf16[128,896]{1,0:T(8,128)(2,1)S(1)}, bf16[128,896]{1,0:T(8,128)(2,1)S(1)}, u32[]{:S(2)}, u32[]{:S(2)}) %collective-permute-start.5) | collective-permute-done | bytes 229408 | tf_op jit(solution)/shard_map/ppermute | solution.py:361
  122.5 5.6 %collective-permute-done.6.w3 = bf16[128,896]{1,0:T(8,128)(2,1)S(1)} collective-permute-done((bf16[128,896]{1,0:T(8,128)(2,1)S(1)}, bf16[128,896]{1,0:T(8,128)(2,1)S(1)}, u32[]{:S(2)}, u32[]{:S(2)}) %collective-permute-start.6) | collective-permute-done | bytes 229408 | tf_op jit(solution)/shard_map/ppermute | solution.py:361
  128.1 0.0 all-to-all-done.3
  128.1 1.3 shard_map.74
  129.5 20.9 %all_to_all.32 = bf16[32,8,8,128]{3,2,1,0:T(8,128)(2,1)S(1)} all-to-all(bf16[32,8,8,128]{3,2,1,0:T(8,128)(2,1)S(1)} %bitcast.28), channel_id=1, replica_groups={{18,19,20,21,22,23,24,25,26,27,28,29,30,31,0,1,2,3,4,5,6,7,8,9,10,11,12..., dimensions={0} | all-to-all | bytes 1048576 | tf_op jit(solution)/shard_map/all_to_all | solution.py:303
  150.4 0.6 shard_map.75
  151.0 25.5 %all_to_all.33 = bf16[32,7,4,128]{3,2,1,0:T(4,128)(2,1)S(1)} all-to-all(bf16[32,7,4,128]{3,2,1,0:T(4,128)(2,1)S(1)} %bitcast.24), channel_id=1, replica_groups={{512,544,576,608,640,672,704,736,768,800,832,864,896,928,960,992,0,32,6..., dimensions={0} | all-to-all | bytes 458752 | tf_op jit(solution)/shard_map/all_to_all | solution.py:303
  176.5 0.7 shard_map.76
Async XLA Ops:
  1.6 63.1 %copy-start = (bf16[1,64,7168]{2,1,0:T(8,128)(2,1)S(1)}, bf16[1,64,7168]{2,1,0:T(8,128)(2,1)}, u32[]{:S(2)}) copy-start(bf16[1,64,7168]{2,1,0:T(8,128)(2,1)} %param.9) | copy-start | bytes 2752516
  41.7 43.0 %all-to-all-start.1 = ((bf16[32,8,8,128]{3,2,1,0:T(8,128)(2,1)}), bf16[32,8,8,128]{3,2,1,0:T(8,128)(2,1)S(1)}, u32[]{:S(2)}, u32[]{:S(2)}) async-start(bf16[32,8,8,128]{3,2,1,0:T(8,128)(2,1)} %bitcast.9), calls=%async_computation.1 | async-start | bytes 1048576 | tf_op jit(solution)/shard_map/all_to_all | solution.py:303
  55.3 11.3 %collective-permute-start = (bf16[896,256]{1,0:T(8,128)(2,1)S(1)}, bf16[896,256]{1,0:T(8,128)(2,1)S(1)}, u32[]{:S(2)}, u32[]{:S(2)}) collective-permute-start(bf16[896,256]{1,0:T(8,128)(2,1)S(1)} %get-tuple-element.20), channel_id=1, source_target_pairs={{0,32},{32,0},{1,33},{33,1},{2,34},{34,2},{3,35},{35,3},{4,36},{36... | collective-permute-start | bytes 1376264 | tf_op jit(solution)/shard_map/ppermute | solution.py:347
  57.2 16.7 %collective-permute-start.1 = (bf16[896,256]{1,0:T(8,128)(2,1)S(1)}, bf16[896,256]{1,0:T(8,128)(2,1)S(1)}, u32[]{:S(2)}, u32[]{:S(2)}) collective-permute-start(bf16[896,256]{1,0:T(8,128)(2,1)S(1)} %get-tuple-element.21), channel_id=1, source_target_pairs={{0,2},{2,0},{1,3},{3,1},{4,6},{6,4},{5,7},{7,5},{8,10},{10,8},{9,1... | collective-permute-start | bytes 1376264 | tf_op jit(solution)/shard_map/ppermute | solution.py:347
  59.5 24.5 %collective-permute-start.2 = (bf16[896,256]{1,0:T(8,128)(2,1)S(1)}, bf16[896,256]{1,0:T(8,128)(2,1)S(1)}, u32[]{:S(2)}, u32[]{:S(2)}) collective-permute-start(bf16[896,256]{1,0:T(8,128)(2,1)S(1)} %get-tuple-element.22), channel_id=1, source_target_pairs={{0,34},{2,32},{32,2},{34,0},{1,35},{3,33},{33,3},{35,1},{4,38},{6,... | collective-permute-start | bytes 1376264 | tf_op jit(solution)/shard_map/ppermute | solution.py:347
  64.7 43.5 %collective-permute-start.3 = (bf16[64,7168]{1,0:T(8,128)(2,1)S(1)}, bf16[64,7168]{1,0:T(8,128)(2,1)S(1)}, u32[]{:S(2)}, u32[]{:S(2)}) collective-permute-start(bf16[64,7168]{1,0:T(8,128)(2,1)S(1)} %bitcast.25), channel_id=1, source_target_pairs={{0,32},{32,0},{1,33},{33,1},{2,34},{34,2},{3,35},{35,3},{4,36},{36... | collective-permute-start | bytes 2752520 | tf_op jit(solution)/shard_map/ppermute | solution.py:352
  83.9 0.8 copy-start.1
  84.7 1.0 copy-start.2
  101.9 26.2 %all-to-all-start.3 = ((bf16[8,18,8,128]{3,2,1,0:T(8,128)(2,1)}), bf16[8,18,8,128]{3,2,1,0:T(8,128)(2,1)S(1)}, u32[]{:S(2)}, u32[]{:S(2)}) async-start(bf16[8,18,8,128]{3,2,1,0:T(8,128)(2,1)} %bitcast.13), calls=%async_computation.3 | async-start | bytes 589824 | tf_op jit(solution)/shard_map/all_to_all | solution.py:303
  108.9 9.6 %collective-permute-start.4 = (bf16[128,896]{1,0:T(8,128)(2,1)S(1)}, bf16[128,896]{1,0:T(8,128)(2,1)S(1)}, u32[]{:S(2)}, u32[]{:S(2)}) collective-permute-start(bf16[128,896]{1,0:T(8,128)(2,1)S(1)} %get-tuple-element.27), channel_id=1, source_target_pairs={{0,1},{1,0},{2,3},{3,2},{4,5},{5,4},{6,7},{7,6},{8,9},{9,8},{10,11... | collective-permute-start | bytes 688136 | tf_op jit(solution)/shard_map/ppermute | solution.py:361
  110.8 11.7 %collective-permute-start.5 = (bf16[128,896]{1,0:T(8,128)(2,1)S(1)}, bf16[128,896]{1,0:T(8,128)(2,1)S(1)}, u32[]{:S(2)}, u32[]{:S(2)}) collective-permute-start(bf16[128,896]{1,0:T(8,128)(2,1)S(1)} %get-tuple-element.28), channel_id=1, source_target_pairs={{0,2},{1,3},{2,0},{3,1},{4,6},{5,7},{6,4},{7,5},{8,10},{9,11},{10,... | collective-permute-start | bytes 688136 | tf_op jit(solution)/shard_map/ppermute | solution.py:361
  114.1 14.0 %collective-permute-start.6 = (bf16[128,896]{1,0:T(8,128)(2,1)S(1)}, bf16[128,896]{1,0:T(8,128)(2,1)S(1)}, u32[]{:S(2)}, u32[]{:S(2)}) collective-permute-start(bf16[128,896]{1,0:T(8,128)(2,1)S(1)} %get-tuple-element.29), channel_id=1, source_target_pairs={{0,3},{1,2},{2,1},{3,0},{4,7},{5,6},{6,5},{7,4},{8,11},{9,10},{10,... | collective-permute-start | bytes 688136 | tf_op jit(solution)/shard_map/ppermute | solution.py:361
